TPU v7x, 32 devices: a whole 2x2x4 slice. The times are simulated.
32 devices in a mesh: dp: 16 (over z, y, x), tensor: 2 (over core).
Axes of the slice: x: 2, y: 2, z: 4, core: 2. Of those that a mesh axis runs over, the one named last changes fastest.
Arguments:
- hidden_in: bfloat16 [16384, 1536], P(('dp', 'tensor')), may hold values from -6 to 6
- query_weight: bfloat16 [1536, 1536], P('dp', 'tensor'), may hold values from -0.15625 to 0.15625
- key_matrix: bfloat16 [1536, 768], P('dp', 'tensor'), may hold values from -0.15625 to 0.15625
- value_matrix: bfloat16 [1536, 768], P('dp', 'tensor'), may hold values from -0.15625 to 0.15625
- out_weight: bfloat16 [1536, 1536], P('tensor', 'dp'), may hold values from -1.25 to 1.25
- gate_weight: bfloat16 [1536, 4096], P('dp', 'tensor'), may hold values from -0.15625 to 0.15625
- up_weight: bfloat16 [1536, 4096], P('dp', 'tensor'), may hold values from -0.15625 to 0.15625
- down_weight: bfloat16 [4096, 1536], P('tensor', 'dp'), may hold values from -0.09375 to 0.09375
- attention_gain: bfloat16 [1536], P('dp'), may hold values from 0.099609375 to 1.8984375
- feedforward_gain: bfloat16 [1536], P('dp'), may hold values from 0.099609375 to 1.8984375
- cotangent: bfloat16 [16384, 1536], P(('dp', 'tensor')), may hold values from -6 to 6
Outputs:
- hidden_out: bfloat16 [16384, 1536], P(('dp', 'tensor'))
- grad_in: float32 [16384, 1536], P(('dp', 'tensor'))
- grad_query: float32 [1536, 1536], P('dp', 'tensor')
- grad_key: float32 [1536, 768], P('dp', 'tensor')
- grad_value: float32 [1536, 768], P('dp', 'tensor')
- grad_out: float32 [1536, 1536], P('tensor', 'dp')
- grad_gate: float32 [1536, 4096], P('dp', 'tensor')
- grad_up: float32 [1536, 4096], P('dp', 'tensor')
- grad_down: float32 [4096, 1536], P('tensor', 'dp')
- grad_attention_gain: float32 [1536], P('dp')
- grad_feedforward_gain: float32 [1536], P('dp')
All inputs are finite; a program needn't handle non-finite values.
Results may differ from a plain program's by a relative error of at most 0.015.
Values may be sent and summed in bfloat16 or wider, within the bound.
A program may use at most 256 MiB of HBM per device.

v0:
```python
import math

import jax
import jax.numpy as jnp
from jax import lax
from jax.sharding import PartitionSpec as P

QUERY_HEADS = 16
KEY_VALUE_HEADS = 8
HEAD_SIZE = 96
SEQUENCE_LENGTH = 512


EPSILON = 1e-05
THETA_BASE = 100000.0


def rope_tables(length, width):
    half_width = width // 2
    inverse = THETA_BASE ** (-(jnp.arange(half_width, dtype=jnp.float32) * 2.0 / width))
    position = jnp.arange(length, dtype=jnp.float32)
    angles = position[:, None] * inverse[None, :]
    return (jnp.cos(angles), jnp.sin(angles))


def apply_rotary(tensor, cosine_table, sine_table, direction):
    half_width = tensor.shape[-1] // 2
    first_half = tensor[..., :half_width]
    second_half = tensor[..., half_width:]
    cos_part = cosine_table[:, None, :]
    sin_part = direction * sine_table[:, None, :]
    return jnp.concatenate(
        [
            first_half * cos_part - second_half * sin_part,
            second_half * cos_part + first_half * sin_part,
        ],
        axis=-1,
    )


def causal_scores(query, keys):
    length = query.shape[0]
    score_scale = 1.0 / math.sqrt(query.shape[-1])
    scores = (
        jnp.einsum("qkgd,tkd->kgqt", query, keys, preferred_element_type=jnp.float32) * score_scale
    )
    earlier = lax.broadcasted_iota(jnp.int32, (length, length), 0) >= lax.broadcasted_iota(
        jnp.int32, (length, length), 1
    )
    return jnp.where(earlier, scores, -jnp.inf)


def attend(bundle):
    query, keys, values = bundle
    scores = causal_scores(query, keys)
    log_total = jnp.log(jnp.sum(jnp.exp(scores), axis=-1))
    soft_weights = jnp.exp(scores - log_total[..., None]).astype(jnp.bfloat16)
    mixture_output = jnp.einsum(
        "kgqt,tkd->qkgd", soft_weights, values, preferred_element_type=jnp.float32
    ).astype(jnp.bfloat16)
    return (mixture_output, log_total)


def attend_back(bundle):
    query, keys, values, mixture_gradient, row_products, log_total = bundle
    score_scale = 1.0 / math.sqrt(query.shape[-1])
    chances = jnp.exp(causal_scores(query, keys) - log_total[..., None])
    soft_weights = chances.astype(jnp.bfloat16)
    value_gradient = jnp.einsum(
        "kgqt,qkgd->tkd", soft_weights, mixture_gradient, preferred_element_type=jnp.float32
    )
    grad_weights = jnp.einsum(
        "qkgd,tkd->kgqt", mixture_gradient, values, preferred_element_type=jnp.float32
    )
    grad_scores = (chances * (grad_weights - row_products[..., None])).astype(jnp.bfloat16)
    grad_query = (
        jnp.einsum("kgqt,tkd->qkgd", grad_scores, keys, preferred_element_type=jnp.float32)
        * score_scale
    )
    grad_keys = (
        jnp.einsum("kgqt,qkgd->tkd", grad_scores, query, preferred_element_type=jnp.float32)
        * score_scale
    )
    return (grad_query, grad_keys, value_gradient)


def matrix_multiply(left, right):
    return jnp.dot(left, right, preferred_element_type=jnp.float32)


def across(left, right):
    return lax.dot_general(
        left, right, (((0,), (0,)), ((), ())), preferred_element_type=jnp.float32
    )


def against(left, right):
    return lax.dot_general(
        left, right, (((1,), (1,)), ((), ())), preferred_element_type=jnp.float32
    )


def norm_back(grad_normed, unit_rows, inverse_rms, gain):
    scaled = grad_normed * gain
    inner = jnp.mean(scaled * unit_rows, axis=1, keepdims=True)
    return (inverse_rms * (scaled - unit_rows * inner), jnp.sum(grad_normed * unit_rows, axis=0))


def shards(
    hidden_in,
    query_weight,
    key_matrix,
    value_matrix,
    out_weight,
    gate_weight,
    up_weight,
    down_weight,
    attention_gain,
    feedforward_gain,
    cotangent,
):
    gathered = (
        lax.all_gather(query_weight, "dp", axis=0, tiled=True),
        lax.all_gather(key_matrix, "dp", axis=0, tiled=True),
        lax.all_gather(value_matrix, "dp", axis=0, tiled=True),
        lax.all_gather(out_weight, "dp", axis=1, tiled=True),
        lax.all_gather(gate_weight, "dp", axis=0, tiled=True),
        lax.all_gather(up_weight, "dp", axis=0, tiled=True),
        lax.all_gather(down_weight, "dp", axis=1, tiled=True),
        lax.all_gather(attention_gain, "dp", axis=0, tiled=True),
        lax.all_gather(feedforward_gain, "dp", axis=0, tiled=True),
    )
    (
        full_query,
        full_key,
        full_value,
        full_out,
        full_gate,
        full_up,
        full_down,
        stored_first,
        stored_second,
    ) = gathered
    gain_first = stored_first.astype(jnp.float32)
    gain_second = stored_second.astype(jnp.float32)
    heads_here = full_query.shape[1] // HEAD_SIZE
    kv_here = full_key.shape[1] // HEAD_SIZE
    heads_per_group = QUERY_HEADS // KEY_VALUE_HEADS
    input_rows = hidden_in.astype(jnp.float32)
    inverse_one = lax.rsqrt(jnp.mean(input_rows * input_rows, axis=1, keepdims=True) + EPSILON)
    unit_one = input_rows * inverse_one
    first_normalized = (unit_one * gain_first).astype(jnp.bfloat16)
    normed_all = lax.all_gather(first_normalized, "tensor", axis=0, tiled=True)
    group_rows = normed_all.shape[0]
    seq_count = group_rows // SEQUENCE_LENGTH
    cosine_table, sine_table = rope_tables(SEQUENCE_LENGTH, HEAD_SIZE)
    query_rows = apply_rotary(
        matrix_multiply(normed_all, full_query).reshape(
            seq_count, SEQUENCE_LENGTH, heads_here, HEAD_SIZE
        ),
        cosine_table,
        sine_table,
        1.0,
    )
    query_rows = query_rows.astype(jnp.bfloat16).reshape(
        seq_count, SEQUENCE_LENGTH, kv_here, heads_per_group, HEAD_SIZE
    )
    every_key = apply_rotary(
        matrix_multiply(normed_all, full_key).reshape(
            seq_count, SEQUENCE_LENGTH, kv_here, HEAD_SIZE
        ),
        cosine_table,
        sine_table,
        1.0,
    ).astype(jnp.bfloat16)
    every_value = (
        matrix_multiply(normed_all, full_value)
        .astype(jnp.bfloat16)
        .reshape(seq_count, SEQUENCE_LENGTH, kv_here, HEAD_SIZE)
    )
    mixture_output, log_totals = lax.map(attend, (query_rows, every_key, every_value))
    mixed_flat = mixture_output.reshape(group_rows, heads_here * HEAD_SIZE)
    attended = lax.psum_scatter(
        matrix_multiply(mixed_flat, full_out), "tensor", scatter_dimension=0, tiled=True
    )
    middle = input_rows + attended
    inverse_two = lax.rsqrt(jnp.mean(middle * middle, axis=1, keepdims=True) + EPSILON)
    unit_two = middle * inverse_two
    normed_two = (unit_two * gain_second).astype(jnp.bfloat16)
    normed_two_all = lax.all_gather(normed_two, "tensor", axis=0, tiled=True)
    gate = matrix_multiply(normed_two_all, full_gate)
    upward = matrix_multiply(normed_two_all, full_up)
    sigma = jax.nn.sigmoid(gate)
    hidden = (gate * sigma * upward).astype(jnp.bfloat16)
    hidden_out = (
        middle
        + lax.psum_scatter(
            matrix_multiply(hidden, full_down).astype(jnp.bfloat16),
            "tensor",
            scatter_dimension=0,
            tiled=True,
        ).astype(jnp.float32)
    ).astype(jnp.bfloat16)
    cotangent_all = lax.all_gather(cotangent, "tensor", axis=0, tiled=True)
    grad_down = across(hidden, cotangent_all)
    grad_hidden = against(cotangent_all, full_down)
    grad_up_act = (grad_hidden * gate * sigma).astype(jnp.bfloat16)
    grad_gate_act = (grad_hidden * upward * sigma * (1.0 + gate * (1.0 - sigma))).astype(
        jnp.bfloat16
    )
    grad_gate = across(normed_two_all, grad_gate_act)
    grad_up = across(normed_two_all, grad_up_act)
    grad_normed_two = lax.psum_scatter(
        against(grad_gate_act, full_gate) + against(grad_up_act, full_up),
        "tensor",
        scatter_dimension=0,
        tiled=True,
    )
    middle_part, second_part = norm_back(grad_normed_two, unit_two, inverse_two, gain_second)
    grad_middle = cotangent.astype(jnp.float32) + middle_part
    grad_middle_round = grad_middle.astype(jnp.bfloat16)
    grad_middle_all = lax.all_gather(grad_middle_round, "tensor", axis=0, tiled=True)
    grad_out = across(mixed_flat, grad_middle_all)
    mixture_gradient = against(grad_middle_all, full_out)
    rounded_mixture_gradient = mixture_gradient.astype(jnp.bfloat16).reshape(
        seq_count, SEQUENCE_LENGTH, kv_here, heads_per_group, HEAD_SIZE
    )
    row_products = jnp.sum(
        mixture_gradient.reshape(seq_count, SEQUENCE_LENGTH, kv_here, heads_per_group, HEAD_SIZE)
        * mixture_output.astype(jnp.float32),
        axis=-1,
    )
    row_products = jnp.transpose(row_products, (0, 2, 3, 1))
    grad_queries_rot, rotated_key_gradient, value_gradient = lax.map(
        attend_back,
        (query_rows, every_key, every_value, rounded_mixture_gradient, row_products, log_totals),
    )
    grad_queries_act = (
        apply_rotary(
            grad_queries_rot.reshape(seq_count, SEQUENCE_LENGTH, heads_here, HEAD_SIZE),
            cosine_table,
            sine_table,
            -1.0,
        )
        .astype(jnp.bfloat16)
        .reshape(group_rows, heads_here * HEAD_SIZE)
    )
    key_activation_gradient = (
        apply_rotary(rotated_key_gradient, cosine_table, sine_table, -1.0)
        .astype(jnp.bfloat16)
        .reshape(group_rows, kv_here * HEAD_SIZE)
    )
    value_activation_gradient = value_gradient.astype(jnp.bfloat16).reshape(
        group_rows, kv_here * HEAD_SIZE
    )
    grad_query = across(normed_all, grad_queries_act)
    grad_key = across(normed_all, key_activation_gradient)
    grad_value = across(normed_all, value_activation_gradient)
    part_query = against(grad_queries_act, full_query)
    part_key = against(key_activation_gradient, full_key)
    part_value = against(value_activation_gradient, full_value)
    grad_normed_one = lax.psum_scatter(
        (part_query + part_key + part_value).astype(jnp.bfloat16),
        "tensor",
        scatter_dimension=0,
        tiled=True,
    ).astype(jnp.float32)
    first_part, gain_one_part = norm_back(grad_normed_one, unit_one, inverse_one, gain_first)
    grad_in = grad_middle + first_part
    (
        grad_query,
        grad_key,
        grad_value,
        grad_out,
        grad_gate,
        grad_up,
        grad_down,
        gain_one_part,
        second_part,
    ) = (
        lax.psum_scatter(grad_query, "dp", scatter_dimension=0, tiled=True),
        lax.psum_scatter(grad_key, "dp", scatter_dimension=0, tiled=True),
        lax.psum_scatter(grad_value, "dp", scatter_dimension=0, tiled=True),
        lax.psum_scatter(grad_out, "dp", scatter_dimension=1, tiled=True),
        lax.psum_scatter(grad_gate, "dp", scatter_dimension=0, tiled=True),
        lax.psum_scatter(grad_up, "dp", scatter_dimension=0, tiled=True),
        lax.psum_scatter(grad_down, "dp", scatter_dimension=1, tiled=True),
        lax.psum_scatter(gain_one_part, "dp", scatter_dimension=0, tiled=True),
        lax.psum_scatter(second_part, "dp", scatter_dimension=0, tiled=True),
    )
    grad_attention_gain, grad_feedforward_gain = lax.psum((gain_one_part, second_part), "tensor")
    return (
        hidden_out,
        grad_in,
        grad_query,
        grad_key,
        grad_value,
        grad_out,
        grad_gate,
        grad_up,
        grad_down,
        grad_attention_gain,
        grad_feedforward_gain,
    )


def solution(mesh):
    in_specs = (
        P(("dp", "tensor"), None),
        P("dp", "tensor"),
        P("dp", "tensor"),
        P("dp", "tensor"),
        P("tensor", "dp"),
        P("dp", "tensor"),
        P("dp", "tensor"),
        P("tensor", "dp"),
        P("dp"),
        P("dp"),
        P(("dp", "tensor"), None),
    )
    out_specs = (
        P(("dp", "tensor"), None),
        P(("dp", "tensor"), None),
        P("dp", "tensor"),
        P("dp", "tensor"),
        P("dp", "tensor"),
        P("tensor", "dp"),
        P("dp", "tensor"),
        P("dp", "tensor"),
        P("tensor", "dp"),
        P("dp"),
        P("dp"),
    )
    return jax.shard_map(shards, mesh=mesh, in_specs=in_specs, out_specs=out_specs, check_vma=False)
```

profile of v0, /device:TPU:0, one launch (start us, length us, event | category | flops | bytes accessed | tf_op | source)
XLA Modules:
  0.0 2068.7 jit_solution(7638144160642563172)
XLA Ops:
  11.7 44.3 %all-reduce.6 = (bf16[1536]{0:T(1024)(128)(2,1)S(1)}, bf16[1536]{0:T(1024)(128)(2,1)S(1)}) all-reduce(bf16[1536]{0:T(1024)(128)(2,1)S(1)} %dynamic-update-slice, bf16[1536]{0:T(1024)(128)(2,1)S(1)} %dynamic-update-slice.1), channel_id=1, replica_groups=mesh['dp'=16,'tensor'=2] {'dp'}, use_global_device_ids=true, to_apply=%add | all-reduce | flops 3072 | bytes 12288
  69.6 13.0 all-gather.12.cloned.1.call-done
  89.6 52.9 %all-gather.14.cloned.1.call-done = bf16[1536,384]{1,0:T(8,128)(2,1)} async-done(((bf16[96,384]{1,0:T(8,128)(2,1)}), bf16[1536,384]{1,0:T(8,128)(2,1)}) %all-gather.14.cloned.1.call-update) | async-done | bytes 1179664 | tf_op jit(solution)/shard_map/all_gather | solution.py:125
  148.0 58.1 %all-gather.18.cloned.1.call-done = bf16[1536,768]{1,0:T(8,128)(2,1)} async-done(((bf16[96,768]{1,0:T(8,128)(2,1)}), bf16[1536,768]{1,0:T(8,128)(2,1)}) %all-gather.18.cloned.1.call-update) | async-done | bytes 2359312 | tf_op jit(solution)/shard_map/all_gather | solution.py:123
  222.0 13.0 while.26
  240.8 28.5 %all-gather.20.cloned.1.call-done = bf16[768,1536]{0,1:T(8,128)(2,1)} async-done(((bf16[768,96]{0,1:T(8,128)(2,1)}), bf16[768,1536]{0,1:T(8,128)(2,1)}) %all-gather.20.cloned.1.call-update) | async-done | bytes 2359312 | tf_op jit(solution)/shard_map/all_gather | solution.py:126
  296.1 91.5 %all-gather.24.cloned.1.call-done = bf16[1536,2048]{1,0:T(8,128)(2,1)} async-done(((bf16[96,2048]{1,0:T(8,128)(2,1)}), bf16[1536,2048]{1,0:T(8,128)(2,1)}) %all-gather.24.cloned.1.call-update) | async-done | bytes 6291472 | tf_op jit(solution)/shard_map/all_gather | solution.py:127
  387.6 12.8 all-gather.22.cloned.1.call-done
  412.5 85.3 %all-gather.26.cloned.1.call-done = bf16[1536,2048]{1,0:T(8,128)(2,1)} async-done(((bf16[96,2048]{1,0:T(8,128)(2,1)}), bf16[1536,2048]{1,0:T(8,128)(2,1)}) %all-gather.26.cloned.1.call-update) | async-done | bytes 6291472 | tf_op jit(solution)/shard_map/all_gather | solution.py:128
  509.9 97.4 %all-gather.28.cloned.1.call-done = bf16[2048,1536]{0,1:T(8,128)(2,1)} async-done(((bf16[2048,96]{0,1:T(8,128)(2,1)}), bf16[2048,1536]{0,1:T(8,128)(2,1)}) %all-gather.28.cloned.1.call-update) | async-done | bytes 6291472 | tf_op jit(solution)/shard_map/all_gather | solution.py:129
  607.3 18.3 multiply_convert_fusion
  665.2 14.2 all-gather.32.cloned.1.call-done
  709.7 126.2 %while.27 = (s32[]{:T(128)}, f32[2,512,4,2,96]{1,0,4,3,2:T(2,128)}, f32[2,512,4,96]{1,0,3,2:T(2,128)}, bf16[2,512,4,96]{1,3,2,0:T(8,128)(2,1)}, bf16[2,512,4,96]...) while((s32[]{:T(128)}, f32[2,512,4,2,96]{1,0,4,3,2:T(2,128)}, ...), condition=%wide.region_11.12_spmd, body=%wide.region_10.11_spmd.sunk | while | flops 2035089408 | bytes 124800344 | solution.py:234
  717.8 28.8 %dynamic_update_slice.30 = f32[2,512,4,2,96]{1,0,4,3,2:T(2,128)} dynamic-update-slice(f32[2,512,4,2,96]{1,0,4,3,2:T(2,128)} %get-tuple-element.359, f32[1,512,4,2,96]{1,0,4,3,2:T(1,128)S(1)} %copy.124, s32[]{:T(128)} %get-tuple-element.358, s32[]{:T(128)} %constant.62.clone.1..sunk, s32[]{:T(128)} %constant.62.clone.1..sunk, s32[]{:T(128)} %constant.62.clone.1..sunk, s32[]{:T(128)} %constant.62.clone.1..sunk) | dynamic-update-slice | bytes 3145732 | tf_op jit(solution)/shard_map/while/body/jit(dynamic_update_index_in_dim)/dynamic_update_slice | solution.py:234
  751.1 15.0 dynamic_update_slice.31
  780.8 28.8 %dynamic_update_slice.30 = f32[2,512,4,2,96]{1,0,4,3,2:T(2,128)} dynamic-update-slice(f32[2,512,4,2,96]{1,0,4,3,2:T(2,128)} %get-tuple-element.359, f32[1,512,4,2,96]{1,0,4,3,2:T(1,128)S(1)} %copy.124, s32[]{:T(128)} %get-tuple-element.358, s32[]{:T(128)} %constant.62.clone.1..sunk, s32[]{:T(128)} %constant.62.clone.1..sunk, s32[]{:T(128)} %constant.62.clone.1..sunk, s32[]{:T(128)} %constant.62.clone.1..sunk) | dynamic-update-slice | bytes 3145732 | tf_op jit(solution)/shard_map/while/body/jit(dynamic_update_index_in_dim)/dynamic_update_slice | solution.py:234
  814.1 15.0 dynamic_update_slice.31
  932.4 77.3 %all-reduce.4 = (f32[1536]{0:T(1024)S(1)}, f32[1536]{0:T(1024)S(1)}) all-reduce(f32[1536]{0:T(1024)S(1)} %get-tuple-element.153, f32[1536]{0:T(1024)S(1)} %copy-done.34), channel_id=13, replica_groups=mesh['dp'=16,'tensor'=2] {'dp'}, use_global_device_ids=true, to_apply=%region_22.23.clone | all-reduce | flops 3072 | bytes 24576
  1019.0 130.3 %reduce-scatter.24.cloned.1.call-done = f32[96,384]{1,0:T(8,128)} async-done(((f32[1536,384]{1,0:T(8,128)}), f32[96,384]{1,0:T(8,128)}) %reduce-scatter.24.cloned.1.call-update) | async-done | bytes 147472 | tf_op jit(solution)/shard_map/reduce_scatter | solution.py:283
  1149.3 207.8 %reduce-scatter.28.cloned.1.call-done = f32[96,2048]{1,0:T(8,128)} async-done(((f32[1536,2048]{1,0:T(8,128)}), f32[96,2048]{1,0:T(8,128)}) %reduce-scatter.28.cloned.1.call-update) | async-done | bytes 786448 | tf_op jit(solution)/shard_map/reduce_scatter | solution.py:285
  1357.0 208.5 %reduce-scatter.30.cloned.1.call-done = f32[96,2048]{1,0:T(8,128)} async-done(((f32[1536,2048]{1,0:T(8,128)}), f32[96,2048]{1,0:T(8,128)}) %reduce-scatter.30.cloned.1.call-update) | async-done | bytes 786448 | tf_op jit(solution)/shard_map/reduce_scatter | solution.py:286
  1565.5 208.3 %reduce-scatter.32.cloned.1.call-done = f32[2048,96]{0,1:T(8,128)} async-done(((f32[2048,1536]{0,1:T(8,128)}), f32[2048,96]{0,1:T(8,128)}) %reduce-scatter.32.cloned.1.call-update) | async-done | bytes 786448 | tf_op jit(solution)/shard_map/reduce_scatter | solution.py:287
  1773.8 144.2 %reduce-scatter.26.cloned.1.call-done = f32[768,96]{0,1:T(8,128)} async-done(((f32[768,1536]{0,1:T(8,128)}), f32[768,96]{0,1:T(8,128)}) %reduce-scatter.26.cloned.1.call-update) | async-done | bytes 294928 | tf_op jit(solution)/shard_map/reduce_scatter | solution.py:284
  1918.0 143.6 %reduce-scatter.20.cloned.1.call-done = f32[96,768]{1,0:T(8,128)} async-done(((f32[1536,768]{1,0:T(8,128)}), f32[96,768]{1,0:T(8,128)}) %reduce-scatter.20.cloned.1.call-update) | async-done | bytes 294928 | tf_op jit(solution)/shard_map/reduce_scatter | solution.py:281
  (257 shorter events, 327.2 us)
Async XLA Ops:
  7.2 62.4 %all-gather.16.cloned.1.call-start = ((), (), s32[]{:S(2)}) async-start(), calls=%async_computation.13 | async-start | bytes 1253376 | tf_op jit(solution)/shard_map/all_gather | solution.py:124
  7.9 74.7 %all-gather.12.cloned.1.call-start = ((), (), s32[]{:S(2)}) async-start(), calls=%async_computation.11 | async-start | bytes 4718592 | tf_op jit(solution)/shard_map/all_gather | solution.py:153
  61.3 81.2 %all-gather.14.cloned.1.call-start = ((), (), s32[]{:S(2)}) async-start(), calls=%async_computation.12 | async-start | bytes 1253376 | tf_op jit(solution)/shard_map/all_gather | solution.py:125
  62.1 144.0 %all-gather.18.cloned.1.call-start = ((), (), s32[]{:S(2)}) async-start(), calls=%async_computation.14 | async-start | bytes 2506752 | tf_op jit(solution)/shard_map/all_gather | solution.py:123
  62.6 206.7 %all-gather.20.cloned.1.call-start = ((), (), s32[]{:S(2)}) async-start(), calls=%async_computation.15 | async-start | bytes 2506752 | tf_op jit(solution)/shard_map/all_gather | solution.py:126
  63.2 226.2 %reduce-scatter.12.cloned.1.call-start = ((), (), s32[]{:S(2)}) async-start(), calls=%async_computation.16 | async-start | bytes 9437184 | tf_op jit(solution)/shard_map/reduce_scatter | solution.py:183
  276.8 110.8 %all-gather.24.cloned.1.call-start = ((), (), s32[]{:S(2)}) async-start(), calls=%async_computation.18 | async-start | bytes 6684672 | tf_op jit(solution)/shard_map/all_gather | solution.py:127
  277.6 122.8 %all-gather.22.cloned.1.call-start = ((), (), s32[]{:S(2)}) async-start(), calls=%async_computation.17 | async-start | bytes 4718592 | tf_op jit(solution)/shard_map/all_gather | solution.py:190
  277.6 384.7 %copy-start.28 = (f32[1536]{0:T(1024)}, f32[1536]{0:T(1024)S(1)}, u32[]{:S(2)}) copy-start(f32[1536]{0:T(1024)S(1)} %convert_element_type.89) | copy-start | bytes 18436
  292.2 370.1 %copy-start.2 = (f32[512,1536]{1,0:T(8,128)}, f32[512,1536]{1,0:T(8,128)S(1)}, u32[]{:S(2)}) copy-start(f32[512,1536]{1,0:T(8,128)S(1)} %get-tuple-element.194) | copy-start | bytes 9437188
  294.0 203.8 %all-gather.26.cloned.1.call-start = ((), (), s32[]{:S(2)}) async-start(), calls=%async_computation.19 | async-start | bytes 6684672 | tf_op jit(solution)/shard_map/all_gather | solution.py:128
  294.7 215.2 %all-gather.30.cloned.1.call-start = ((), (), s32[]{:S(2)}) async-start(), calls=%async_computation.22 | async-start | bytes 4718592 | tf_op jit(solution)/shard_map/all_gather | solution.py:204
  295.3 312.0 %all-gather.28.cloned.1.call-start = ((), (), s32[]{:S(2)}) async-start(), calls=%async_computation.20 | async-start | bytes 6684672 | tf_op jit(solution)/shard_map/all_gather | solution.py:129
  296.0 362.9 %reduce-scatter.16.cloned.1.call-start = ((), (), s32[]{:S(2)}) async-start(), calls=%async_computation.23 | async-start | bytes 9437184 | tf_op jit(solution)/shard_map/reduce_scatter | solution.py:213
  646.2 33.2 %all-gather.32.cloned.1.call-start = ((), (), s32[]{:S(2)}) async-start(), calls=%async_computation.24 | async-start | bytes 4718592 | tf_op jit(solution)/shard_map/all_gather | solution.py:222
  665.1 264.1 %reduce-scatter.18.cloned.1.call-start = ((), (), s32[]{:S(2)}) async-start(), calls=%async_computation.25 | async-start | bytes 4718592 | tf_op jit(solution)/shard_map/reduce_scatter | solution.py:262
  853.2 159.6 %reduce-scatter.14.cloned.1.call-start = ((), (), s32[]{:S(2)}) async-start(), calls=%async_computation.21 | async-start | bytes 4718592 | tf_op jit(solution)/shard_map/reduce_scatter | solution.py:197
  864.7 154.2 %reduce-scatter.22.cloned.1.call-start = ((), (), s32[]{:S(2)}) async-start(), calls=%async_computation.27 | async-start | bytes 2506752 | tf_op jit(solution)/shard_map/reduce_scatter | solution.py:282
  870.1 279.2 %reduce-scatter.24.cloned.1.call-start = ((), (), s32[]{:S(2)}) async-start(), calls=%async_computation.28 | async-start | bytes 2506752 | tf_op jit(solution)/shard_map/reduce_scatter | solution.py:283
  875.3 481.7 %reduce-scatter.28.cloned.1.call-start = ((), (), s32[]{:S(2)}) async-start(), calls=%async_computation.30 | async-start | bytes 13369344 | tf_op jit(solution)/shard_map/reduce_scatter | solution.py:285
  888.0 677.5 %reduce-scatter.30.cloned.1.call-start = ((), (), s32[]{:S(2)}) async-start(), calls=%async_computation.31 | async-start | bytes 13369344 | tf_op jit(solution)/shard_map/reduce_scatter | solution.py:286
  900.6 873.2 %reduce-scatter.32.cloned.1.call-start = ((), (), s32[]{:S(2)}) async-start(), calls=%async_computation.32 | async-start | bytes 13369344 | tf_op jit(solution)/shard_map/reduce_scatter | solution.py:287
  913.1 1004.9 %reduce-scatter.26.cloned.1.call-start = ((), (), s32[]{:S(2)}) async-start(), calls=%async_computation.29 | async-start | bytes 5013504 | tf_op jit(solution)/shard_map/reduce_scatter | solution.py:284
  921.2 1140.3 %reduce-scatter.20.cloned.1.call-start = ((), (), s32[]{:S(2)}) async-start(), calls=%async_computation.26 | async-start | bytes 5013504 | tf_op jit(solution)/shard_map/reduce_scatter | solution.py:281
  (49 other events, 1198.2 us)
Sparse Core Ops, SparseCore 0:
  10.8 58.7 all-gather.15
  71.7 10.8 all-gather.11
  85.4 57.0 all-gather.13
  145.1 60.8 all-gather.17
  208.7 60.5 all-gather.19
  276.9 12.3 reduce-scatter.11
  292.2 95.4 all-gather.23
  389.7 10.6 all-gather.21
  403.2 94.5 all-gather.25
  499.2 10.6 all-gather.29
  512.7 94.5 all-gather.27
  646.3 12.5 reduce-scatter.15
  665.2 14.1 all-gather.31
  853.3 12.3 reduce-scatter.17
  867.8 12.4 reduce-scatter.13
  885.6 130.3 reduce-scatter.21
  1021.4 127.8 reduce-scatter.23
  1155.3 201.6 reduce-scatter.27
  1363.2 202.2 reduce-scatter.29
  1571.6 202.2 reduce-scatter.31
  1779.6 138.3 reduce-scatter.25
  1923.7 137.7 reduce-scatter.19
where the time goes:
time: 2080 us; the launch traced here: 2070 us
  waiting for transfers between devices  1530 us (74%)
  matrix products  211 us (10%)
  local copies, waits for them, and re-layouts  142 us (7%)
  blocking collectives  124 us (6%)
  other arithmetic  41.2 us (2%)
    reduce_scatter x1, waiting for transfers between devices, shards(): lax.psum_scatter(grad_up, 'dp', scatter_dimension=0, tiled=True)  208 us
    reduce_scatter x1, waiting for transfers between devices, shards(): lax.psum_scatter(grad_down, 'dp', scatter_dimension=1, tiled=True)  208 us
    reduce_scatter x1, waiting for transfers between devices, shards(): lax.psum_scatter(grad_gate, 'dp', scatter_dimension=0, tiled=True)  208 us
    reduce_scatter x1, waiting for transfers between devices, shards(): lax.psum_scatter(grad_out, 'dp', scatter_dimension=1, tiled=True)  144 us
    reduce_scatter x1, waiting for transfers between devices, shards(): lax.psum_scatter(grad_query, 'dp', scatter_dimension=0, tiled=True)  144 us
    reduce_scatter x1, waiting for transfers between devices, shards(): lax.psum_scatter(grad_value, 'dp', scatter_dimension=0, tiled=True)  130 us
    unnamed x2, blocking collectives  122 us
    all_gather x1, waiting for transfers between devices, shards(): lax.all_gather(down_weight, 'dp', axis=1, tiled=True)  97.4 us
  transfers between devices with their start and end apart: 22, of which 19 were waited for; matrix products, arithmetic and copies ran while one was open for 8% of the time, Pallas kernels for 0%

commit v1 on v0

v1 whole, which is shorter than its diff:
```python
import functools
import math

import jax
import jax.numpy as jnp
from jax import lax
from jax.experimental import pallas as pl
from jax.experimental.pallas import tpu as pltpu
from jax.sharding import PartitionSpec as P

QUERY_HEADS = 16
KEY_VALUE_HEADS = 8
HEAD_SIZE = 96
SEQUENCE_LENGTH = 512

EPSILON = 1e-05
THETA_BASE = 100000.0
MESH = pl.DeviceIdType.MESH


def place():
    d = lax.axis_index("dp")
    return lax.div(d, 4), lax.rem(lax.div(d, 2), 2), lax.rem(d, 2), lax.axis_index("tensor")

def dev(z, y, x, c):
    return (z * 4 + y * 2 + x, c)

def enter(line, pos):
    z, y, x, c = pos
    barrier = pltpu.get_barrier_semaphore()
    def greet(who):
        pl.semaphore_signal(barrier, inc=1, device_id=who, device_id_type=MESH)
    greet(dev(z, y, x, 1 - c)); greet(dev(z, y, 1 - x, c)); greet(dev(z, 1 - y, x, c))
    @pl.when(z > 0)
    def _(): greet(dev(z - 1, y, x, c))
    @pl.when(z < line - 1)
    def _(): greet(dev(z + 1, y, x, c))
    pl.semaphore_wait(barrier, 3 + (z > 0).astype(jnp.int32) + (z < line - 1).astype(jnp.int32))

class Gather:
    def __init__(self, line, pos, shards, fulls, chunks, send, recv, local):
        self.line, self.pos, self.shards, self.fulls, self.chunks = line, pos, shards, fulls, chunks
        self.send, self.recv, self.local = send, recv, local
        self.steps = line + 3
    def region(self, t, have, z=None):
        w, off, width, _ = self.chunks[t]
        pz, py, px, c = self.pos
        full = self.fulls[w]
        half = full.shape[-1] // 2
        cols = pl.ds(pl.multiple_of(c * half + off, 128), width)
        every = slice(None)
        zi = z if z is not None else (every if "z" in have else pz)
        return full.at[zi, every if "y" in have else py, every if "x" in have else px, :, cols]
    def own(self, t):
        w, off, width, _ = self.chunks[t]
        return self.shards[w].at[:, pl.ds(off, width)]
    def local_copy(self, t):
        return pltpu.make_async_copy(self.own(t), self.region(t, ""), self.local.at[t])
    def copy(self, t, slot, src, dst, who):
        return pltpu.make_async_remote_copy(src_ref=src, dst_ref=dst, send_sem=self.send.at[t, slot], recv_sem=self.recv.at[t, slot], device_id=who, device_id_type=MESH)
    def swap(self, t, axis, have):
        z, y, x, c = self.pos
        who = {"y": dev(z, 1 - y, x, c), "x": dev(z, y, 1 - x, c), "c": dev(z, y, x, 1 - c)}[axis]
        slot = 2 * (self.line - 1) + "yxc".index(axis)
        mine = self.region(t, have) if have else self.own(t)
        land = self.region(t, have)
        if axis == "y":
            w, off, width, _ = self.chunks[t]
        return self.copy(t, slot, mine, land, who)
    def hop(self, t, h, up, have, act):
        z, y, x, c = self.pos
        slot = (h - 1) * 2 + up
        if up:
            block, who, there, here = z - (h - 1), dev(z + 1, y, x, c), (z + 1 < self.line) & (z >= h - 1), z >= h
            incoming = z - h
        else:
            block, who, there, here = z + (h - 1), dev(z - 1, y, x, c), (z > 0) & (z + h - 1 < self.line), z + h < self.line
            incoming = z + h
        if act == "recv":
            @pl.when(here)
            def _():
                r = self.region(t, have, incoming)
                self.copy(t, slot, r, r, dev(z, y, x, 1 - c)).wait_recv()
        else:
            @pl.when(there)
            def _():
                r = self.region(t, have, block)
                src = self.own(t) if (h == 1 and not have) else r
                cp = self.copy(t, slot, src, r, who)
                if act == "start": cp.start()
                else: cp.wait_send()
    def plan(self, t):
        order, out, have = self.chunks[t][3], [], ""
        acts = []
        for axis in order:
            if axis == "z":
                for h in range(1, self.line): acts.append(("z", h, have))
            else: acts.append((axis, 0, have))
            have += axis
        acts.append(("c", 0, have))
        return acts
    def act(self, t, a, what):
        axis, h, have = a
        if axis == "z":
            for up in (1, 0): self.hop(t, h, up, have, what)
        else:
            cp = self.swap(t, axis, have)
            {"start": cp.start, "recv": cp.wait_recv, "sent": cp.wait_send}[what]()
    def step(self, t, s):
        acts = self.plan(t)
        if s > 0: self.act(t, acts[s - 1], "recv")
        if s == 1: self.local_copy(t).wait()
        if s < len(acts): self.act(t, acts[s], "start")
    def finish(self, t):
        for a in self.plan(t): self.act(t, a, "sent")

def gather_body(line, chunks, n, *refs):
    shards, fulls, (send, recv, local) = refs[:n], refs[n:2 * n], refs[2 * n:]
    pos = place()
    g = Gather(line, pos, shards, fulls, chunks, send, recv, local)
    for t in range(len(chunks)): g.local_copy(t).start()
    enter(line, pos)
    for p in range(len(chunks) + g.steps - 1):
        for s in range(g.steps):
            if 0 <= p - s < len(chunks): g.step(p - s, s)
    for t in range(len(chunks)): g.finish(t)

def gather(line, chunks, shards, cid):
    n = len(shards)
    slots = 2 * (line - 1) + 3
    return pl.pallas_call(
        functools.partial(gather_body, line, chunks, n),
        out_shape=[jax.ShapeDtypeStruct((line, 2, 2, s.shape[0], 2 * s.shape[1]), s.dtype) for s in shards],
        in_specs=[pl.BlockSpec(memory_space=pltpu.VMEM)] * n,
        out_specs=[pl.BlockSpec(memory_space=pl.ANY)] * n,
        scratch_shapes=[pltpu.SemaphoreType.DMA((len(chunks), slots)), pltpu.SemaphoreType.DMA((len(chunks), slots)), pltpu.SemaphoreType.DMA((len(chunks),))],
        compiler_params=pltpu.CompilerParams(collective_id=cid, has_side_effects=True),
        name="weight_gather",
    )(*shards)


class Scatter:
    def __init__(self, line, pos, grads, outs, chunks, bufs, send, recv, load):
        self.line, self.pos, self.grads, self.outs, self.chunks, self.bufs = line, pos, grads, outs, chunks, bufs
        self.send, self.recv, self.load = send, recv, load
    def copy(self, t, slot, src, dst, who):
        return pltpu.make_async_remote_copy(src_ref=src, dst_ref=dst, send_sem=self.send.at[t, slot], recv_sem=self.recv.at[t, slot], device_id=who, device_id_type=MESH)
    def pick(self, ref, dims, **at):
        return ref.at[tuple(at.get(d, slice(None)) for d in dims)]
    def source(self, t):
        w, off, width, _ = self.chunks[t]
        return self.grads[w].at[:, :, :, :, pl.ds(off, width)]
    def merge(self, dst, a, b, dims):
        def go(lead, rest):
            if not rest:
                dst[lead] = a[lead] + b[lead]
            elif rest[0] == "z":
                @pl.loop(0, self.line)
                def _(i): go(lead + (i,), rest[1:])
            else:
                for i in range(2): go(lead + (i,), rest[1:])
        go((), dims)
    def final(self, t, *parts):
        w, off, width, _ = self.chunks[t]
        total = parts[0].astype(jnp.float32)
        for p in parts[1:]: total = total + p.astype(jnp.float32)
        self.outs[w][:, pl.ds(off, width)] = total
    def steps(self, t):
        z, y, x, c = self.pos
        order = self.chunks[t][3]
        buf = self.bufs[t]
        todo, dims, cur, first, used = [], "zyx", self.source(t), True, 0
        pending = []
        line = self.line
        for n, axis in enumerate(order):
            last = n == 2
            rest = dims.replace(axis, "")
            if axis in "xy":
                me = {"x": x, "y": y}[axis]
                who = {"x": dev(z, y, 1 - x, c), "y": dev(z, 1 - y, x, c)}[axis]
                slot = 2 * (line - 1) + "yx".index(axis)
                land = buf[axis]
                give = self.pick(cur, dims, **{axis: 1 - me})
                keep = self.pick(cur, dims, **{axis: me})
                cp = self.copy(t, slot, give, land, who)
                if first:
                    ld = pltpu.make_async_copy(keep, buf["own"], self.load.at[t])
                    def begin(cp=cp, ld=ld): cp.start(); ld.start()
                    todo.append(begin)
                    have = buf["own"]
                else:
                    ld = None
                    have = keep
                    self_begin = cp.start
                    prev = todo.pop()
                    todo.append(lambda prev=prev, b=self_begin: (prev(), b()))
                def end(cp=cp, ld=ld, have=have, land=land, rest=rest, last=last):
                    if ld is not None: ld.wait()
                    cp.wait_recv()
                    if last: self.final(t, land[...], have[...])
                    else: self.merge(land, land, have, rest)
                todo.append(end)
                cur = land
                pending.append(cp.wait_send)
            else:
                up, dn = buf["up"], buf["dn"]
                if first:
                    ld = pltpu.make_async_copy(cur, buf["own"], self.load.at[t])
                    todo.append(ld.start)
                    cur = buf["own"]
                else: ld = None
                for j in range(line - 1):
                    def hop(j=j, cur=cur, ld=ld, rest=rest):
                        if j == 0 and ld is not None: ld.wait()
                        for way, ref, target, src_z, edge in ((0, up, line - 1 - j, z - 1, z == 0), (1, dn, j, z + 1, z == line - 1)):
                            slot = 2 * j + way
                            nxt = dev(z + 1, y, x, c) if way == 0 else dev(z - 1, y, x, c)
                            passes = (target > z) if way == 0 else (target < z)
                            @pl.when(passes & edge)
                            def _(): self.copy(t, slot, cur.at[target], ref.at[j], nxt).start()
                            @pl.when(passes & ~edge)
                            def _():
                                cp = self.copy(t, slot, ref.at[j], ref.at[j], nxt)
                                cp.wait_recv()
                                self.merge(ref.at[j], ref.at[j], cur.at[target], rest)
                                cp.start()
                    todo.append(hop)
                    for way in (0, 1):
                        def drain(j=j, way=way, cur=cur):
                            target = line - 1 - j if way == 0 else j
                            passes = (target > z) if way == 0 else (target < z)
                            @pl.when(passes)
                            def _(): self.copy(t, 2 * j + way, cur.at[target], (up if way == 0 else dn).at[j], dev(z, y, x, 1 - c)).wait_send()
                        pending.append(drain)
                def close(cur=cur, rest=rest, last=last):
                    ku, kd = line - 1 - z, z
                    def arrived(way, k):
                        ref = up if way == 0 else dn
                        self.copy(t, 2 * k + way, ref.at[k], ref.at[k], dev(z, y, x, 1 - c)).wait_recv()
                    mine = cur.at[z]
                    @pl.when(z == 0)
                    def _():
                        arrived(1, kd)
                        if last: self.final(t, mine[...], dn[kd])
                        else: self.merge(mine, mine, dn.at[kd], rest)
                    @pl.when(z == line - 1)
                    def _():
                        arrived(0, ku)
                        if last: self.final(t, mine[...], up[ku])
                        else: self.merge(mine, mine, up.at[ku], rest)
                    @pl.when((z > 0) & (z < line - 1))
                    def _():
                        arrived(0, ku)
                        arrived(1, kd)
                        if last: self.final(t, mine[...], up[ku], dn[kd])
                        else:
                            self.merge(mine, mine, up.at[ku], rest)
                            self.merge(mine, mine, dn.at[kd], rest)
                todo.append(close)
                cur = cur.at[z]
            dims, first = rest, False
        return todo, pending

def scatter_bufs(line, rows, width, order):
    size = {"z": line, "y": 2, "x": 2}
    dims, out = "zyx", {}
    for n, axis in enumerate(order):
        rest = dims.replace(axis, "")
        shape = tuple(size[d] for d in rest) + (rows, width)
        if axis == "z":
            if n == 0: out["own"] = (line,) + shape
            out["up"] = (line - 1,) + shape
            out["dn"] = (line - 1,) + shape
        else:
            if n == 0: out["own"] = shape
            out[axis] = shape
        dims = rest
    return out

def scatter_body(line, chunks, n, names, *refs):
    grads, outs, rest = refs[:n], refs[n:2 * n], list(refs[2 * n:])
    bufs = [{k: rest.pop(0) for k in ks} for ks in names]
    land, pair, send, recv, load = rest
    pos = place()
    s = Scatter(line, pos, grads, outs, chunks, bufs, send, recv, load)
    enter(line, pos)
    plans = [s.steps(t) for t in range(len(chunks))]
    depth = max(len(p[0]) for p in plans)
    for p in range(len(chunks) + depth - 1):
        for k in range(depth):
            t = p - k
            if 0 <= t < len(chunks) and k < len(plans[t][0]): plans[t][0][k]()
    for _, pending in plans:
        for f in pending: f()
    z, y, x, c = pos
    cp = pltpu.make_async_remote_copy(src_ref=outs[0], dst_ref=land, send_sem=pair.at[0], recv_sem=pair.at[1], device_id=dev(z, y, x, 1 - c), device_id_type=MESH)
    cp.start()
    cp.wait()
    outs[0][...] += land[...]

def scatter(line, chunks, grads, cid):
    n = len(grads)
    slots = 2 * (line - 1) + 2
    scratch, names = [], []
    for w, off, width, order in chunks:
        shapes = scatter_bufs(line, grads[w].shape[3], width, order)
        names.append(tuple(shapes))
        scratch += [pltpu.VMEM(s, grads[w].dtype) for s in shapes.values()]
    T = len(chunks)
    return pl.pallas_call(
        functools.partial(scatter_body, line, chunks, n, names),
        out_shape=[jax.ShapeDtypeStruct(g.shape[3:], jnp.float32) for g in grads],
        in_specs=[pl.BlockSpec(memory_space=pl.ANY)] * n,
        out_specs=[pl.BlockSpec(memory_space=pltpu.VMEM)] * n,
        scratch_shapes=scratch + [pltpu.VMEM(grads[0].shape[3:], jnp.float32), pltpu.SemaphoreType.DMA((2,)), pltpu.SemaphoreType.DMA((T, slots)), pltpu.SemaphoreType.DMA((T, slots)), pltpu.SemaphoreType.DMA((T,))],
        compiler_params=pltpu.CompilerParams(collective_id=cid, has_side_effects=True, vmem_limit_bytes=63 * 2**20),
        name="gradient_scatter",
    )(*grads)


def rope_tables(length, width):
    half_width = width // 2
    inverse = THETA_BASE ** (-(jnp.arange(half_width, dtype=jnp.float32) * 2.0 / width))
    angles = jnp.arange(length, dtype=jnp.float32)[:, None] * inverse[None, :]
    cosine, sine = jnp.cos(angles), jnp.sin(angles)
    return jnp.concatenate([cosine, cosine], axis=1), jnp.concatenate([-sine, sine], axis=1)


def turn(x, cosine, sine):
    half = x.shape[-1] // 2
    return x * cosine + jnp.concatenate([x[:, half:], x[:, :half]], axis=1) * sine


def dot_nt(a, b):
    return lax.dot_general(a, b, (((1,), (1,)), ((), ())), preferred_element_type=jnp.float32)


def dot_tn(a, b):
    return lax.dot_general(a, b, (((0,), (0,)), ((), ())), preferred_element_type=jnp.float32)


def dot_nn(a, b):
    return jnp.dot(a, b, preferred_element_type=jnp.float32)


BLOCK = 128


def causal_weights(q, k, b, heads):
    scores = dot_nt(q, k) * (1.0 / math.sqrt(HEAD_SIZE))
    n = scores.shape[1]
    row = lax.broadcasted_iota(jnp.int32, scores.shape, 0) % BLOCK + b * BLOCK
    keep = row >= lax.broadcasted_iota(jnp.int32, scores.shape, 1)
    scores = jnp.where(keep, scores, -jnp.inf)
    log_total = jnp.log(jnp.sum(jnp.exp(scores), axis=1, keepdims=True))
    return jnp.exp(scores - log_total)


def rows_of(ref, first, heads, rows):
    return jnp.concatenate([ref[first + i, rows] for i in range(heads)], axis=0)


def attend_kernel(heads, groups, qkv, cosine, sine, q_out, k_out, v_out, mixed_out, mixed):
    share = heads // groups
    blocks = qkv.shape[0] // BLOCK

    @pl.loop(0, blocks)
    def _(r):
        rows = pl.ds(pl.multiple_of(r * BLOCK, BLOCK), BLOCK)
        cos, sin = cosine[rows, :], sine[rows, :]
        for h in range(heads + 2 * groups):
            x = qkv[rows, h * HEAD_SIZE : (h + 1) * HEAD_SIZE]
            if h < heads:
                q_out[h, rows] = turn(x, cos, sin).astype(q_out.dtype)
            elif h < heads + groups:
                k_out[h - heads, rows] = turn(x, cos, sin).astype(k_out.dtype)
            else:
                v_out[h - heads - groups, rows] = x.astype(v_out.dtype)

    @pl.loop(0, groups)
    def _(g):
        for b in range(blocks):
            rows, n = pl.ds(b * BLOCK, BLOCK), (b + 1) * BLOCK
            q = rows_of(q_out, g * share, share, rows)
            w = causal_weights(q, k_out[g, :n], b, share).astype(v_out.dtype)
            m = dot_nn(w, v_out[g, :n]).astype(mixed.dtype)
            for i in range(share):
                mixed[g * share + i, rows] = m[i * BLOCK : (i + 1) * BLOCK]

    @pl.loop(0, blocks)
    def _(r):
        rows = pl.ds(pl.multiple_of(r * BLOCK, BLOCK), BLOCK)
        mixed_out[rows, :] = jnp.concatenate([mixed[h, rows] for h in range(heads)], axis=1)


def attend(qkv, cosine, sine, halves):
    tokens = qkv.shape[0]
    heads, groups = QUERY_HEADS // halves, KEY_VALUE_HEADS // halves
    width = qkv.shape[1] // halves
    head = lambda n: pl.BlockSpec((n, tokens, HEAD_SIZE), lambda c: (c, 0, 0))
    table = pl.BlockSpec((tokens, HEAD_SIZE), lambda c: (0, 0))
    bf16 = jnp.bfloat16
    return pl.pallas_call(
        functools.partial(attend_kernel, heads, groups),
        grid=(halves,),
        out_shape=[
            jax.ShapeDtypeStruct((QUERY_HEADS, tokens, HEAD_SIZE), bf16),
            jax.ShapeDtypeStruct((KEY_VALUE_HEADS, tokens, HEAD_SIZE), bf16),
            jax.ShapeDtypeStruct((KEY_VALUE_HEADS, tokens, HEAD_SIZE), bf16),
            jax.ShapeDtypeStruct((tokens, QUERY_HEADS * HEAD_SIZE), bf16),
        ],
        in_specs=[pl.BlockSpec((tokens, width), lambda c: (0, c)), table, table],
        out_specs=[head(heads), head(groups), head(groups), pl.BlockSpec((tokens, heads * HEAD_SIZE), lambda c: (0, c))],
        scratch_shapes=[pltpu.VMEM((heads, tokens, HEAD_SIZE), bf16)],
        compiler_params=pltpu.CompilerParams(vmem_limit_bytes=60 * 2**20),
        name="attend",
    )(qkv, cosine, sine)


def attend_back_kernel(heads, groups, q, k, v, mixed, grad_mixed, cosine, sine, out, gm, dots, dq, dk, dv):
    share = heads // groups
    blocks = out.shape[0] // BLOCK
    scale = 1.0 / math.sqrt(HEAD_SIZE)

    @pl.loop(0, blocks)
    def _(r):
        rows = pl.ds(pl.multiple_of(r * BLOCK, BLOCK), BLOCK)
        for h in range(heads):
            lanes = slice(h * HEAD_SIZE, (h + 1) * HEAD_SIZE)
            g = grad_mixed[rows, lanes]
            dots[h, rows] = jnp.sum(g * mixed[rows, lanes].astype(jnp.float32), axis=1, keepdims=True)
            gm[h, rows] = g.astype(gm.dtype)

    dk[...] = jnp.zeros_like(dk)
    dv[...] = jnp.zeros_like(dv)

    @pl.loop(0, groups)
    def _(g):
        for b in range(blocks):
            rows, n = pl.ds(b * BLOCK, BLOCK), (b + 1) * BLOCK
            qb, gb, db = (rows_of(ref, g * share, share, rows) for ref in (q, gm, dots))
            kb, vb = k[g, :n], v[g, :n]
            p = causal_weights(qb, kb, b, share)
            ds = (p * (dot_nt(gb, vb) - db)).astype(qb.dtype)
            dv[g, :n] += dot_tn(p.astype(qb.dtype), gb)
            dk[g, :n] += dot_tn(ds, qb)
            d = dot_nn(ds, kb) * scale
            for i in range(share):
                dq[g * share + i, rows] = d[i * BLOCK : (i + 1) * BLOCK]

    @pl.loop(0, blocks)
    def _(r):
        rows = pl.ds(pl.multiple_of(r * BLOCK, BLOCK), BLOCK)
        cos, sin = cosine[rows, :], -sine[rows, :]
        parts = [turn(dq[h, rows], cos, sin) for h in range(heads)]
        parts += [turn(dk[g, rows] * scale, cos, sin) for g in range(groups)]
        parts += [dv[g, rows] for g in range(groups)]
        out[rows, :] = jnp.concatenate([part.astype(out.dtype) for part in parts], axis=1)


def attend_back(q, k, v, mixed, grad_mixed, cosine, sine, halves):
    tokens = q.shape[1]
    heads, groups = QUERY_HEADS // halves, KEY_VALUE_HEADS // halves
    width = (heads + 2 * groups) * HEAD_SIZE
    head = lambda n: pl.BlockSpec((n, tokens, HEAD_SIZE), lambda c: (c, 0, 0))
    table = pl.BlockSpec((tokens, HEAD_SIZE), lambda c: (0, 0))
    flat = pl.BlockSpec((tokens, heads * HEAD_SIZE), lambda c: (0, c))
    return pl.pallas_call(
        functools.partial(attend_back_kernel, heads, groups),
        grid=(halves,),
        out_shape=jax.ShapeDtypeStruct((tokens, width * halves), jnp.bfloat16),
        in_specs=[head(heads), head(groups), head(groups), flat, flat, table, table],
        out_specs=pl.BlockSpec((tokens, width), lambda c: (0, c)),
        scratch_shapes=[
            pltpu.VMEM((heads, tokens, HEAD_SIZE), jnp.bfloat16),
            pltpu.VMEM((heads, tokens, 1), jnp.float32),
            pltpu.VMEM((heads, tokens, HEAD_SIZE), jnp.float32),
            pltpu.VMEM((groups, tokens, HEAD_SIZE), jnp.float32),
            pltpu.VMEM((groups, tokens, HEAD_SIZE), jnp.float32),
        ],
        compiler_params=pltpu.CompilerParams(vmem_limit_bytes=60 * 2**20),
        name="attend_back",
    )(q, k, v, mixed, grad_mixed, cosine, sine)


def norm_back(grad_normed, unit_rows, inverse_rms, gain):
    scaled = grad_normed * gain
    inner = jnp.mean(scaled * unit_rows, axis=1, keepdims=True)
    return (inverse_rms * (scaled - unit_rows * inner), jnp.sum(grad_normed * unit_rows, axis=0))


def cut(halves, width, mix):
    chunks, k = [], 0
    for w, half in enumerate(halves):
        pieces = -(-half // width)
        while half % (pieces * 128):
            pieces += 1
        for i in range(pieces):
            chunks.append((w, i * (half // pieces), half // pieces, mix[k % len(mix)]))
            k += 1
    return tuple(chunks)


GATHER_MIX = ("xyz", "zyx", "zxy", "yxz", "zyx", "zxy", "zyx", "zxy")
SCATTER_MIX = ("xyz", "yxz")


def layer(n_dp, n_tensor, hidden_in, query_weight, key_matrix, value_matrix, out_weight, gate_weight, up_weight, down_weight, attention_gain, feedforward_gain, cotangent):
    line = n_dp // 4
    rows = attention_gain.shape[0]
    width = rows * n_dp
    bf16, f32 = jnp.bfloat16, jnp.float32
    side = lax.axis_index("tensor")

    gains = jnp.zeros((8, 128), bf16).at[0, :rows].set(attention_gain).at[1, :rows].set(feedforward_gain)
    shards = [gains, jnp.concatenate([query_weight, key_matrix, value_matrix], axis=1), out_weight.T, gate_weight, up_weight, down_weight.T]
    fulls = gather(line, cut([s.shape[1] for s in shards], 512, GATHER_MIX), shards, 0)
    all_gains = fulls[0].reshape(n_dp, 8, -1)
    gain_first = all_gains[:, 0, :rows].reshape(1, width).astype(f32)
    gain_second = all_gains[:, 1, :rows].reshape(1, width).astype(f32)
    w_qkv, w_out, w_gate, w_up, w_down = (f.reshape(width, f.shape[-1]) for f in fulls[1:])

    cosine, sine = rope_tables(SEQUENCE_LENGTH, HEAD_SIZE)
    x = hidden_in.astype(f32)
    inverse_one = lax.rsqrt(jnp.mean(x * x, axis=1, keepdims=True) + EPSILON)
    unit_one = x * inverse_one
    normed_one = (unit_one * gain_first).astype(bf16)
    q, k, v, mixed = attend(dot_nn(normed_one, w_qkv), cosine, sine, n_tensor)
    middle = x + dot_nt(mixed, w_out)
    inverse_two = lax.rsqrt(jnp.mean(middle * middle, axis=1, keepdims=True) + EPSILON)
    unit_two = middle * inverse_two
    normed_two = (unit_two * gain_second).astype(bf16)
    gate = dot_nn(normed_two, w_gate)
    up = dot_nn(normed_two, w_up)
    sigma = jax.nn.sigmoid(gate)
    hidden = (gate * sigma * up).astype(bf16)
    hidden_out = (middle + dot_nt(hidden, w_down)).astype(bf16)
    grad_hidden = dot_nn(cotangent, w_down)
    grad_up_act = (grad_hidden * gate * sigma).astype(bf16)
    grad_gate_act = (grad_hidden * up * sigma * (1.0 + gate * (1.0 - sigma))).astype(bf16)
    grad_normed_two = dot_nt(grad_gate_act, w_gate) + dot_nt(grad_up_act, w_up)
    middle_part, second_part = norm_back(grad_normed_two, unit_two, inverse_two, gain_second)
    grad_middle = cotangent.astype(f32) + middle_part
    grad_middle_round = grad_middle.astype(bf16)
    grad_mixed = dot_nn(grad_middle_round, w_out)
    grad_qkv_act = attend_back(q, k, v, mixed, grad_mixed, cosine, sine, n_tensor)
    grad_normed_one = dot_nt(grad_qkv_act, w_qkv)
    first_part, first_gain = norm_back(grad_normed_one, unit_one, inverse_one, gain_first)
    grad_in = grad_middle + first_part

    swap = [(i, i ^ 1) for i in range(n_tensor)]
    other = lambda a: lax.ppermute(a, "tensor", swap)

    def of_half(a, which):
        size = a.shape[1] // n_tensor
        return lax.dynamic_slice_in_dim(a, which * size, size, axis=1)

    both = lambda a: jnp.concatenate([a, other(a)], axis=0)
    both_half = lambda a: jnp.concatenate([of_half(a, side), other(of_half(a, 1 - side))], axis=0)
    n1, n2, ct, gm = both(normed_one), both(normed_two), both(cotangent), both(grad_middle_round)
    weight_grad = lambda a, b: dot_tn(a, both_half(b)).astype(bf16)
    grads = [
        weight_grad(ct, hidden),
        weight_grad(n2, grad_gate_act),
        weight_grad(n2, grad_up_act),
        weight_grad(gm, mixed),
        weight_grad(n1, grad_qkv_act),
    ]
    parts = jnp.stack([first_gain, second_part]).reshape(2, n_dp, rows).transpose(1, 0, 2)
    parts = jnp.pad(parts, ((0, 0), (0, 6), (0, 128 - rows))).astype(bf16)
    grads = [parts.reshape(line, 2, 2, 8, 128)] + [g.reshape(line, 2, 2, rows, g.shape[1]) for g in grads]
    g_gains, g_down, g_gate, g_up, g_out, g_qkv = scatter(line, cut([g.shape[-1] for g in grads], 512, SCATTER_MIX), grads, 1)
    nq, nk = query_weight.shape[1], key_matrix.shape[1]
    return (
        hidden_out,
        grad_in,
        g_qkv[:, :nq],
        g_qkv[:, nq : nq + nk],
        g_qkv[:, nq + nk :],
        g_out.T,
        g_gate,
        g_up,
        g_down.T,
        g_gains[0, :rows],
        g_gains[1, :rows],
    )


def solution(mesh):
    split = P(("dp", "tensor"), None)
    row, column, gain = P("dp", "tensor"), P("tensor", "dp"), P("dp")
    return jax.shard_map(
        functools.partial(layer, mesh.shape["dp"], mesh.shape["tensor"]),
        mesh=mesh,
        in_specs=(split, row, row, row, column, row, row, column, gain, gain, split),
        out_specs=(split, split, row, row, row, column, row, row, column, gain, gain),
        check_vma=False,
    )
```

time: 2080 us -> 789 us (0.38)
  waiting for transfers between devices: 1530 us -> 0.02 us
  Pallas kernels: 0 us -> 582 us
  blocking collectives: 124 us -> 0 us
  local copies, waits for them, and re-layouts: 142 us -> 31.5 us
  matrix products: 211 us -> 155 us
  other arithmetic: 41.2 us -> 13.5 us
    reduce_scatter x11 -> x0, waiting for transfers between devices: 1070 us -> none  [the longest x1 208 us: shards(): lax.psum_scatter(grad_up, 'dp', scatter_dimension=0, tiled=True)]
    pallas_call x0 -> x4, Pallas kernels: none -> 582 us  [the longest x1 282 us: scatter(): pl.pallas_call(functools.partial(scatter_body, line, chunks, n, names), o...]
    all_gather x11 -> x0, waiting for transfers between devices: 460 us -> none  [the longest x1 97.4 us: shards(): lax.all_gather(down_weight, 'dp', axis=1, tiled=True)]
    unnamed x2 -> x0, blocking collectives: 122 us -> none
    dynamic_update_slice x10 -> x0, local copies, waits for them, and re-layouts: 93.8 us -> none  [the longest x8 92.5 us: shards(): lax.map(attend_back, (query_rows, every_key, every_value, rounded_mixture...]
    dot_general x35 -> x15, matrix products: 211 us -> 155 us  [the longest x5 58.3 us: dot_nn(): return jnp.dot(a, b, preferred_element_type=jnp.float32)]
  transfers between devices with their start and end apart: 22 -> 9, of which waited for: 19 -> 0; matrix products, arithmetic and copies ran while one was open for 8% -> 22% of each run, Pallas kernels for 0% -> 8%
where the time goes in v1:
time: 789 us; the launch traced here: 785 us
  Pallas kernels  582 us (74%)
  matrix products  155 us (20%)
  local copies, waits for them, and re-layouts  31.5 us (4%)
  other arithmetic  13.5 us (2%)
    pallas_call x1, Pallas kernels, scatter(): pl.pallas_call(functools.partial(scatter_body, line, chunks, n, names), o...  282 us
    pallas_call x1, Pallas kernels, gather(): pl.pallas_call(functools.partial(gather_body, line, chunks, n), out_shape...  235 us
    dot_general x5, matrix products, dot_nn(): return jnp.dot(a, b, preferred_element_type=jnp.float32)  58.3 us
    dot_general x5, matrix products, dot_nt(): lax.dot_general(a, b, (((1,), (1,)), ((), ())), preferred_element_type=jn...  50.1 us
    dot_general x5, matrix products, dot_tn(): lax.dot_general(a, b, (((0,), (0,)), ((), ())), preferred_element_type=jn...  46.8 us
    pallas_call x1, Pallas kernels, attend_back(): pl.pallas_call(functools.partial(attend_back_kernel, heads, groups), grid...  33.6 us
    pallas_call x1, Pallas kernels, attend(): pl.pallas_call(functools.partial(attend_kernel, heads, groups), grid=(hal...  31 us
  transfers between devices with their start and end apart: 9, of which 0 were waited for; matrix products, arithmetic and copies ran while one was open for 22% of the time, Pallas kernels for 8%

profile of v1, /device:TPU:0, one launch (start us, length us, event | category | flops | bytes accessed | tf_op | source)
XLA Modules:
  0.0 785.2 jit_solution(7027814746684417721)
XLA Ops:
  4.5 235.3 %weight_gather.1 = (bf16[4,2,2,8,256]{4,3,2,1,0:T(8,128)(2,1)}, bf16[4,2,2,96,3072]{4,3,2,1,0:T(8,128)(2,1)}, bf16[4,2,2,96,1536]{4,3,2,1,0:T(8,128)(2,1)}, bf16...) custom-call(bf16[8,128]{1,0:T(8,128)(2,1)} %copy-done.20, ...), custom_call_target="tpu_custom_call" | custom-call | tf_op jit(solution)/shard_map/weight_gather/pallas_call | solution.py:131
  243.3 10.2 %fusion.53.qkv = f32[512,3072]{1,0:T(8,128)} fusion(bf16[512,1536]{1,0:T(8,128)(2,1)} %fusion.18, bf16[1536,3072]{1,0:T(8,128)(2,1)} %bitcast.78), kind=kOutput, calls=%fused_computation.97 | convolution fusion | flops 4831838208 | bytes 17301504 | tf_op jit(solution)/shard_map/dot_general | solution.py:343
  255.6 31.0 %attend.1 = (bf16[16,512,96]{2,1,0:T(8,128)(2,1)}, bf16[8,512,96]{2,1,0:T(8,128)(2,1)}, bf16[8,512,96]{2,1,0:T(8,128)(2,1)}, bf16[512,1536]{1,0:T(8,128)(2,1)}) custom-call(f32[512,3072]{1,0:T(8,128)} %fusion.53.qkv, f32[512,96]{1,0:T(8,128)} %get-tuple-element.97.cosine, f32[512,96]{1,0:T(8,128)} %get-tuple-element.98.sine), custom_call_target="tpu_custom_call" | custom-call | tf_op jit(solution)/shard_map/attend/pallas_call | solution.py:403
  286.5 6.0 multiply_reduce_fusion.2
  294.1 12.4 %fusion.54 = f32[512,4096]{1,0:T(8,128)} fusion(bf16[512,1536]{1,0:T(8,128)(2,1)} %multiply_convert_fusion.1, bf16[1536,4096]{1,0:T(8,128)(2,1)} %bitcast.74), kind=kOutput, calls=%fused_computation.98 | convolution fusion | flops 6442450944 | bytes 22544384 | tf_op jit(solution)/shard_map/dot_general | solution.py:343
  306.5 8.8 %fusion.57 = f32[4096,512]{0,1:T(8,128)} fusion(bf16[512,1536]{1,0:T(8,128)(2,1)S(1)} %copy-done.6, bf16[1536,4096]{1,0:T(8,128)(2,1)S(1)} %bitcast.73), kind=kOutput, calls=%fused_computation.101 | convolution fusion | flops 6442450944 | bytes 22544384 | tf_op jit(solution)/shard_map/dot_general | solution.py:343
  315.3 19.8 %fusion.4 = (bf16[512,4096]{1,0:T(8,128)(2,1)}, bf16[512,4096]{1,0:T(8,128)(2,1)}, bf16[512,4096]{1,0:T(8,128)(2,1)}) fusion(f32[4096,512]{0,1:T(8,128)} %fusion.57, f32[512,4096]{1,0:T(8,128)} %fusion.54, bf16[512,1536]{1,0:T(8,128)(2,1)} %multiply_convert_fusion.1, bf16[1536,4096]{1,0:T(8,128)(2,1)} %bitcast.76), kind=kOutput, calls=%fused_computation.6 | convolution fusion | flops 6476005376 | bytes 43515904 | tf_op jit(solution)/shard_map/dot_general | solution.py:343
  335.1 12.2 %fusion.55 = f32[512,1536]{1,0:T(8,128)} fusion(bf16[512,4096]{1,0:T(8,128)(2,1)} %get-tuple-element.74, bf16[1536,4096]{1,0:T(8,128)(2,1)} %bitcast.77), kind=kOutput, calls=%fused_computation.99 | convolution fusion | flops 6442450944 | bytes 19922944 | tf_op jit(solution)/shard_map/dot_general | solution.py:335
  347.4 10.7 %multiply_reduce_fusion = (bf16[1536]{0:T(1024)(128)(2,1)S(1)}, f32[512]{0:T(512)S(1)}, f32[512,1536]{1,0:T(8,128)S(1)}) fusion(f32[512,1536]{1,0:T(8,128)S(1)} %get-tuple-element.94, f32[512]{0:T(512)S(1)} %add_rsqrt_fusion, f32[1536]{0:T(1024)S(1)} %reshape.187, f32[512,1536]{1,0:T(8,128)} %fusion.55, bf16[512,4096]{1,0:T(8,128)(2,1)S(1)} %copy-done.11, ...), kind=kOutput, calls=%fused_computation.52 | convolution fusion | flops 6447953920 | bytes 26227712 | tf_op jit(solution)/shard_map/dot_general | solution.py:335
  360.5 7.1 fusion.56.grad_mixed
  367.6 33.6 %attend_back.1 = bf16[512,3072]{1,0:T(8,128)(2,1)} custom-call(bf16[16,512,96]{2,1,0:T(8,128)(2,1)} %get-tuple-element.58.q, bf16[8,512,96]{2,1,0:T(8,128)(2,1)} %get-tuple-element.59.k, bf16[8,512,96]{2,1,0:T(8,128)(2,1)} %get-tuple-element.60.v, bf16[512,1536]{1,0:T(8,128)(2,1)} %get-tuple-element.53.mixed, f32[512,1536]{1,0:T(8,128)} %fusion.56.grad_mixed, ...), custom_call_target="tpu_custom_call" | custom-call | tf_op jit(solution)/shard_map/attend_back/pallas_call | solution.py:468
  401.2 3.7 constant_dynamic-slice_fusion.1
  405.1 4.9 constant_dynamic-slice_fusion.5
  410.3 2.5 constant_dynamic-slice_fusion.7
  413.9 9.2 %fusion.23 = (bf16[1536]{0:T(1024)(128)(2,1)S(1)}, f32[512]{0:T(512)S(1)}, f32[512,1536]{1,0:T(8,128)}) fusion(bf16[512,1536]{1,0:T(8,128)(2,1)S(1)} %copy-done.1, f32[512]{0:T(512)S(1)} %add_rsqrt_fusion.1, f32[1536]{0:T(1024)S(1)} %reshape.186, bf16[512,3072]{1,0:T(8,128)(2,1)S(1)} %copy-done.5, bf16[1536,3072]{1,0:T(8,128)(2,1)} %bitcast.79), kind=kOutput, calls=%fused_computation.37 | convolution fusion | flops 4837341184 | bytes 17314816 | tf_op jit(solution)/shard_map/dot_general | solution.py:335
  423.3 12.0 %fusion.37 = bf16[512,1536]{1,0:T(8,128)(2,1)} fusion(f32[512,1536]{1,0:T(8,128)S(1)} %get-tuple-element.94, bf16[512,4096]{1,0:T(8,128)(2,1)} %get-tuple-element.75, bf16[1536,4096]{1,0:T(8,128)(2,1)} %bitcast.70), kind=kOutput, calls=%fused_computation.57 | convolution fusion | flops 6444023808 | bytes 21495808 | tf_op jit(solution)/shard_map/dot_general | solution.py:335
  435.3 2.5 constant_dynamic-slice_fusion.9
  439.6 3.2 fusion.22
  445.6 10.0 %convolution_convert_fusion = bf16[1536,1536]{1,0:T(8,128)(2,1)} fusion(bf16[512,1536]{1,0:T(8,128)(2,1)} %collective-permute-done.7, bf16[512,1536]{1,0:T(8,128)(2,1)} %fusion.18, bf16[512,1536]{1,0:T(8,128)(2,1)} %collective-permute-done.8, bf16[512,1536]{1,0:T(8,128)(2,1)} %get-tuple-element.82), kind=kOutput, calls=%fused_computation.9 | convolution fusion | flops 4846780416 | bytes 11010048 | tf_op jit(solution)/shard_map/dot_general | solution.py:339
  456.1 6.2 convolution_convert_fusion.4
  462.4 11.0 %convolution_convert_fusion.1 = bf16[1536,2048]{1,0:T(8,128)(2,1)} fusion(bf16[512,2048]{1,0:T(8,128)(2,1)} %collective-permute-done.4, bf16[512,2048]{1,0:T(8,128)(2,1)S(1)} %copy-done.14, bf16[512,1536]{1,0:T(8,128)(2,1)} %collective-permute-done.2, bf16[512,1536]{1,0:T(8,128)(2,1)} %multiply_convert_fusion.1), kind=kOutput, calls=%fused_computation.10 | convolution fusion | flops 6460276736 | bytes 13631488 | tf_op jit(solution)/shard_map/dot_general | solution.py:339
  473.4 10.7 %convolution_convert_fusion.2 = bf16[1536,2048]{1,0:T(8,128)(2,1)} fusion(bf16[512,2048]{1,0:T(8,128)(2,1)S(1)} %collective-permute-done.3, bf16[512,2048]{1,0:T(8,128)(2,1)S(1)} %copy-done.13, bf16[512,1536]{1,0:T(8,128)(2,1)} %collective-permute-done.2, bf16[512,1536]{1,0:T(8,128)(2,1)} %multiply_convert_fusion.1), kind=kOutput, calls=%fused_computation.11 | convolution fusion | flops 6460276736 | bytes 13631488 | tf_op jit(solution)/shard_map/dot_general | solution.py:339
  484.1 8.8 %convolution_convert_fusion.3 = bf16[1536,2048]{1,0:T(8,128)(2,1)} fusion(bf16[512,2048]{1,0:T(8,128)(2,1)S(1)} %collective-permute-done.1, bf16[512,2048]{1,0:T(8,128)(2,1)S(1)} %copy-done.16, bf16[512,1536]{1,0:T(8,128)(2,1)S(1)} %collective-permute-done, bf16[512,1536]{1,0:T(8,128)(2,1)S(1)} %copy-done.8), kind=kOutput, calls=%fused_computation.12 | convolution fusion | flops 6460276736 | bytes 13631488 | tf_op jit(solution)/shard_map/dot_general | solution.py:339
  493.0 281.7 %gradient_scatter.1 = (f32[8,128]{1,0:T(8,128)}, f32[96,2048]{1,0:T(8,128)}, f32[96,2048]{1,0:T(8,128)}, f32[96,2048]{1,0:T(8,128)}, f32[96,768]{1,0:T(8,128)}, /*index=5*/f32[96,1536]{1,0:T(8,128)}) custom-call(bf16[4,2,2,8,128]{4,3,2,1,0:T(8,128)(2,1)} %bitcast.66, bf16[4,2,2,96,2048]{4,3,2,1,0:T(8,128)(2,1)} %bitcast.59, ...), custom_call_target="tpu_custom_call" | custom-call | tf_op jit(solution)/shard_map/gradient_scatter/pallas_call | solution.py:310
  (97 shorter events, 30.7 us)
Async XLA Ops:
  0.6 240.2 %copy-start = (bf16[512,1536]{1,0:T(8,128)(2,1)S(1)}, bf16[512,1536]{1,0:T(8,128)(2,1)}, u32[]{:S(2)}) copy-start(bf16[512,1536]{1,0:T(8,128)(2,1)} %param.15) | copy-start | bytes 4718596
  242.8 202.6 %collective-permute-start.7 = (bf16[512,1536]{1,0:T(8,128)(2,1)}, bf16[512,1536]{1,0:T(8,128)(2,1)}, u32[]{:S(2)}, u32[]{:S(2)}) collective-permute-start(bf16[512,1536]{1,0:T(8,128)(2,1)} %fusion.18), channel_id=1, source_target_pairs={{0,1},{1,0},{2,3},{3,2},{4,5},{5,4},{6,7},{7,6},{8,9},{9,8},{10,11... | collective-permute-start | bytes 4718600 | tf_op jit(solution)/shard_map/ppermute | solution.py:552
  292.6 13.9 %slice-start = ((s8[12582912]{0:T(1024)(128)(4,1)}), s8[4194304]{0:T(1024)(128)(4,1)S(1)}, s32[]{:S(2)}) async-start(s8[12582912]{0:T(1024)(128)(4,1)} %bitcast.71), calls=%async_computation | async-start | bytes 8388608
  294.1 168.2 %collective-permute-start.2 = (bf16[512,1536]{1,0:T(8,128)(2,1)}, bf16[512,1536]{1,0:T(8,128)(2,1)}, u32[]{:S(2)}, u32[]{:S(2)}) collective-permute-start(bf16[512,1536]{1,0:T(8,128)(2,1)} %multiply_convert_fusion.1), channel_id=1, source_target_pairs={{0,1},{1,0},{2,3},{3,2},{4,5},{5,4},{6,7},{7,6},{8,9},{9,8},{10,11... | collective-permute-start | bytes 4718600 | tf_op jit(solution)/shard_map/ppermute | solution.py:552
  294.1 12.4 %copy-start.6 = (bf16[512,1536]{1,0:T(8,128)(2,1)S(1)}, bf16[512,1536]{1,0:T(8,128)(2,1)}, u32[]{:S(2)}) copy-start(bf16[512,1536]{1,0:T(8,128)(2,1)} %param.25) | copy-start | bytes 4718596
  294.1 12.4 %slice-start.1 = ((s8[12582912]{0:T(1024)(128)(4,1)}), s8[4194304]{0:T(1024)(128)(4,1)S(1)}, s32[]{:S(2)}) async-start(s8[12582912]{0:T(1024)(128)(4,1)} %bitcast.71), calls=%async_computation.1 | async-start | bytes 8388608
  294.1 12.4 %slice-start.2 = ((s8[12582912]{0:T(1024)(128)(4,1)}), s8[4194304]{0:T(1024)(128)(4,1)S(1)}, s32[]{:S(2)}) async-start(s8[12582912]{0:T(1024)(128)(4,1)} %bitcast.71), calls=%async_computation.2 | async-start | bytes 8388608
  335.1 12.2 %copy-start.11 = (bf16[512,4096]{1,0:T(8,128)(2,1)S(1)}, bf16[512,4096]{1,0:T(8,128)(2,1)}, u32[]{:S(2)}) copy-start(bf16[512,4096]{1,0:T(8,128)(2,1)} %get-tuple-element.73) | copy-start | bytes 12582916
  360.2 95.7 %collective-permute-start.5 = (bf16[512,1536]{1,0:T(8,128)(2,1)}, bf16[512,1536]{1,0:T(8,128)(2,1)}, u32[]{:S(2)}, u32[]{:S(2)}) collective-permute-start(bf16[512,1536]{1,0:T(8,128)(2,1)} %fusion.51), channel_id=1, source_target_pairs={{0,1},{1,0},{2,3},{3,2},{4,5},{5,4},{6,7},{7,6},{8,9},{9,8},{10,11... | collective-permute-start | bytes 4718600 | tf_op jit(solution)/shard_map/ppermute | solution.py:552
  404.9 40.1 %collective-permute-start.8 = (bf16[512,1536]{1,0:T(8,128)(2,1)}, bf16[512,1536]{1,0:T(8,128)(2,1)}, u32[]{:S(2)}, u32[]{:S(2)}) collective-permute-start(bf16[512,1536]{1,0:T(8,128)(2,1)} %get-tuple-element.83), channel_id=1, source_target_pairs={{0,1},{1,0},{2,3},{3,2},{4,5},{5,4},{6,7},{7,6},{8,9},{9,8},{10,11... | collective-permute-start | bytes 4718600 | tf_op jit(solution)/shard_map/ppermute | solution.py:552
  410.0 52.3 %collective-permute-start.4 = (bf16[512,2048]{1,0:T(8,128)(2,1)}, bf16[512,2048]{1,0:T(8,128)(2,1)}, u32[]{:S(2)}, u32[]{:S(2)}) collective-permute-start(bf16[512,2048]{1,0:T(8,128)(2,1)} %get-tuple-element.77), channel_id=1, source_target_pairs={{0,1},{1,0},{2,3},{3,2},{4,5},{5,4},{6,7},{7,6},{8,9},{9,8},{10,11... | collective-permute-start | bytes 6291464 | tf_op jit(solution)/shard_map/ppermute | solution.py:552
  423.3 12.0 %copy-start.9 = (bf16[512,4096]{1,0:T(8,128)(2,1)S(1)}, bf16[512,4096]{1,0:T(8,128)(2,1)}, u32[]{:S(2)}) copy-start(bf16[512,4096]{1,0:T(8,128)(2,1)} %get-tuple-element.75) | copy-start | bytes 12582916
  423.3 14.5 %copy-start.12 = (f32[512,1536]{1,0:T(8,128)S(1)}, f32[512,1536]{1,0:T(8,128)}, u32[]{:S(2)}) copy-start(f32[512,1536]{1,0:T(8,128)} %get-tuple-element.96) | copy-start | bytes 9437188
  445.0 10.6 %collective-permute-start.6 = (bf16[512,768]{1,0:T(8,128)(2,1)S(1)}, bf16[512,768]{1,0:T(8,128)(2,1)S(1)}, u32[]{:S(2)}, u32[]{:S(2)}) collective-permute-start(bf16[512,768]{1,0:T(8,128)(2,1)S(1)} %get-tuple-element.85), channel_id=1, source_target_pairs={{0,1},{1,0},{2,3},{3,2},{4,5},{5,4},{6,7},{7,6},{8,9},{9,8},{10,11... | collective-permute-start | bytes 2359304 | tf_op jit(solution)/shard_map/ppermute | solution.py:552
  445.3 28.1 %collective-permute-start.3 = (bf16[512,2048]{1,0:T(8,128)(2,1)S(1)}, bf16[512,2048]{1,0:T(8,128)(2,1)S(1)}, u32[]{:S(2)}, u32[]{:S(2)}) collective-permute-start(bf16[512,2048]{1,0:T(8,128)(2,1)S(1)} %copy-done.15), channel_id=1, source_target_pairs={{0,1},{1,0},{2,3},{3,2},{4,5},{5,4},{6,7},{7,6},{8,9},{9,8},{10,11... | collective-permute-start | bytes 6291464 | tf_op jit(solution)/shard_map/ppermute | solution.py:552
  445.6 10.0 %copy-start.8 = (bf16[512,1536]{1,0:T(8,128)(2,1)S(1)}, bf16[512,1536]{1,0:T(8,128)(2,1)}, u32[]{:S(2)}) copy-start(bf16[512,1536]{1,0:T(8,128)(2,1)} %param.25) | copy-start | bytes 4718596
  445.6 10.4 %copy-start.17 = (bf16[512,2048]{1,0:T(8,128)(2,1)S(1)}, bf16[512,2048]{1,0:T(8,128)(2,1)}, u32[]{:S(2)}) copy-start(bf16[512,2048]{1,0:T(8,128)(2,1)} %get-tuple-element.81) | copy-start | bytes 6291460
  455.5 28.6 %collective-permute-start = (bf16[512,1536]{1,0:T(8,128)(2,1)S(1)}, bf16[512,1536]{1,0:T(8,128)(2,1)S(1)}, u32[]{:S(2)}, u32[]{:S(2)}) collective-permute-start(bf16[512,1536]{1,0:T(8,128)(2,1)S(1)} %copy-done.8), channel_id=1, source_target_pairs={{0,1},{1,0},{2,3},{3,2},{4,5},{5,4},{6,7},{7,6},{8,9},{9,8},{10,11... | collective-permute-start | bytes 4718600 | tf_op jit(solution)/shard_map/ppermute | solution.py:552
  455.9 28.2 %collective-permute-start.1 = (bf16[512,2048]{1,0:T(8,128)(2,1)S(1)}, bf16[512,2048]{1,0:T(8,128)(2,1)S(1)}, u32[]{:S(2)}, u32[]{:S(2)}) collective-permute-start(bf16[512,2048]{1,0:T(8,128)(2,1)S(1)} %copy-done.17), channel_id=1, source_target_pairs={{0,1},{1,0},{2,3},{3,2},{4,5},{5,4},{6,7},{7,6},{8,9},{9,8},{10,11... | collective-permute-start | bytes 6291464 | tf_op jit(solution)/shard_map/ppermute | solution.py:552
  456.1 6.2 copy-start.14
  462.3 11.1 %copy-start.13 = (bf16[512,2048]{1,0:T(8,128)(2,1)S(1)}, bf16[512,2048]{1,0:T(8,128)(2,1)}, u32[]{:S(2)}) copy-start(bf16[512,2048]{1,0:T(8,128)(2,1)} %get-tuple-element.78) | copy-start | bytes 6291460
  473.4 10.7 %copy-start.16 = (bf16[512,2048]{1,0:T(8,128)(2,1)S(1)}, bf16[512,2048]{1,0:T(8,128)(2,1)}, u32[]{:S(2)}) copy-start(bf16[512,2048]{1,0:T(8,128)(2,1)} %get-tuple-element.80) | copy-start | bytes 6291460
  774.7 8.6 %copy-start.19 = (f32[96,2048]{1,0:T(8,128)S(1)}, f32[96,2048]{1,0:T(8,128)}, u32[]{:S(2)}) copy-start(f32[96,2048]{1,0:T(8,128)} %get-tuple-element.117) | copy-start | bytes 2359300
  774.7 9.4 %copy-start.18 = (f32[96,2048]{1,0:T(8,128)S(1)}, f32[96,2048]{1,0:T(8,128)}, u32[]{:S(2)}) copy-start(f32[96,2048]{1,0:T(8,128)} %get-tuple-element.65) | copy-start | bytes 2359300
  (9 other events, 27.8 us)

commit v2 on v1

--- a/solution.py
+++ b/solution.py
@@ -22,121 +22,136 @@
     d = lax.axis_index("dp")
     return lax.div(d, 4), lax.rem(lax.div(d, 2), 2), lax.rem(d, 2), lax.axis_index("tensor")
 
+
 def dev(z, y, x, c):
     return (z * 4 + y * 2 + x, c)
+
 
 def enter(line, pos):
     z, y, x, c = pos
     barrier = pltpu.get_barrier_semaphore()
+
     def greet(who):
         pl.semaphore_signal(barrier, inc=1, device_id=who, device_id_type=MESH)
-    greet(dev(z, y, x, 1 - c)); greet(dev(z, y, 1 - x, c)); greet(dev(z, 1 - y, x, c))
+
+    greet(dev(z, y, x, 1 - c))
+    greet(dev(z, y, 1 - x, c))
+    greet(dev(z, 1 - y, x, c))
+
     @pl.when(z > 0)
-    def _(): greet(dev(z - 1, y, x, c))
+    def _():
+        greet(dev(z - 1, y, x, c))
+
     @pl.when(z < line - 1)
-    def _(): greet(dev(z + 1, y, x, c))
+    def _():
+        greet(dev(z + 1, y, x, c))
+
     pl.semaphore_wait(barrier, 3 + (z > 0).astype(jnp.int32) + (z < line - 1).astype(jnp.int32))
 
+
+def remote(src, dst, send, recv, who):
+    return pltpu.make_async_remote_copy(src_ref=src, dst_ref=dst, send_sem=send, recv_sem=recv, device_id=who, device_id_type=MESH)
+
+
 class Gather:
-    def __init__(self, line, pos, shards, fulls, chunks, send, recv, local):
-        self.line, self.pos, self.shards, self.fulls, self.chunks = line, pos, shards, fulls, chunks
-        self.send, self.recv, self.local = send, recv, local
-        self.steps = line + 3
-    def region(self, t, have, z=None):
-        w, off, width, _ = self.chunks[t]
+    def __init__(self, line, pos, shard, full, width, orders, paired, send, recv):
+        self.line, self.pos, self.shard, self.full, self.width = line, pos, shard, full, width
+        self.orders, self.paired, self.send, self.recv = orders, paired, send, recv
+        self.count = shard.shape[-1] // width
+        self.depth = line + 1 + paired
+
+    def columns(self, t, sub):
+        part = self.width // len(self.orders[0])
+        return t * self.width + sub * part, part
+
+    def region(self, t, sub, have, z=None):
+        first, part = self.columns(t, sub)
         pz, py, px, c = self.pos
-        full = self.fulls[w]
-        half = full.shape[-1] // 2
-        cols = pl.ds(pl.multiple_of(c * half + off, 128), width)
+        if self.paired:
+            first = first + c * self.shard.shape[-1]
         every = slice(None)
         zi = z if z is not None else (every if "z" in have else pz)
-        return full.at[zi, every if "y" in have else py, every if "x" in have else px, :, cols]
-    def own(self, t):
-        w, off, width, _ = self.chunks[t]
-        return self.shards[w].at[:, pl.ds(off, width)]
-    def local_copy(self, t):
-        return pltpu.make_async_copy(self.own(t), self.region(t, ""), self.local.at[t])
-    def copy(self, t, slot, src, dst, who):
-        return pltpu.make_async_remote_copy(src_ref=src, dst_ref=dst, send_sem=self.send.at[t, slot], recv_sem=self.recv.at[t, slot], device_id=who, device_id_type=MESH)
-    def swap(self, t, axis, have):
-        z, y, x, c = self.pos
-        who = {"y": dev(z, 1 - y, x, c), "x": dev(z, y, 1 - x, c), "c": dev(z, y, x, 1 - c)}[axis]
-        slot = 2 * (self.line - 1) + "yxc".index(axis)
-        mine = self.region(t, have) if have else self.own(t)
-        land = self.region(t, have)
-        if axis == "y":
-            w, off, width, _ = self.chunks[t]
-        return self.copy(t, slot, mine, land, who)
-    def hop(self, t, h, up, have, act):
+        cols = pl.ds(pl.multiple_of(first, 128), part)
+        return self.full.at[zi, every if "y" in have else py, every if "x" in have else px, :, cols]
+
+    def own(self, t, sub):
+        first, part = self.columns(t, sub)
+        return self.shard.at[:, pl.ds(pl.multiple_of(first, 128), part)]
+
+    def copy(self, t, sub, slot, src, dst, who):
+        return remote(src, dst, self.send.at[t, sub, slot], self.recv.at[t, sub, slot], who)
+
+    def hop(self, t, sub, h, up, have, what):
         z, y, x, c = self.pos
         slot = (h - 1) * 2 + up
         if up:
-            block, who, there, here = z - (h - 1), dev(z + 1, y, x, c), (z + 1 < self.line) & (z >= h - 1), z >= h
-            incoming = z - h
+            block, incoming, who = z - (h - 1), z - h, dev(z + 1, y, x, c)
+            there, here = (z + 1 < self.line) & (z >= h - 1), z >= h
         else:
-            block, who, there, here = z + (h - 1), dev(z - 1, y, x, c), (z > 0) & (z + h - 1 < self.line), z + h < self.line
-            incoming = z + h
-        if act == "recv":
-            @pl.when(here)
+            block, incoming, who = z + (h - 1), z + h, dev(z - 1, y, x, c)
+            there, here = (z > 0) & (z + h - 1 < self.line), z + h < self.line
+
+        @pl.when(here if what == "recv" else there)
+        def _():
+            if what == "recv":
+                r = self.region(t, sub, have, incoming)
+                self.copy(t, sub, slot, r, r, dev(z, y, x, 1 - c)).wait_recv()
+                return
+            r = self.region(t, sub, have, block)
+            cp = self.copy(t, sub, slot, self.own(t, sub) if h == 1 and not have else r, r, who)
+            cp.start() if what == "start" else cp.wait_send()
+
+    def act(self, t, sub, order, i, what):
+        z, y, x, c = self.pos
+        moves, have = [], ""
+        for axis in order:
+            moves += [(axis, h, have) for h in (range(1, self.line) if axis == "z" else (0,))]
+            have += axis
+        if self.paired:
+            moves.append(("c", 0, have))
+        axis, h, have = moves[i]
+        if axis == "z":
+            for up in (1, 0):
+                self.hop(t, sub, h, up, have, what)
+            return
+        who = {"y": dev(z, 1 - y, x, c), "x": dev(z, y, 1 - x, c), "c": dev(z, y, x, 1 - c)}[axis]
+        land = self.region(t, sub, have)
+        cp = self.copy(t, sub, 2 * (self.line - 1) + "yxc".index(axis), land if have else self.own(t, sub), land, who)
+        {"start": cp.start, "recv": cp.wait_recv, "sent": cp.wait_send}[what]()
+
+    def each(self, t, fn):
+        there = (t >= 0) & (t < self.count)
+        for v, orders in enumerate(self.orders):
+            turn_of = there if len(self.orders) == 1 else there & ((lax.rem(t + 4, 4) == 0) == (v == 1))
+
+            @pl.when(turn_of)
             def _():
-                r = self.region(t, have, incoming)
-                self.copy(t, slot, r, r, dev(z, y, x, 1 - c)).wait_recv()
-        else:
-            @pl.when(there)
-            def _():
-                r = self.region(t, have, block)
-                src = self.own(t) if (h == 1 and not have) else r
-                cp = self.copy(t, slot, src, r, who)
-                if act == "start": cp.start()
-                else: cp.wait_send()
-    def plan(self, t):
-        order, out, have = self.chunks[t][3], [], ""
-        acts = []
-        for axis in order:
-            if axis == "z":
-                for h in range(1, self.line): acts.append(("z", h, have))
-            else: acts.append((axis, 0, have))
-            have += axis
-        acts.append(("c", 0, have))
-        return acts
-    def act(self, t, a, what):
-        axis, h, have = a
-        if axis == "z":
-            for up in (1, 0): self.hop(t, h, up, have, what)
-        else:
-            cp = self.swap(t, axis, have)
-            {"start": cp.start, "recv": cp.wait_recv, "sent": cp.wait_send}[what]()
+                for sub, order in enumerate(orders):
+                    fn(sub, order)
+
     def step(self, t, s):
-        acts = self.plan(t)
-        if s > 0: self.act(t, acts[s - 1], "recv")
-        if s == 1: self.local_copy(t).wait()
-        if s < len(acts): self.act(t, acts[s], "start")
-    def finish(self, t):
-        for a in self.plan(t): self.act(t, a, "sent")
-
-def gather_body(line, chunks, n, *refs):
-    shards, fulls, (send, recv, local) = refs[:n], refs[n:2 * n], refs[2 * n:]
-    pos = place()
-    g = Gather(line, pos, shards, fulls, chunks, send, recv, local)
-    for t in range(len(chunks)): g.local_copy(t).start()
-    enter(line, pos)
-    for p in range(len(chunks) + g.steps - 1):
-        for s in range(g.steps):
-            if 0 <= p - s < len(chunks): g.step(p - s, s)
-    for t in range(len(chunks)): g.finish(t)
-
-def gather(line, chunks, shards, cid):
-    n = len(shards)
-    slots = 2 * (line - 1) + 3
-    return pl.pallas_call(
-        functools.partial(gather_body, line, chunks, n),
-        out_shape=[jax.ShapeDtypeStruct((line, 2, 2, s.shape[0], 2 * s.shape[1]), s.dtype) for s in shards],
-        in_specs=[pl.BlockSpec(memory_space=pltpu.VMEM)] * n,
-        out_specs=[pl.BlockSpec(memory_space=pl.ANY)] * n,
-        scratch_shapes=[pltpu.SemaphoreType.DMA((len(chunks), slots)), pltpu.SemaphoreType.DMA((len(chunks), slots)), pltpu.SemaphoreType.DMA((len(chunks),))],
-        compiler_params=pltpu.CompilerParams(collective_id=cid, has_side_effects=True),
-        name="weight_gather",
-    )(*shards)
+        def go(sub, order):
+            if s > 0:
+                self.act(t, sub, order, s - 1, "recv")
+            if s < self.depth:
+                self.act(t, sub, order, s, "start")
+
+        self.each(t, go)
+
+    def advance(self, p):
+        for s in range(self.depth + 1):
+            self.step(p - s, s)
+
+    def finish(self):
+        @pl.loop(0, self.count)
+        def _(t):
+            self.each(t, lambda sub, order: [self.act(t, sub, order, i, "sent") for i in range(self.depth)])
+
+
+def own_copy(g, sem):
+    z, y, x, c = g.pos
+    first = c * g.shard.shape[-1] if g.paired else 0
+    return pltpu.make_async_copy(g.shard, g.full.at[z, y, x, :, pl.ds(pl.multiple_of(first, 128), g.shard.shape[-1])], sem)
 
 
 class Scatter:
@@ -483,6 +498,373 @@
     )(q, k, v, mixed, grad_mixed, cosine, sine)
 
 
+ROWS = 128
+
+
+def each_rows(tokens, step, fn):
+    @pl.loop(0, tokens // step)
+    def _(r):
+        fn(pl.ds(pl.multiple_of(r * step, step), step))
+
+
+def forward_kernel(line, width, block, *refs):
+    refs = list(refs)
+    take = lambda n: [refs.pop(0) for _ in range(n)]
+    shard, gains, hid, ct, cosine, sine = take(6)
+    full, gains_full, q_out, k_out, v_out, mixed_out, n1_pair, n2_pair, ct_pair, mixed_pair, gm_pair = take(11)
+    tile_pairs = take(3)
+    hidden_out, grad_middle, grad_mixed, gain_sum = take(4)
+    wbuf, gain_buf, gain, n1, n2, flat, qh, kh, vh, mh, mixed, middle, acc, grad_n2, act, tiles = take(16)
+    send, recv, gsend, grecv, own_sem, load_sem, gain_sem, local_sem, pair_send, pair_recv, tile_local, tile_send, tile_recv = take(13)
+
+    pos = place()
+    z, y, x, c = pos
+    tokens, d_model = hid.shape
+    half = shard.shape[-1]
+    heads, groups = qh.shape[0] // 2, kh.shape[0] // 2
+    sibling = dev(z, y, x, 1 - c)
+    bf16, f32 = jnp.bfloat16, jnp.float32
+
+    g = Gather(line, pos, shard, full, width, (("zyx", "zxy"), ("xyz", "yxz")), 1, send, recv)
+    gg = Gather(line, pos, gains, gains_full, gains.shape[-1], (("zyx",),), 0, gsend, grecv)
+    g_own, gg_own = own_copy(g, own_sem.at[0]), own_copy(gg, own_sem.at[1])
+    g_own.start()
+    gg_own.start()
+    enter(line, pos)
+
+    def load(t, hh, slot):
+        cols = pl.ds(pl.multiple_of(hh * half + t * width, 128), width)
+        return pltpu.make_async_copy(full.at[:, :, :, :, cols], wbuf.at[slot, hh], load_sem.at[slot, hh])
+
+    def weight(slot, hh):
+        return wbuf[slot, hh].reshape(d_model, width)
+
+    def share(i, own_src, own_dst, other_src, other_dst):
+        return pltpu.make_async_copy(own_src, own_dst, local_sem.at[i]), remote(other_src, other_dst, pair_send.at[i], pair_recv.at[i], sibling)
+
+    shares = [share(i, src, pair.at[0], src, pair.at[1]) for i, (src, pair) in enumerate(((ct, ct_pair), (n1, n1_pair), (n2, n2_pair), (n1, gm_pair)))]
+    hw = mixed.shape[1] // 2
+    side = lambda ref, s, w: ref.at[:, pl.ds(pl.multiple_of(s * w, 128), w)]
+    shares.append(share(4, side(mixed, c, hw), mixed_pair.at[0], side(mixed, 1 - c, hw), mixed_pair.at[1]))
+    keeps = [pltpu.make_async_copy(src, dst, local_sem.at[5 + i]) for i, (src, dst) in enumerate(((qh, q_out), (kh, k_out), (vh, v_out), (mixed, mixed_out)))]
+
+    def begin(i):
+        for cp in shares[i]:
+            cp.start()
+
+    def end(i):
+        for cp in shares[i]:
+            cp.wait()
+
+    def tile_copies(j, hh):
+        slot = lax.rem(j, 2)
+        cols = pl.ds(pl.multiple_of(j * block, 128), block)
+        own = [pltpu.make_async_copy(tiles.at[slot, hh, i], pair.at[0, :, cols], tile_local.at[j, i]) for i, pair in enumerate(tile_pairs)]
+        out = [remote(tiles.at[slot, hh, i], pair.at[1, :, cols], tile_send.at[j, i], tile_recv.at[j, i], sibling) for i, pair in enumerate(tile_pairs)]
+        return own, out
+
+    def drain_tiles(j):
+        for cp in tile_copies(j, 0)[0]:
+            cp.wait()
+        for cp in tile_copies(j, 0)[1]:
+            cp.wait_send()
+
+    def normalize():
+        loaded = pltpu.make_async_copy(gains_full, gain_buf, gain_sem)
+        loaded.start()
+        loaded.wait()
+        n = d_model // (gain_buf.shape[0] * 4)
+        table = gain_buf[...].astype(f32)
+        for i in range(2):
+            gain[i : i + 1, :] = jnp.concatenate([table[a, b, e, i : i + 1, :n] for a in range(gain_buf.shape[0]) for b in range(2) for e in range(2)], axis=1)
+
+        def rows_of_norm(rows):
+            v = hid[rows, :].astype(f32)
+            v = v * lax.rsqrt(jnp.mean(v * v, axis=1, keepdims=True) + EPSILON)
+            n1[rows, :] = (v * gain[0:1, :]).astype(bf16)
+
+        each_rows(tokens, ROWS, rows_of_norm)
+        begin(1)
+
+    def project(slot, outs):
+        @pl.loop(0, 2)
+        def _(hh):
+            flat[...] = dot_nn(n1[...], weight(slot, hh))
+
+            def to_heads(rows):
+                cos, sin = cosine[rows, :], sine[rows, :]
+                first = 0
+                for n, target, turned in outs:
+                    for h in range(n):
+                        v = flat[rows, (first + h) * HEAD_SIZE : (first + h + 1) * HEAD_SIZE]
+                        target[hh * n + h, rows] = (turn(v, cos, sin) if turned else v).astype(bf16)
+                    first += n
+
+            each_rows(tokens, ROWS, to_heads)
+
+    def attend_half(hh):
+        per = heads // groups
+        blocks = tokens // BLOCK
+
+        @pl.loop(0, groups)
+        def _(i):
+            kv = hh * groups + i
+            for b in range(blocks):
+                rows, n = pl.ds(b * BLOCK, BLOCK), (b + 1) * BLOCK
+                w = causal_weights(rows_of(qh, kv * per, per, rows), kh[kv, :n], b, per).astype(bf16)
+                m = dot_nn(w, vh[kv, :n]).astype(bf16)
+                for e in range(per):
+                    mh[kv * per + e, rows] = m[e * BLOCK : (e + 1) * BLOCK]
+
+    def leave_attention(slot):
+        def join(rows):
+            mixed[rows, :] = jnp.concatenate([mh[h, rows] for h in range(2 * heads)], axis=1)
+
+        each_rows(tokens, ROWS, join)
+        begin(4)
+        for cp in keeps:
+            cp.start()
+        middle[...] = hid[...].astype(f32) + dot_nt(mixed[:, :hw], weight(slot, 0))
+        middle[...] += dot_nt(mixed[:, hw:], weight(slot, 1))
+
+        def rows_of_norm(rows):
+            v = middle[rows, :]
+            acc[rows, :] = v
+            v = v * lax.rsqrt(jnp.mean(v * v, axis=1, keepdims=True) + EPSILON)
+            n2[rows, :] = (v * gain[1:2, :]).astype(bf16)
+            grad_n2[rows, :] = jnp.zeros_like(v)
+
+        each_rows(tokens, ROWS, rows_of_norm)
+        begin(2)
+
+    def feed_forward(j, slot):
+        @pl.when(j >= 2)
+        def _():
+            drain_tiles(j - 2)
+
+        part = lax.rem(j, 2)
+
+        @pl.loop(0, 2)
+        def _(hh):
+            act[0] = dot_nn(n2[...], weight(slot, hh)[:, :block])
+            act[1] = dot_nn(n2[...], weight(slot, hh)[:, block : 2 * block])
+            act[2] = dot_nn(ct[...], weight(slot, hh)[:, 2 * block :])
+
+            def gated(rows):
+                gate, up, grad = act[0, rows], act[1, rows], act[2, rows]
+                sigma = jax.nn.sigmoid(gate)
+                tiles[part, hh, 0, rows] = (gate * sigma * up).astype(bf16)
+                tiles[part, hh, 1, rows] = (grad * up * sigma * (1.0 + gate * (1.0 - sigma))).astype(bf16)
+                tiles[part, hh, 2, rows] = (grad * gate * sigma).astype(bf16)
+
+            each_rows(tokens, ROWS // 2, gated)
+            own, out = tile_copies(j, hh)
+
+            @pl.when(hh == c)
+            def _():
+                for cp in own:
+                    cp.start()
+
+            @pl.when(hh != c)
+            def _():
+                for cp in out:
+                    cp.start()
+
+            acc[...] += dot_nt(tiles[part, hh, 0], weight(slot, hh)[:, 2 * block :])
+            both = jnp.concatenate([tiles[part, hh, 1], tiles[part, hh, 2]], axis=1)
+            grad_n2[...] += dot_nt(both, weight(slot, hh)[:, : 2 * block])
+
+    count, lead = g.count, g.depth + 1
+
+    @pl.loop(0, count + lead)
+    def _(p):
+        @pl.when(p == 0)
+        def _():
+            g_own.wait()
+            gg_own.wait()
+            begin(0)
+
+        gg.advance(p)
+        g.advance(p)
+        u = p - lead
+
+        @pl.when((u >= -1) & (u + 1 < count))
+        def _():
+            for hh in range(2):
+                load(u + 1, hh, lax.rem(u + 1, 2)).start()
+
+        @pl.when(u >= 0)
+        def _():
+            slot = lax.rem(u, 2)
+            for hh in range(2):
+                load(u, hh, slot).wait()
+
+            @pl.when(u == 0)
+            def _():
+                normalize()
+                project(slot, ((heads, qh, True),))
+
+            @pl.when(u == 1)
+            def _():
+                project(slot, ((groups, kh, True), (groups, vh, False)))
+                attend_half(0)
+
+            @pl.when(u == 2)
+            def _():
+                attend_half(1)
+                leave_attention(slot)
+
+            @pl.when(u >= 3)
+            def _():
+                feed_forward(u - 3, slot)
+
+    for hh in range(2):
+        load(2, hh, 0).start()
+    end(1)
+    gain_sum[...] = jnp.zeros_like(gain_sum)
+
+    def rows_back(rows):
+        v = middle[rows, :]
+        inverse = lax.rsqrt(jnp.mean(v * v, axis=1, keepdims=True) + EPSILON)
+        unit, grad = v * inverse, grad_n2[rows, :]
+        scaled = grad * gain[1:2, :]
+        inner = jnp.mean(scaled * unit, axis=1, keepdims=True)
+        total = ct[rows, :].astype(f32) + inverse * (scaled - unit * inner)
+        grad_middle[rows, :] = total
+        n1[rows, :] = total.astype(bf16)
+        gain_sum[...] += jnp.sum(grad * unit, axis=0, keepdims=True)
+        hidden_out[rows, :] = acc[rows, :].astype(bf16)
+
+    each_rows(tokens, ROWS, rows_back)
+    begin(3)
+    for hh in range(2):
+        load(2, hh, 0).wait()
+        grad_mixed[:, hh * hw : (hh + 1) * hw] = dot_nn(n1[...], weight(0, hh))
+
+    steps = count - 3
+    for i in (0, 2, 3, 4):
+        end(i)
+    for cp in keeps:
+        cp.wait()
+    for j in range(max(steps - 2, 0), steps):
+        drain_tiles(j)
+
+    @pl.loop(0, steps)
+    def _(j):
+        for cp in tile_copies(j, 0)[1]:
+            cp.wait_recv()
+
+    g.finish()
+    gg.finish()
+
+
+def forward(line, shard, gains, hidden_in, cotangent, cosine, sine, block):
+    tokens, d_model = hidden_in.shape
+    rows, half = shard.shape
+    width = 3 * block
+    count = half // width
+    steps = count - 3
+    heads, groups = QUERY_HEADS // 2, KEY_VALUE_HEADS // 2
+    bf16, f32 = jnp.bfloat16, jnp.float32
+    struct = jax.ShapeDtypeStruct
+    hbm, vmem = pl.BlockSpec(memory_space=pl.ANY), pl.BlockSpec(memory_space=pltpu.VMEM)
+    dma = pltpu.SemaphoreType.DMA
+    pair = struct((2, tokens, d_model), bf16)
+    tile_pair = struct((2, tokens, steps * block), bf16)
+    head_shape = lambda n: (n, tokens, HEAD_SIZE)
+    slots = 2 * (line - 1) + 3
+    outs = [
+        struct((line, 2, 2, rows, 2 * half), bf16),
+        struct((line, 2, 2) + gains.shape, bf16),
+        struct(head_shape(2 * heads), bf16),
+        struct(head_shape(2 * groups), bf16),
+        struct(head_shape(2 * groups), bf16),
+        struct((tokens, 2 * heads * HEAD_SIZE), bf16),
+        pair,
+        pair,
+        pair,
+        struct((2, tokens, heads * HEAD_SIZE), bf16),
+        pair,
+        tile_pair,
+        tile_pair,
+        tile_pair,
+        struct((tokens, d_model), bf16),
+        struct((tokens, d_model), f32),
+        struct((tokens, 2 * heads * HEAD_SIZE), f32),
+        struct((1, d_model), f32),
+    ]
+    V = pltpu.VMEM
+    return pl.pallas_call(
+        functools.partial(forward_kernel, line, width, block),
+        out_shape=outs,
+        in_specs=[vmem] * 6,
+        out_specs=[hbm] * 14 + [vmem] * 4,
+        scratch_shapes=[
+            V((2, 2, line, 2, 2, rows, width), bf16),
+            V((line, 2, 2) + gains.shape, bf16),
+            V((8, d_model), f32),
+            V((tokens, d_model), bf16),
+            V((tokens, d_model), bf16),
+            V((tokens, width), f32),
+            V(head_shape(2 * heads), bf16),
+            V(head_shape(2 * groups), bf16),
+            V(head_shape(2 * groups), bf16),
+            V(head_shape(2 * heads), bf16),
+            V((tokens, 2 * heads * HEAD_SIZE), bf16),
+            V((tokens, d_model), f32),
+            V((tokens, d_model), f32),
+            V((tokens, d_model), f32),
+            V((3, tokens, block), f32),
+            V((2, 2, 3, tokens, block), bf16),
+            dma((count, 2, slots)),
+            dma((count, 2, slots)),
+            dma((1, 1, slots)),
+            dma((1, 1, slots)),
+            dma((2,)),
+            dma((2, 2)),
+            dma,
+            dma((9,)),
+            dma((5,)),
+            dma((5,)),
+            dma((steps, 3)),
+            dma((steps, 3)),
+            dma((steps, 3)),
+        ],
+        compiler_params=pltpu.CompilerParams(collective_id=0, has_side_effects=True, vmem_limit_bytes=64 * 2**20 - 2**17),
+        name="gather_forward",
+    )(shard, gains, hidden_in, cotangent, cosine, sine)
+
+
+def against_kernel(grad, weight, out):
+    part = dot_nt(grad[...], weight[...].reshape(out.shape[1], grad.shape[1]))
+
+    @pl.when(pl.program_id(0) == 0)
+    def _():
+        out[...] = part
+
+    @pl.when(pl.program_id(0) > 0)
+    def _():
+        out[...] += part
+
+
+def against_columns(grad, full, width):
+    tokens, columns = grad.shape
+    line, rows = full.shape[0], full.shape[3]
+    each, half = columns // 2 // width, full.shape[4] // 2 // width
+    return pl.pallas_call(
+        against_kernel,
+        grid=(2 * each,),
+        out_shape=jax.ShapeDtypeStruct((tokens, line * 4 * rows), jnp.float32),
+        in_specs=[
+            pl.BlockSpec((tokens, width), lambda i: (0, i)),
+            pl.BlockSpec((line, 2, 2, rows, width), lambda i: (0, 0, 0, 0, (i // each) * half + i % each)),
+        ],
+        out_specs=pl.BlockSpec((tokens, line * 4 * rows), lambda i: (0, 0)),
+        compiler_params=pltpu.CompilerParams(vmem_limit_bytes=40 * 2**20),
+        name="against_columns",
+    )(grad, full)
+
+
 def norm_back(grad_normed, unit_rows, inverse_rms, gain):
     scaled = grad_normed * gain
     inner = jnp.mean(scaled * unit_rows, axis=1, keepdims=True)
@@ -513,38 +895,22 @@
     side = lax.axis_index("tensor")
 
     gains = jnp.zeros((8, 128), bf16).at[0, :rows].set(attention_gain).at[1, :rows].set(feedforward_gain)
-    shards = [gains, jnp.concatenate([query_weight, key_matrix, value_matrix], axis=1), out_weight.T, gate_weight, up_weight, down_weight.T]
-    fulls = gather(line, cut([s.shape[1] for s in shards], 512, GATHER_MIX), shards, 0)
-    all_gains = fulls[0].reshape(n_dp, 8, -1)
-    gain_first = all_gains[:, 0, :rows].reshape(1, width).astype(f32)
-    gain_second = all_gains[:, 1, :rows].reshape(1, width).astype(f32)
-    w_qkv, w_out, w_gate, w_up, w_down = (f.reshape(width, f.shape[-1]) for f in fulls[1:])
-
+    block = (query_weight.shape[1] // 3) & -128
+    out_t, down_t = out_weight.T, down_weight.T
+    pieces = [query_weight, key_matrix, value_matrix, out_t]
+    for j in range(0, gate_weight.shape[1], block):
+        pieces += [w[:, j : j + block] for w in (gate_weight, up_weight, down_t)]
     cosine, sine = rope_tables(SEQUENCE_LENGTH, HEAD_SIZE)
+    (full, gains_full, q, k, v, mixed, n1, n2, ct, mixed_pair, gm, hidden, grad_gate_act, grad_up_act, hidden_out, grad_middle, grad_mixed, second_gain) = forward(
+        line, jnp.concatenate(pieces, axis=1), gains, hidden_in, cotangent, cosine, sine, block
+    )
+    nq, nk = query_weight.shape[1], key_matrix.shape[1]
+    gain_first = gains_full.reshape(n_dp, 8, 128)[:, 0, :rows].reshape(1, width).astype(f32)
     x = hidden_in.astype(f32)
     inverse_one = lax.rsqrt(jnp.mean(x * x, axis=1, keepdims=True) + EPSILON)
     unit_one = x * inverse_one
-    normed_one = (unit_one * gain_first).astype(bf16)
-    q, k, v, mixed = attend(dot_nn(normed_one, w_qkv), cosine, sine, n_tensor)
-    middle = x + dot_nt(mixed, w_out)
-    inverse_two = lax.rsqrt(jnp.mean(middle * middle, axis=1, keepdims=True) + EPSILON)
-    unit_two = middle * inverse_two
-    normed_two = (unit_two * gain_second).astype(bf16)
-    gate = dot_nn(normed_two, w_gate)
-    up = dot_nn(normed_two, w_up)
-    sigma = jax.nn.sigmoid(gate)
-    hidden = (gate * sigma * up).astype(bf16)
-    hidden_out = (middle + dot_nt(hidden, w_down)).astype(bf16)
-    grad_hidden = dot_nn(cotangent, w_down)
-    grad_up_act = (grad_hidden * gate * sigma).astype(bf16)
-    grad_gate_act = (grad_hidden * up * sigma * (1.0 + gate * (1.0 - sigma))).astype(bf16)
-    grad_normed_two = dot_nt(grad_gate_act, w_gate) + dot_nt(grad_up_act, w_up)
-    middle_part, second_part = norm_back(grad_normed_two, unit_two, inverse_two, gain_second)
-    grad_middle = cotangent.astype(f32) + middle_part
-    grad_middle_round = grad_middle.astype(bf16)
-    grad_mixed = dot_nn(grad_middle_round, w_out)
     grad_qkv_act = attend_back(q, k, v, mixed, grad_mixed, cosine, sine, n_tensor)
-    grad_normed_one = dot_nt(grad_qkv_act, w_qkv)
+    grad_normed_one = against_columns(grad_qkv_act, full, 3 * block)
     first_part, first_gain = norm_back(grad_normed_one, unit_one, inverse_one, gain_first)
     grad_in = grad_middle + first_part
 
@@ -555,22 +921,20 @@
         size = a.shape[1] // n_tensor
         return lax.dynamic_slice_in_dim(a, which * size, size, axis=1)
 
-    both = lambda a: jnp.concatenate([a, other(a)], axis=0)
-    both_half = lambda a: jnp.concatenate([of_half(a, side), other(of_half(a, 1 - side))], axis=0)
-    n1, n2, ct, gm = both(normed_one), both(normed_two), both(cotangent), both(grad_middle_round)
-    weight_grad = lambda a, b: dot_tn(a, both_half(b)).astype(bf16)
+    stack = lambda a: a.reshape(-1, a.shape[-1])
+    qkv_pair = jnp.concatenate([of_half(grad_qkv_act, side), other(of_half(grad_qkv_act, 1 - side))], axis=0)
+    weight_grad = lambda a, b: dot_tn(stack(a), b).astype(bf16)
     grads = [
-        weight_grad(ct, hidden),
-        weight_grad(n2, grad_gate_act),
-        weight_grad(n2, grad_up_act),
-        weight_grad(gm, mixed),
-        weight_grad(n1, grad_qkv_act),
+        weight_grad(ct, stack(hidden)),
+        weight_grad(n2, stack(grad_gate_act)),
+        weight_grad(n2, stack(grad_up_act)),
+        weight_grad(gm, stack(mixed_pair)),
+        weight_grad(n1, qkv_pair),
     ]
-    parts = jnp.stack([first_gain, second_part]).reshape(2, n_dp, rows).transpose(1, 0, 2)
+    parts = jnp.stack([first_gain, second_gain[0]]).reshape(2, n_dp, rows).transpose(1, 0, 2)
     parts = jnp.pad(parts, ((0, 0), (0, 6), (0, 128 - rows))).astype(bf16)
     grads = [parts.reshape(line, 2, 2, 8, 128)] + [g.reshape(line, 2, 2, rows, g.shape[1]) for g in grads]
     g_gains, g_down, g_gate, g_up, g_out, g_qkv = scatter(line, cut([g.shape[-1] for g in grads], 512, SCATTER_MIX), grads, 1)
-    nq, nk = query_weight.shape[1], key_matrix.shape[1]
     return (
         hidden_out,
         grad_in,

time: 789 us -> 689 us (0.87)
  matrix products: 155 us -> 41.7 us
  local copies, waits for them, and re-layouts: 31.5 us -> 40.7 us
  Pallas kernels: 582 us -> 590 us
    dot_general x10 -> x0, matrix products: 108 us -> none  [the longest x5 58.3 us: dot_nn(): return jnp.dot(a, b, preferred_element_type=jnp.float32)]
    unnamed x53 -> x81, local copies, waits for them, and re-layouts: 9.17 us -> 30.5 us
    pallas_call x2, Pallas kernels: 266 us -> 279 us  [the longest x1 270 us: forward(): pl.pallas_call(functools.partial(forward_kernel, line, width, block), out...]
    dynamic_slice x5 -> x1, local copies, waits for them, and re-layouts: 15 us -> 3.86 us  [of_half(): return lax.dynamic_slice_in_dim(a, which * size, size, axis=1)]
  transfers between devices with their start and end apart: 9 -> 1, of which waited for: 0 -> 0; matrix products, arithmetic and copies ran while one was open for 22% -> 6% of each run, Pallas kernels for 8% -> 1%
where the time goes in v2:
time: 689 us; the launch traced here: 680 us
  Pallas kernels  590 us (86%)
  matrix products  41.7 us (6%)
  local copies, waits for them, and re-layouts  40.7 us (6%)
    pallas_call x1, Pallas kernels, scatter(): pl.pallas_call(functools.partial(scatter_body, line, chunks, n, names), o...  277 us
    pallas_call x1, Pallas kernels, forward(): pl.pallas_call(functools.partial(forward_kernel, line, width, block), out...  270 us
    dot_general x5, matrix products, dot_tn(): lax.dot_general(a, b, (((0,), (0,)), ((), ())), preferred_element_type=jn...  41.7 us
    pallas_call x1, Pallas kernels, attend_back(): pl.pallas_call(functools.partial(attend_back_kernel, heads, groups), grid...  33.2 us
    unnamed x81, local copies, waits for them, and re-layouts  30.5 us
  transfers between devices with their start and end apart: 1, of which 0 were waited for; matrix products, arithmetic and copies ran while one was open for 6% of the time, Pallas kernels for 1%

profile of v2, /device:TPU:0, one launch (start us, length us, event | category | flops | bytes accessed | tf_op | source)
XLA Modules:
  0.0 679.9 jit_solution(4689556674122778764)
XLA Ops:
  0.7 1.0 fusion.14
  1.7 1.6 constant_dynamic-update-slice_fusion.26
  3.3 1.5 constant_dynamic-update-slice_fusion.25
  4.8 1.5 constant_dynamic-update-slice_fusion.24
  6.4 1.6 bitcast_dynamic-update-slice_fusion
  23.2 1.0 pad_maximum_fusion
  24.2 270.4 %gather_forward.1 = (bf16[4,2,2,96,16896]{4,3,2,1,0:T(8,128)(2,1)}, bf16[4,2,2,8,128]{4,3,2,1,0:T(8,128)(2,1)}, bf16[16,512,96]{2,1,0:T(8,128)(2,1)}, bf16[8,512...) custom-call(bf16[96,8448]{1,0:T(8,128)(2,1)} %constant_dynamic-updat, ...), custom_call_target="tpu_custom_call" | custom-call | tf_op jit(solution)/shard_map/gather_forward/pallas_call | solution.py:797
  294.6 33.2 %attend_back.1.grad = bf16[512,3072]{1,0:T(8,128)(2,1)} custom-call(bf16[16,512,96]{2,1,0:T(8,128)(2,1)} %get-tuple-element.61.q, bf16[8,512,96]{2,1,0:T(8,128)(2,1)} %get-tuple-element.62.k, bf16[8,512,96]{2,1,0:T(8,128)(2,1)} %get-tuple-element.63.v, bf16[512,1536]{1,0:T(8,128)(2,1)} %get-tuple-element.64.mixed, f32[512,1536]{1,0:T(8,128)} %get-tuple-element.65.grad_mixed, ...), custom_call_target="tpu_custom_call" | custom-call | tf_op jit(solution)/shard_map/attend_back/pallas_call | solution.py:483
  327.8 3.9 constant_dynamic-slice_fusion.1
  333.1 1.9 copy-done
  334.9 8.9 %against_columns.1 = f32[512,1536]{1,0:T(8,128)S(1)} custom-call(bf16[512,3072]{1,0:T(8,128)(2,1)S(1)} %copy-done, bf16[4,2,2,96,16896]{4,3,2,1,0:T(8,128)(2,1)} %get-tuple-element.66.weight), custom_call_target="tpu_custom_call" | custom-call | tf_op jit(solution)/shard_map/against_columns/pallas_call | solution.py:854
  343.9 0.9 fusion.7
  345.6 11.6 %bitcast_convert_fusion.1 = bf16[1536,2048]{1,0:T(8,128)(2,1)} fusion(bf16[2,512,1536]{2,1,0:T(8,128)(2,1)} %get-tuple-element.71, bf16[2,512,2048]{2,1,0:T(8,128)(2,1)} %get-tuple-element.72), kind=kOutput, calls=%fused_computation.1 | convolution fusion | flops 6445596672 | bytes 13631488 | tf_op jit(solution)/shard_map/dot_general | solution.py:354
  357.2 8.8 %bitcast_convert_fusion = bf16[1536,2048]{1,0:T(8,128)(2,1)} fusion(bf16[2,512,1536]{2,1,0:T(8,128)(2,1)S(1)} %copy-done.22, bf16[2,512,2048]{2,1,0:T(8,128)(2,1)S(1)} %copy-done.18), kind=kOutput, calls=%fused_computation | convolution fusion | flops 6445596672 | bytes 13631488 | tf_op jit(solution)/shard_map/dot_general | solution.py:354
  366.1 4.0 bitcast_convert_fusion.3
  370.1 2.5 fusion.6
  373.3 1.1 copy-done.20
  374.4 8.8 %bitcast_convert_fusion.2 = bf16[1536,2048]{1,0:T(8,128)(2,1)} fusion(bf16[2,512,1536]{2,1,0:T(8,128)(2,1)S(1)} %copy-done.20, bf16[2,512,2048]{2,1,0:T(8,128)(2,1)S(1)} %copy-done.17), kind=kOutput, calls=%fused_computation.2 | convolution fusion | flops 6445596672 | bytes 13631488 | tf_op jit(solution)/shard_map/dot_general | solution.py:354
  383.2 8.5 %convolution_convert_fusion = bf16[1536,1536]{1,0:T(8,128)(2,1)} fusion(bf16[1024,1536]{1,0:T(8,128)(2,1)S(1)} %bitcast.57, bf16[512,1536]{1,0:T(8,128)(2,1)} %collective-permute-done, bf16[512,1536]{1,0:T(8,128)(2,1)S(1)} %copy-done.5), kind=kOutput, calls=%fused_computation.3 | convolution fusion | flops 4840488960 | bytes 11010048 | tf_op jit(solution)/shard_map/dot_general | solution.py:354
  391.6 277.0 %gradient_scatter.1 = (f32[8,128]{1,0:T(8,128)}, f32[96,2048]{1,0:T(8,128)}, f32[96,2048]{1,0:T(8,128)}, f32[96,2048]{1,0:T(8,128)}, f32[96,768]{1,0:T(8,128)}, /*index=5*/f32[96,1536]{1,0:T(8,128)}) custom-call(bf16[4,2,2,8,128]{4,3,2,1,0:T(8,128)(2,1)} %bitcast.53, bf16[4,2,2,96,2048]{4,3,2,1,0:T(8,128)(2,1)} %bitcast.40, ...), custom_call_target="tpu_custom_call" | custom-call | tf_op jit(solution)/shard_map/gradient_scatter/pallas_call | solution.py:325
  668.7 1.7 slice.150
  670.4 1.7 fusion.17
  672.1 1.3 slice_bitcast_fusion
  673.4 2.7 copy.70
  (90 shorter events, 21.5 us)
Async XLA Ops:
  0.6 7.3 %copy-start.9 = (bf16[96,2048]{1,0:T(8,128)(2,1)S(1)}, bf16[96,2048]{1,0:T(8,128)(2,1)}, u32[]{:S(2)}) copy-start(bf16[96,2048]{1,0:T(8,128)(2,1)} %param.20) | copy-start | bytes 1179652
  0.7 7.9 %copy-start.10 = (bf16[96,2048]{1,0:T(8,128)(2,1)S(1)}, bf16[96,2048]{1,0:T(8,128)(2,1)}, u32[]{:S(2)}) copy-start(bf16[96,2048]{1,0:T(8,128)(2,1)} %param.21) | copy-start | bytes 1179652
  0.7 8.5 %copy-start.11 = (bf16[2048,96]{0,1:T(8,128)(2,1)S(1)}, bf16[2048,96]{0,1:T(8,128)(2,1)}, u32[]{:S(2)}) copy-start(bf16[2048,96]{0,1:T(8,128)(2,1)} %param.22) | copy-start | bytes 1179652
  1.7 21.3 %copy-start.15 = (bf16[96]{0:T(256)(128)(2,1)S(1)}, bf16[96]{0:T(256)(128)(2,1)}, u32[]{:S(2)}) copy-start(bf16[96]{0:T(256)(128)(2,1)} %param.23) | copy-start | bytes 580
  1.7 21.3 %copy-start.16 = (bf16[96]{0:T(256)(128)(2,1)S(1)}, bf16[96]{0:T(256)(128)(2,1)}, u32[]{:S(2)}) copy-start(bf16[96]{0:T(256)(128)(2,1)} %param.24) | copy-start | bytes 580
  327.8 3.9 copy-start.1
  327.8 4.3 copy-start.14
  331.7 51.5 %collective-permute-start = (bf16[512,1536]{1,0:T(8,128)(2,1)}, bf16[512,1536]{1,0:T(8,128)(2,1)}, u32[]{:S(2)}, u32[]{:S(2)}) collective-permute-start(bf16[512,1536]{1,0:T(8,128)(2,1)} %get-tuple-element.86), channel_id=1, source_target_pairs={{0,1},{1,0},{2,3},{3,2},{4,5},{5,4},{6,7},{7,6},{8,9},{9,8},{10,11... | collective-permute-start | bytes 4718600 | tf_op jit(solution)/shard_map/ppermute | solution.py:918
  333.0 1.9 copy-start
  334.9 8.9 %copy-start.2 = (bf16[512,1536]{1,0:T(8,128)(2,1)S(1)}, bf16[512,1536]{1,0:T(8,128)(2,1)}, u32[]{:S(2)}) copy-start(bf16[512,1536]{1,0:T(8,128)(2,1)} %refs_2_.1) | copy-start | bytes 4718596
  345.6 11.6 %copy-start.18 = (bf16[2,512,2048]{2,1,0:T(8,128)(2,1)S(1)}, bf16[2,512,2048]{2,1,0:T(8,128)(2,1)}, u32[]{:S(2)}) copy-start(bf16[2,512,2048]{2,1,0:T(8,128)(2,1)} %get-tuple-element.73) | copy-start | bytes 12582916
  345.6 11.6 %copy-start.22 = (bf16[2,512,1536]{2,1,0:T(8,128)(2,1)S(1)}, bf16[2,512,1536]{2,1,0:T(8,128)(2,1)}, u32[]{:S(2)}) copy-start(bf16[2,512,1536]{2,1,0:T(8,128)(2,1)} %get-tuple-element.71) | copy-start | bytes 9437188
  357.2 8.8 %copy-start.21 = (bf16[2,512,1536]{2,1,0:T(8,128)(2,1)S(1)}, bf16[2,512,1536]{2,1,0:T(8,128)(2,1)}, u32[]{:S(2)}) copy-start(bf16[2,512,1536]{2,1,0:T(8,128)(2,1)} %get-tuple-element.74) | copy-start | bytes 9437188
  357.2 8.8 %copy-start.23 = (bf16[2,512,768]{2,1,0:T(8,128)(2,1)S(1)}, bf16[2,512,768]{2,1,0:T(8,128)(2,1)}, u32[]{:S(2)}) copy-start(bf16[2,512,768]{2,1,0:T(8,128)(2,1)} %get-tuple-element.75) | copy-start | bytes 4718596
  366.1 4.0 copy-start.3
  366.1 4.0 copy-start.4
  370.1 3.2 copy-start.17
  370.1 4.3 copy-start.20
  374.4 8.8 %copy-start.5 = (bf16[512,1536]{1,0:T(8,128)(2,1)S(1)}, bf16[512,1536]{1,0:T(8,128)(2,1)}, u32[]{:S(2)}) copy-start(bf16[512,1536]{1,0:T(8,128)(2,1)} %get-tuple-element.85) | copy-start | bytes 4718596
  374.4 8.8 %copy-start.19 = (bf16[2,512,1536]{2,1,0:T(8,128)(2,1)S(1)}, bf16[2,512,1536]{2,1,0:T(8,128)(2,1)}, u32[]{:S(2)}) copy-start(bf16[2,512,1536]{2,1,0:T(8,128)(2,1)} %get-tuple-element.76) | copy-start | bytes 9437188
  672.1 4.0 copy-start.12
  673.4 3.4 copy-start.8
  676.1 1.6 copy-start.7
  676.8 1.8 copy-start.6
  (1 other events, 1.0 us)

commit v3 on v2

v3 whole, which is shorter than its diff:
```python
import functools
import math

import jax
import jax.numpy as jnp
from jax import lax
from jax.experimental import pallas as pl
from jax.experimental.pallas import tpu as pltpu
from jax.sharding import PartitionSpec as P

QUERY_HEADS = 16
KEY_VALUE_HEADS = 8
HEAD_SIZE = 96
SEQUENCE_LENGTH = 512

EPSILON = 1e-05
THETA_BASE = 100000.0
MESH = pl.DeviceIdType.MESH


def place():
    d = lax.axis_index("dp")
    return lax.div(d, 4), lax.rem(lax.div(d, 2), 2), lax.rem(d, 2), lax.axis_index("tensor")


def dev(z, y, x, c):
    return (z * 4 + y * 2 + x, c)


def enter(line, pos):
    z, y, x, c = pos
    barrier = pltpu.get_barrier_semaphore()

    def greet(who):
        pl.semaphore_signal(barrier, inc=1, device_id=who, device_id_type=MESH)

    greet(dev(z, y, x, 1 - c))
    greet(dev(z, y, 1 - x, c))
    greet(dev(z, 1 - y, x, c))

    @pl.when(z > 0)
    def _():
        greet(dev(z - 1, y, x, c))

    @pl.when(z < line - 1)
    def _():
        greet(dev(z + 1, y, x, c))

    pl.semaphore_wait(barrier, 3 + (z > 0).astype(jnp.int32) + (z < line - 1).astype(jnp.int32))


def remote(src, dst, send, recv, who):
    return pltpu.make_async_remote_copy(src_ref=src, dst_ref=dst, send_sem=send, recv_sem=recv, device_id=who, device_id_type=MESH)


class Gather:
    def __init__(self, line, pos, shard, full, width, orders, paired, send, recv):
        self.line, self.pos, self.shard, self.full, self.width = line, pos, shard, full, width
        self.orders, self.paired, self.send, self.recv = orders, paired, send, recv
        self.count = shard.shape[-1] // width
        self.depth = line + 1 + paired

    def columns(self, t, sub):
        part = self.width // len(self.orders[0])
        return t * self.width + sub * part, part

    def region(self, t, sub, have, z=None):
        first, part = self.columns(t, sub)
        pz, py, px, c = self.pos
        if self.paired:
            first = first + c * self.shard.shape[-1]
        every = slice(None)
        zi = z if z is not None else (every if "z" in have else pz)
        cols = pl.ds(pl.multiple_of(first, 128), part)
        return self.full.at[zi, every if "y" in have else py, every if "x" in have else px, :, cols]

    def own(self, t, sub):
        first, part = self.columns(t, sub)
        return self.shard.at[:, pl.ds(pl.multiple_of(first, 128), part)]

    def copy(self, t, sub, slot, src, dst, who):
        return remote(src, dst, self.send.at[t, sub, slot], self.recv.at[t, sub, slot], who)

    def hop(self, t, sub, h, up, have, what):
        z, y, x, c = self.pos
        slot = (h - 1) * 2 + up
        if up:
            block, incoming, who = z - (h - 1), z - h, dev(z + 1, y, x, c)
            there, here = (z + 1 < self.line) & (z >= h - 1), z >= h
        else:
            block, incoming, who = z + (h - 1), z + h, dev(z - 1, y, x, c)
            there, here = (z > 0) & (z + h - 1 < self.line), z + h < self.line

        @pl.when(here if what == "recv" else there)
        def _():
            if what == "recv":
                r = self.region(t, sub, have, incoming)
                self.copy(t, sub, slot, r, r, dev(z, y, x, 1 - c)).wait_recv()
                return
            r = self.region(t, sub, have, block)
            cp = self.copy(t, sub, slot, self.own(t, sub) if h == 1 and not have else r, r, who)
            cp.start() if what == "start" else cp.wait_send()

    def act(self, t, sub, order, i, what):
        z, y, x, c = self.pos
        moves, have = [], ""
        for axis in order:
            moves += [(axis, h, have) for h in (range(1, self.line) if axis == "z" else (0,))]
            have += axis
        if self.paired:
            moves.append(("c", 0, have))
        axis, h, have = moves[i]
        if axis == "z":
            for up in (1, 0):
                self.hop(t, sub, h, up, have, what)
            return
        who = {"y": dev(z, 1 - y, x, c), "x": dev(z, y, 1 - x, c), "c": dev(z, y, x, 1 - c)}[axis]
        land = self.region(t, sub, have)
        cp = self.copy(t, sub, 2 * (self.line - 1) + "yxc".index(axis), land if have else self.own(t, sub), land, who)
        {"start": cp.start, "recv": cp.wait_recv, "sent": cp.wait_send}[what]()

    def each(self, t, fn):
        there = (t >= 0) & (t < self.count)
        for v, orders in enumerate(self.orders):
            turn_of = there if len(self.orders) == 1 else there & ((lax.rem(t + 4, 4) == 0) == (v == 1))

            @pl.when(turn_of)
            def _():
                for sub, order in enumerate(orders):
                    fn(sub, order)

    def step(self, t, s):
        def go(sub, order):
            if s > 0:
                self.act(t, sub, order, s - 1, "recv")
            if s < self.depth:
                self.act(t, sub, order, s, "start")

        self.each(t, go)

    def advance(self, p):
        for s in range(self.depth + 1):
            self.step(p - s, s)

    def finish(self):
        @pl.loop(0, self.count)
        def _(t):
            self.each(t, lambda sub, order: [self.act(t, sub, order, i, "sent") for i in range(self.depth)])


def own_copy(g, sem):
    z, y, x, c = g.pos
    first = c * g.shard.shape[-1] if g.paired else 0
    return pltpu.make_async_copy(g.shard, g.full.at[z, y, x, :, pl.ds(pl.multiple_of(first, 128), g.shard.shape[-1])], sem)


def rope_tables(length, width):
    half_width = width // 2
    inverse = THETA_BASE ** (-(jnp.arange(half_width, dtype=jnp.float32) * 2.0 / width))
    angles = jnp.arange(length, dtype=jnp.float32)[:, None] * inverse[None, :]
    cosine, sine = jnp.cos(angles), jnp.sin(angles)
    return jnp.concatenate([cosine, cosine], axis=1), jnp.concatenate([-sine, sine], axis=1)


def turn(x, cosine, sine):
    half = x.shape[-1] // 2
    return x * cosine + jnp.concatenate([x[:, half:], x[:, :half]], axis=1) * sine


def dot_nt(a, b):
    return lax.dot_general(a, b, (((1,), (1,)), ((), ())), preferred_element_type=jnp.float32)


def dot_tn(a, b):
    return lax.dot_general(a, b, (((0,), (0,)), ((), ())), preferred_element_type=jnp.float32)


def dot_nn(a, b):
    return jnp.dot(a, b, preferred_element_type=jnp.float32)


BLOCK = 128


def causal_weights(q, k, b, heads):
    scores = dot_nt(q, k) * (1.0 / math.sqrt(HEAD_SIZE))
    n = scores.shape[1]
    row = lax.broadcasted_iota(jnp.int32, scores.shape, 0) % BLOCK + b * BLOCK
    keep = row >= lax.broadcasted_iota(jnp.int32, scores.shape, 1)
    scores = jnp.where(keep, scores, -jnp.inf)
    log_total = jnp.log(jnp.sum(jnp.exp(scores), axis=1, keepdims=True))
    return jnp.exp(scores - log_total)


def rows_of(ref, first, heads, rows):
    return jnp.concatenate([ref[first + i, rows] for i in range(heads)], axis=0)


ROWS = 128


def each_rows(tokens, step, fn):
    @pl.loop(0, tokens // step)
    def _(r):
        fn(pl.ds(pl.multiple_of(r * step, step), step))


def forward_kernel(line, width, block, *refs):
    refs = list(refs)
    take = lambda n: [refs.pop(0) for _ in range(n)]
    query_in, key_in, value_in, gate_in, up_in, out_in, down_in, gain_a, gain_b, hid, ct, cosine, sine = take(13)
    full, gains_full, q_out, k_out, v_out, mixed_out, n1_pair, n2_pair, ct_pair, mixed_pair, gm_pair = take(11)
    tile_pairs = take(3)
    hidden_out, grad_middle, grad_mixed, gain_sum, gain = take(5)
    wbuf, gain_buf, n1, n2, flat, qh, kh, vh, mh, mixed, middle, acc, grad_n2, act, tiles, shard, gains, turned = take(18)
    send, recv, gsend, grecv, own_sem, load_sem, gain_sem, local_sem, pair_send, pair_recv, tile_local, tile_send, tile_recv, shard_sem = take(14)

    pos = place()
    z, y, x, c = pos
    tokens, d_model = hid.shape
    half = shard.shape[-1]
    heads, groups = qh.shape[0] // 2, kh.shape[0] // 2
    sibling = dev(z, y, x, 1 - c)
    bf16, f32 = jnp.bfloat16, jnp.float32

    g = Gather(line, pos, shard, full, width, (("zyx", "zxy"), ("xyz", "yxz")), 1, send, recv)
    gg = Gather(line, pos, gains, gains_full, gains.shape[-1], (("zyx",),), 0, gsend, grecv)
    g_own, gg_own = own_copy(g, own_sem.at[0]), own_copy(gg, own_sem.at[1])
    steps = (half // width) - 3
    fills, at = [], 0
    for src in (query_in, key_in, value_in):
        fills.append((src, at, src.shape[1]))
        at += src.shape[1]
    out_at, at = at, at + out_in.shape[0]
    for j in range(steps):
        for i, src in enumerate((gate_in, up_in)):
            fills.append((src.at[:, pl.ds(j * block, block)], at + j * width + i * block, block))
    fills = [pltpu.make_async_copy(src, shard.at[:, pl.ds(to, n)], shard_sem.at[i]) for i, (src, to, n) in enumerate(fills)]
    for cp in fills:
        cp.start()
    gains[...] = jnp.zeros_like(gains)
    top = lax.broadcasted_iota(jnp.int32, (gains.shape[0], gain_a.shape[1]), 0) == 0
    gains[:, : gain_a.shape[1]] = jnp.where(top, gain_a[...].astype(f32), gain_b[...].astype(f32)).astype(bf16)
    shard[:, out_at:at] = out_in[...].T
    for j in range(steps):
        shard[:, at + j * width + 2 * block : at + (j + 1) * width] = down_in[j * block : (j + 1) * block, :].T
    enter(line, pos)
    for cp in fills:
        cp.wait()
    g_own.start()
    gg_own.start()

    def load(t, hh, slot):
        cols = pl.ds(pl.multiple_of(hh * half + t * width, 128), width)
        return pltpu.make_async_copy(full.at[:, :, :, :, cols], wbuf.at[slot, hh], load_sem.at[slot, hh])

    def weight(slot, hh):
        return wbuf[slot, hh].reshape(d_model, width)

    def share(i, own_src, own_dst, other_src, other_dst):
        return pltpu.make_async_copy(own_src, own_dst, local_sem.at[i]), remote(other_src, other_dst, pair_send.at[i], pair_recv.at[i], sibling)

    ends = (pl.ds(0, tokens), pl.ds(tokens, tokens))
    lefts = ((ct, ct_pair), (n1, n1_pair), (n2, n2_pair), (n1, gm_pair))
    shares = [share(i, turned.at[i], pair.at[:, ends[0]], turned.at[i], pair.at[:, ends[1]]) for i, (_, pair) in enumerate(lefts)]
    hw = mixed.shape[1] // 2
    side = lambda ref, s, w: ref.at[:, pl.ds(pl.multiple_of(s * w, 128), w)]
    shares.append(share(4, side(mixed, c, hw), mixed_pair.at[0], side(mixed, 1 - c, hw), mixed_pair.at[1]))
    keeps = [pltpu.make_async_copy(src, dst, local_sem.at[5 + i]) for i, (src, dst) in enumerate(((qh, q_out), (kh, k_out), (vh, v_out), (mixed, mixed_out)))]

    def begin(i):
        if i < len(lefts):
            span = 256

            @pl.loop(0, d_model // span)
            def _(e):
                at = pl.ds(pl.multiple_of(e * span, span), span)
                turned[i, at, :] = lefts[i][0][:, at].T

        for cp in shares[i]:
            cp.start()

    def end(i):
        for cp in shares[i]:
            cp.wait()

    def tile_copies(j, hh):
        slot = lax.rem(j, 2)
        cols = pl.ds(pl.multiple_of(j * block, 128), block)
        own = [pltpu.make_async_copy(tiles.at[slot, hh, i], pair.at[0, :, cols], tile_local.at[j, i]) for i, pair in enumerate(tile_pairs)]
        out = [remote(tiles.at[slot, hh, i], pair.at[1, :, cols], tile_send.at[j, i], tile_recv.at[j, i], sibling) for i, pair in enumerate(tile_pairs)]
        return own, out

    def drain_tiles(j):
        for cp in tile_copies(j, 0)[0]:
            cp.wait()
        for cp in tile_copies(j, 0)[1]:
            cp.wait_send()

    def normalize():
        loaded = pltpu.make_async_copy(gains_full, gain_buf, gain_sem)
        loaded.start()
        loaded.wait()
        n = d_model // (gain_buf.shape[0] * 4)
        table = gain_buf[...].astype(f32)
        for i in range(2):
            gain[i : i + 1, :] = jnp.concatenate([table[a, b, e, i : i + 1, :n] for a in range(gain_buf.shape[0]) for b in range(2) for e in range(2)], axis=1)

        def rows_of_norm(rows):
            v = hid[rows, :].astype(f32)
            v = v * lax.rsqrt(jnp.mean(v * v, axis=1, keepdims=True) + EPSILON)
            n1[rows, :] = (v * gain[0:1, :]).astype(bf16)

        each_rows(tokens, ROWS, rows_of_norm)
        begin(1)

    def project(slot, outs):
        @pl.loop(0, 2)
        def _(hh):
            flat[...] = dot_nn(n1[...], weight(slot, hh))

            def to_heads(rows):
                cos, sin = cosine[rows, :], sine[rows, :]
                first = 0
                for n, target, turned in outs:
                    for h in range(n):
                        v = flat[rows, (first + h) * HEAD_SIZE : (first + h + 1) * HEAD_SIZE]
                        target[hh * n + h, rows] = (turn(v, cos, sin) if turned else v).astype(bf16)
                    first += n

            each_rows(tokens, ROWS, to_heads)

    def attend_half(hh):
        per = heads // groups
        blocks = tokens // BLOCK

        @pl.loop(0, groups)
        def _(i):
            kv = hh * groups + i
            for b in range(blocks):
                rows, n = pl.ds(b * BLOCK, BLOCK), (b + 1) * BLOCK
                w = causal_weights(rows_of(qh, kv * per, per, rows), kh[kv, :n], b, per).astype(bf16)
                m = dot_nn(w, vh[kv, :n]).astype(bf16)
                for e in range(per):
                    mh[kv * per + e, rows] = m[e * BLOCK : (e + 1) * BLOCK]

    def leave_attention(slot):
        def join(rows):
            mixed[rows, :] = jnp.concatenate([mh[h, rows] for h in range(2 * heads)], axis=1)

        each_rows(tokens, ROWS, join)
        begin(4)
        for cp in keeps:
            cp.start()
        middle[...] = hid[...].astype(f32) + dot_nt(mixed[:, :hw], weight(slot, 0))
        middle[...] += dot_nt(mixed[:, hw:], weight(slot, 1))

        def rows_of_norm(rows):
            v = middle[rows, :]
            acc[rows, :] = v
            v = v * lax.rsqrt(jnp.mean(v * v, axis=1, keepdims=True) + EPSILON)
            n2[rows, :] = (v * gain[1:2, :]).astype(bf16)
            grad_n2[rows, :] = jnp.zeros_like(v)

        each_rows(tokens, ROWS, rows_of_norm)
        begin(2)

    def feed_forward(j, slot):
        @pl.when(j >= 2)
        def _():
            drain_tiles(j - 2)

        part = lax.rem(j, 2)

        @pl.loop(0, 2)
        def _(hh):
            act[0] = dot_nn(n2[...], weight(slot, hh)[:, :block])
            act[1] = dot_nn(n2[...], weight(slot, hh)[:, block : 2 * block])
            act[2] = dot_nn(ct[...], weight(slot, hh)[:, 2 * block :])

            def gated(rows):
                gate, up, grad = act[0, rows], act[1, rows], act[2, rows]
                sigma = jax.nn.sigmoid(gate)
                tiles[part, hh, 0, rows] = (gate * sigma * up).astype(bf16)
                tiles[part, hh, 1, rows] = (grad * up * sigma * (1.0 + gate * (1.0 - sigma))).astype(bf16)
                tiles[part, hh, 2, rows] = (grad * gate * sigma).astype(bf16)

            each_rows(tokens, ROWS // 2, gated)
            own, out = tile_copies(j, hh)

            @pl.when(hh == c)
            def _():
                for cp in own:
                    cp.start()

            @pl.when(hh != c)
            def _():
                for cp in out:
                    cp.start()

            acc[...] += dot_nt(tiles[part, hh, 0], weight(slot, hh)[:, 2 * block :])
            both = jnp.concatenate([tiles[part, hh, 1], tiles[part, hh, 2]], axis=1)
            grad_n2[...] += dot_nt(both, weight(slot, hh)[:, : 2 * block])

    count, lead = g.count, g.depth + 1

    @pl.loop(0, count + lead)
    def _(p):
        @pl.when(p == 0)
        def _():
            g_own.wait()
            gg_own.wait()
            begin(0)

        gg.advance(p)
        g.advance(p)
        u = p - lead

        @pl.when((u >= -1) & (u + 1 < count))
        def _():
            for hh in range(2):
                load(u + 1, hh, lax.rem(u + 1, 2)).start()

        @pl.when(u >= 0)
        def _():
            slot = lax.rem(u, 2)
            for hh in range(2):
                load(u, hh, slot).wait()

            @pl.when(u == 0)
            def _():
                normalize()
                project(slot, ((heads, qh, True),))

            @pl.when(u == 1)
            def _():
                project(slot, ((groups, kh, True), (groups, vh, False)))
                attend_half(0)

            @pl.when(u == 2)
            def _():
                attend_half(1)
                leave_attention(slot)

            @pl.when(u >= 3)
            def _():
                feed_forward(u - 3, slot)

    for hh in range(2):
        load(2, hh, 0).start()
    gain_sum[...] = jnp.zeros_like(gain_sum)

    def rows_back(rows):
        v = middle[rows, :]
        inverse = lax.rsqrt(jnp.mean(v * v, axis=1, keepdims=True) + EPSILON)
        unit, grad = v * inverse, grad_n2[rows, :]
        scaled = grad * gain[1:2, :]
        inner = jnp.mean(scaled * unit, axis=1, keepdims=True)
        total = ct[rows, :].astype(f32) + inverse * (scaled - unit * inner)
        grad_middle[rows, :] = total
        n1[rows, :] = total.astype(bf16)
        gain_sum[...] += jnp.sum(grad * unit, axis=0, keepdims=True)
        hidden_out[rows, :] = acc[rows, :].astype(bf16)

    each_rows(tokens, ROWS, rows_back)
    begin(3)
    for hh in range(2):
        load(2, hh, 0).wait()
        grad_mixed[:, hh * hw : (hh + 1) * hw] = dot_nn(n1[...], weight(0, hh))

    for i in (0, 1, 2, 3, 4):
        end(i)
    for cp in keeps:
        cp.wait()
    for j in range(max(steps - 2, 0), steps):
        drain_tiles(j)

    @pl.loop(0, steps)
    def _(j):
        for cp in tile_copies(j, 0)[1]:
            cp.wait_recv()

    g.finish()
    gg.finish()


def forward(line, shards, gain_pair, hidden_in, cotangent, cosine, sine, block):
    tokens, d_model = hidden_in.shape
    rows = gain_pair[0].shape[1]
    half = sum(s.shape[1] for s in shards[:5]) + sum(s.shape[0] for s in shards[5:])
    gains = jax.ShapeDtypeStruct((8, 128), jnp.bfloat16)
    width = 3 * block
    count = half // width
    steps = count - 3
    heads, groups = QUERY_HEADS // 2, KEY_VALUE_HEADS // 2
    bf16, f32 = jnp.bfloat16, jnp.float32
    struct = jax.ShapeDtypeStruct
    hbm, vmem = pl.BlockSpec(memory_space=pl.ANY), pl.BlockSpec(memory_space=pltpu.VMEM)
    dma = pltpu.SemaphoreType.DMA
    pair = struct((d_model, 2 * tokens), bf16)
    tile_pair = struct((2, tokens, steps * block), bf16)
    head_shape = lambda n: (n, tokens, HEAD_SIZE)
    slots = 2 * (line - 1) + 3
    outs = [
        struct((line, 2, 2, rows, 2 * half), bf16),
        struct((line, 2, 2) + gains.shape, bf16),
        struct(head_shape(2 * heads), bf16),
        struct(head_shape(2 * groups), bf16),
        struct(head_shape(2 * groups), bf16),
        struct((tokens, 2 * heads * HEAD_SIZE), bf16),
        pair,
        pair,
        pair,
        struct((2, tokens, heads * HEAD_SIZE), bf16),
        pair,
        tile_pair,
        tile_pair,
        tile_pair,
        struct((tokens, d_model), bf16),
        struct((tokens, d_model), f32),
        struct((tokens, 2 * heads * HEAD_SIZE), f32),
        struct((1, d_model), f32),
        struct((8, d_model), f32),
    ]
    V = pltpu.VMEM
    return pl.pallas_call(
        functools.partial(forward_kernel, line, width, block),
        out_shape=outs,
        in_specs=[hbm] * 5 + [vmem] * 8,
        out_specs=[hbm] * 14 + [vmem] * 5,
        scratch_shapes=[
            V((2, 2, line, 2, 2, rows, width), bf16),
            V((line, 2, 2) + gains.shape, bf16),
            V((tokens, d_model), bf16),
            V((tokens, d_model), bf16),
            V((tokens, width), f32),
            V(head_shape(2 * heads), bf16),
            V(head_shape(2 * groups), bf16),
            V(head_shape(2 * groups), bf16),
            V(head_shape(2 * heads), bf16),
            V((tokens, 2 * heads * HEAD_SIZE), bf16),
            V((tokens, d_model), f32),
            V((tokens, d_model), f32),
            V((tokens, d_model), f32),
            V((3, tokens, block), f32),
            V((2, 2, 3, tokens, block), bf16),
            V((rows, half), bf16),
            V(gains.shape, bf16),
            V((4, d_model, tokens), bf16),
            dma((count, 2, slots)),
            dma((count, 2, slots)),
            dma((1, 1, slots)),
            dma((1, 1, slots)),
            dma((2,)),
            dma((2, 2)),
            dma,
            dma((9,)),
            dma((5,)),
            dma((5,)),
            dma((steps, 3)),
            dma((steps, 3)),
            dma((steps, 3)),
            dma((3 + 2 * steps,)),
        ],
        compiler_params=pltpu.CompilerParams(collective_id=0, has_side_effects=True, vmem_limit_bytes=64 * 2**20 - 2**17),
        name="gather_forward",
    )(*shards, *gain_pair, hidden_in, cotangent, cosine, sine)


class Scatter:
    def __init__(self, line, pos, count, own, first, second, up, down, send, recv, final):
        self.line, self.pos, self.count, self.final = line, pos, count, final
        self.own, self.first, self.second, self.up, self.down, self.send, self.recv = own, first, second, up, down, send, recv
        self.ring, self.own_ring = first.shape[0], own.shape[0]
        self.lags = [0, 2, 4] + [5 + j for j in range(line - 1)] + [4 + line, 5 + line]
        self.depth = self.lags[-1]

    def copy(self, t, slot, src, dst, who):
        r = lax.rem(t, self.ring)
        return remote(src, dst, self.send.at[r, slot], self.recv.at[r, slot], who)

    def merge(self, dst, a, b, loops):
        def go(lead, rest):
            if not rest:
                dst[lead] = a[lead] + b[lead]
            elif rest[0] > 2:
                @pl.loop(0, rest[0])
                def _(i):
                    go(lead + (i,), rest[1:])
            else:
                for i in range(rest[0]):
                    go(lead + (i,), rest[1:])

        go((), loops)

    def pair_moves(self, t, v):
        z, y, x, c = self.pos
        r, o = lax.rem(t, self.ring), lax.rem(t, self.own_ring)
        own, first, second = self.own.at[o], self.first.at[r], self.second.at[r]
        over_x, over_y = dev(z, y, 1 - x, c), dev(z, 1 - y, x, c)
        if v == 0:
            give, keep, who = own.at[:, :, 1 - x], own.at[:, :, x], (over_x, over_y)
        else:
            give, keep, who = own.at[:, 1 - y], own.at[:, y], (over_y, over_x)
        a, b = (1 - y, y) if v == 0 else (1 - x, x)
        one = self.copy(t, 0, give, first, who[0])
        two = self.copy(t, 1, first.at[:, a], second, who[1])
        return one, two, keep, first, second, first.at[:, b]

    def hop(self, t, j):
        z, y, x, c = self.pos
        r = lax.rem(t, self.ring)
        cur = self.second.at[r]
        for way, ref, target, edge in ((0, self.up.at[r, j], self.line - 1 - j, z == 0), (1, self.down.at[r, j], j, z == self.line - 1)):
            nxt = dev(z + 1, y, x, c) if way == 0 else dev(z - 1, y, x, c)
            passes = (target > z) if way == 0 else (target < z)

            @pl.when(passes & edge)
            def _():
                self.copy(t, 2 + 2 * j + way, cur.at[target], ref, nxt).start()

            @pl.when(passes & ~edge)
            def _():
                cp = self.copy(t, 2 + 2 * j + way, ref, ref, nxt)
                cp.wait_recv()
                ref[...] = ref[...] + cur[target]
                cp.start()

    def close(self, t):
        z, y, x, c = self.pos
        r = lax.rem(t, self.ring)
        ku, kd = self.line - 1 - z, z
        has_up, has_down = z > 0, z < self.line - 1
        for has, way, ref, k in ((has_up, 0, self.up, ku), (has_down, 1, self.down, kd)):

            @pl.when(has)
            def _():
                self.copy(t, 2 + 2 * k + way, ref.at[r, k], ref.at[r, k], dev(z, y, x, 1 - c)).wait_recv()

        f32 = jnp.float32
        total = self.second[r, z].astype(f32)
        last = self.line - 2
        below = self.up[r, jnp.minimum(ku, last)].astype(f32)
        above = self.down[r, jnp.minimum(kd, last)].astype(f32)
        total = total + jnp.where(has_up, below, 0.0) + jnp.where(has_down, above, 0.0)
        self.final(t, total)

    def drain(self, t):
        z, y, x, c = self.pos
        r = lax.rem(t, self.ring)
        self.pair_moves(t, 0)[1].wait_send()
        for j in range(self.line - 1):
            for way, ref, target in ((0, self.up, self.line - 1 - j), (1, self.down, j)):

                @pl.when((target > z) if way == 0 else (target < z))
                def _():
                    self.copy(t, 2 + 2 * j + way, ref.at[r, j], ref.at[r, j], dev(z, y, x, 1 - c)).wait_send()

    def when(self, t, fn):
        @pl.when((t >= 0) & (t < self.count))
        def _():
            fn()

    def both(self, t, fn):
        for v in range(2):
            @pl.when((t >= 0) & (t < self.count) & (lax.rem(t + 2, 2) == v))
            def _():
                fn(v)

    def begin(self, t):
        self.both(t, lambda v: self.pair_moves(t, v)[0].start())

    def release(self, t):
        self.when(t, lambda: self.pair_moves(t, 0)[0].wait_send())

    def advance(self, p):
        line = self.line

        def one(v, t):
            first_copy, second_copy, keep, first, second, _ = self.pair_moves(t, v)
            first_copy.wait_recv()
            self.merge(first, first, keep, (line, 2))
            second_copy.start()

        def two(v, t):
            _, second_copy, _, _, second, keep = self.pair_moves(t, v)
            second_copy.wait_recv()
            self.merge(second, second, keep, (line,))

        t = p - self.lags[1]
        self.both(t, lambda v, t=t: one(v, t))
        t = p - self.lags[2]
        self.both(t, lambda v, t=t: two(v, t))
        for j in range(line - 1):
            t = p - self.lags[3 + j]
            self.when(t, lambda t=t, j=j: self.hop(t, j))
        t = p - self.lags[-2]
        self.when(t, lambda t=t: self.close(t))
        t = p - self.lags[-1]
        self.when(t, lambda t=t: self.drain(t))


def greet_all(n, pos):
    z, y, x, c = pos
    d = z * 4 + y * 2 + x
    barrier = pltpu.get_barrier_semaphore()

    @pl.loop(1, n)
    def _(i):
        pl.semaphore_signal(barrier, inc=1, device_id=(lax.rem(d + i, n), c), device_id_type=MESH)

    pl.semaphore_signal(barrier, inc=1, device_id=(d, 1 - c), device_id_type=MESH)
    pl.semaphore_wait(barrier, n)


def backward_kernel(line, cols, starts, *refs):
    refs = list(refs)
    take = lambda n: [refs.pop(0) for _ in range(n)]
    q, k, v, mixed, grad_mixed, full, hid, grad_middle, gains, gain_two, cosine, sine = take(12)
    n1_pair, n2_pair, ct_pair, gm_pair, mixed_pair, hidden_pair, gate_pair, up_pair = take(8)
    qkv_pair, grad_query, grad_key, grad_value, grad_in, out_out, out_gate, out_up, out_down, out_gains = take(10)
    own, first, second, up, down, xt, ybuf, qh, kh, vh, mh, gh, gm, dots, dq, dk, dv, dqkv, wbuf, gmid, hbuf, out_qkv, gain_one, part, parts_in, pair_in = take(26)
    send, recv, xsem, ysem, half_sem, wsem, msem, qkv_local, qkv_send, qkv_recv, part_send, part_recv, out_sem, swap_sem = take(14)

    pos = place()
    z, y, x, c = pos
    d = z * 4 + y * 2 + x
    n = line * 4
    tokens, d_model = hid.shape
    count = starts[-1]
    heads, groups = qh.shape[0], kh.shape[0]
    share = heads // groups
    blocks = tokens // BLOCK
    width = wbuf.shape[-1]
    half_width = dqkv.shape[1] // 2
    scale = 1.0 / math.sqrt(HEAD_SIZE)
    bf16, f32 = jnp.bfloat16, jnp.float32
    sources = (hidden_pair, gate_pair, up_pair, mixed_pair, qkv_pair)
    lefts = ((0, ct_pair), (starts[1], n2_pair), (starts[3], gm_pair), (starts[4], n1_pair))

    def final(t, total):
        for i, (out, turned) in enumerate(((out_down, True), (out_gate, False), (out_up, False), (out_out, True), (out_qkv, False))):
            at = pl.ds(pl.multiple_of((t - starts[i]) * cols, 128), cols)

            @pl.when((t >= starts[i]) & (t < starts[i + 1]))
            def _():
                if turned:
                    out[at, :] = total.T
                else:
                    out[:, at] = total

    s = Scatter(line, pos, count, own, first, second, up, down, send, recv, final)

    def load_left(i):
        return pltpu.make_async_copy(lefts[i][1], xt.at[i % 2], xsem.at[i % 2])

    def load_right(t, act):
        slot = lax.rem(t, 2)
        for i, src in enumerate(sources):
            at = pl.ds(pl.multiple_of((t - starts[i]) * cols, 128), cols)

            @pl.when((t >= starts[i]) & (t < starts[i + 1]))
            def _():
                cp = pltpu.make_async_copy(src.at[:, :, at], ybuf.at[slot], ysem.at[slot])
                cp.start() if act == "start" else cp.wait()

    def half_loads(hh):
        take_heads = lambda ref, m: ref.at[pl.ds(hh * m, m)]
        lanes = pl.ds(pl.multiple_of(hh * mh.shape[1], 128), mh.shape[1])
        pairs = ((take_heads(q, heads), qh), (take_heads(k, groups), kh), (take_heads(v, groups), vh), (mixed.at[:, lanes], mh), (grad_mixed.at[:, lanes], gh))
        return [pltpu.make_async_copy(src, dst, half_sem.at[i]) for i, (src, dst) in enumerate(pairs)]

    def half_load(hh, act):
        for cp in half_loads(hh):
            cp.start() if act == "start" else cp.wait()

    each = half_width // width
    half_columns = full.shape[-1] // 2

    def weights(i):
        at = pl.ds(pl.multiple_of((i // each) * half_columns + (i % each) * width, 128), width)
        return pltpu.make_async_copy(full.at[:, :, :, :, at], wbuf.at[i % 2], wsem.at[i % 2])

    others = [pltpu.make_async_copy(grad_middle, gmid, msem.at[0]), pltpu.make_async_copy(hid, hbuf, msem.at[1])]

    own_half = lambda ref, which: ref.at[:, pl.ds(pl.multiple_of(which * half_width, 128), half_width)]

    def qkv_copies():
        return (
            pltpu.make_async_copy(own_half(dqkv, c), qkv_pair.at[0], qkv_local),
            remote(own_half(dqkv, 1 - c), qkv_pair.at[1], qkv_send, qkv_recv, (d, 1 - c)),
        )

    def prepare(hh):
        half_load(hh, "wait")

        def rows_of_dots(rows):
            for h in range(heads):
                lanes = slice(h * HEAD_SIZE, (h + 1) * HEAD_SIZE)
                g = gh[rows, lanes]
                dots[h, rows] = jnp.sum(g * mh[rows, lanes].astype(f32), axis=1, keepdims=True)
                gm[h, rows] = g.astype(bf16)

        each_rows(tokens, ROWS, rows_of_dots)
        dk[...] = jnp.zeros_like(dk)
        dv[...] = jnp.zeros_like(dv)

    def group_back(g, which):
        for b in which:
            rows, m = pl.ds(b * BLOCK, BLOCK), (b + 1) * BLOCK
            qb, gb, db = (rows_of(ref, g * share, share, rows) for ref in (qh, gm, dots))
            kb, vb = kh[g, :m], vh[g, :m]
            p = causal_weights(qb, kb, b, share)
            ds = (p * (dot_nt(gb, vb) - db)).astype(bf16)
            dv[g, :m] += dot_tn(p.astype(bf16), gb)
            dk[g, :m] += dot_tn(ds, qb)
            r = dot_nn(ds, kb) * scale
            for i in range(share):
                dq[g * share + i, rows] = r[i * BLOCK : (i + 1) * BLOCK]

    def join(hh):
        def rows_of_join(rows):
            cos, sin = cosine[rows, :], -sine[rows, :]
            parts = [turn(dq[h, rows], cos, sin) for h in range(heads)]
            parts += [turn(dk[g, rows] * scale, cos, sin) for g in range(groups)]
            parts += [dv[g, rows] for g in range(groups)]
            dqkv[rows, pl.ds(pl.multiple_of(hh * half_width, 128), half_width)] = jnp.concatenate([a.astype(bf16) for a in parts], axis=1)

        each_rows(tokens, ROWS, rows_of_join)

    def against(i):
        weights(i).wait()
        r = dot_nt(dqkv[:, i * width : (i + 1) * width], wbuf[i % 2].reshape(d_model, width))
        if i == 0:
            grad_in[...] = r
        else:
            grad_in[...] += r
        if i + 2 < 2 * each:
            weights(i + 2).start()

    def norm_one_back():
        for cp in others:
            cp.wait()
        gain_one[...] = jnp.zeros_like(gain_one)

        def rows_back(rows):
            a = hbuf[rows, :].astype(f32)
            inverse = lax.rsqrt(jnp.mean(a * a, axis=1, keepdims=True) + EPSILON)
            unit, grad = a * inverse, grad_in[rows, :]
            scaled = grad * gains[0:1, :]
            inner = jnp.mean(scaled * unit, axis=1, keepdims=True)
            grad_in[rows, :] = gmid[rows, :] + inverse * (scaled - unit * inner)
            gain_one[...] += jnp.sum(grad * unit, axis=0, keepdims=True)

        each_rows(tokens, ROWS, rows_back)
        size = d_model // n
        part[...] = jnp.zeros_like(part)
        for i in range(n):
            for row, ref in enumerate((gain_one, gain_two)):
                part[i, row : row + 1, :size] = ref[:, i * size : (i + 1) * size]

    def part_copy(i):
        to = lax.rem(d + i, n)
        return remote(part.at[to], parts_in.at[i], part_send.at[i], part_recv.at[i], (to, c))

    load_left(0).start()
    load_left(1).start()
    load_right(0, "start")
    half_load(0, "start")
    for cp in others:
        cp.start()
    for i in range(2):
        weights(i).start()
    greet_all(n, pos)

    stages = 2 * groups + 2
    turns = 2 * stages
    norm_at = turns + 2 * each

    @pl.loop(0, count + s.depth)
    def _(p):
        s.release(p - s.own_ring)
        for i, (at, _) in enumerate(lefts):

            @pl.when(p == at)
            def _():
                load_left(i).wait()
                if 1 <= i < len(lefts) - 1:
                    load_left(i + 1).start()

        @pl.when(p == starts[4] - 2)
        def _():
            for cp in qkv_copies():
                cp.wait()

        @pl.when(p < count)
        def _():
            load_right(p, "wait")

            @pl.when(p + 1 < count)
            def _():
                load_right(p + 1, "start")

            side = lax.rem(sum((p >= at).astype(jnp.int32) for at, _ in lefts[1:]), 2)
            right = ybuf[lax.rem(p, 2)].reshape(2 * tokens, cols)
            own[lax.rem(p, s.own_ring)] = dot_nn(xt[side], right).reshape(own.shape[1:]).astype(bf16)
            s.begin(p)

        s.advance(p)

        @pl.when(p < turns)
        def _():
            hh, r = lax.div(p, stages), lax.rem(p, stages)

            @pl.when(r == 0)
            def _():
                prepare(hh)

            for e, which in enumerate((range(blocks - 1), range(blocks - 1, blocks))):

                @pl.when((r > 0) & (r <= 2 * groups) & (lax.rem(r + 1, 2) == e))
                def _():
                    group_back(lax.div(r - 1, 2), which)

            @pl.when(r == stages - 1)
            def _():
                join(hh)

                @pl.when(hh == 0)
                def _():
                    half_load(1, "start")

                @pl.when(hh == 1)
                def _():
                    for cp in qkv_copies():
                        cp.start()

        for i in range(2 * each):

            @pl.when(p == turns + i)
            def _():
                against(i)

        @pl.when(p == norm_at)
        def _():
            norm_one_back()

        @pl.when(p == norm_at + 1)
        def _():
            @pl.loop(1, n)
            def _(i):
                part_copy(i).start()

    total = part[d]

    @pl.loop(1, n)
    def _(i):
        part_copy(i).wait()

    total = total + jnp.sum(parts_in[1:], axis=0)
    out_gains[...] = total
    swap = remote(out_gains, pair_in, swap_sem.at[0], swap_sem.at[1], (d, 1 - c))
    swap.start()
    first_column = 0
    for i, out in enumerate((grad_query, grad_key, grad_value)):
        cp = pltpu.make_async_copy(out_qkv.at[:, pl.ds(first_column, out.shape[1])], out, out_sem.at[i])
        cp.start()
        cp.wait()
        first_column += out.shape[1]
    swap.wait()
    out_gains[...] += pair_in[...]
    for t in range(count - s.own_ring + s.depth, count):
        s.release(t)


def backward(line, cols, arrays, halves):
    q, k, v, mixed, grad_mixed, full, hid = arrays[:7]
    tokens, d_model = hid.shape
    rows = full.shape[3]
    n = line * 4
    down_w, gate_w, up_w, out_w, q_w, k_w, v_w = halves
    qkv_w = q_w + k_w + v_w
    starts = [0]
    for w in (down_w, gate_w, up_w, out_w, qkv_w):
        starts.append(starts[-1] + w // cols)
    heads, groups = q.shape[0] // 2, k.shape[0] // 2
    width = q_w
    bf16, f32 = jnp.bfloat16, jnp.float32
    struct, V, dma = jax.ShapeDtypeStruct, pltpu.VMEM, pltpu.SemaphoreType.DMA
    hbm, vmem = pl.BlockSpec(memory_space=pl.ANY), pl.BlockSpec(memory_space=pltpu.VMEM)
    ring, own_ring = line + 12, 4
    head = lambda m: (m, tokens, HEAD_SIZE)
    sems = 2 + 2 * (line - 1)
    outs = [struct((2, tokens, qkv_w), bf16)]
    outs += [struct((rows, w), f32) for w in (q_w, k_w, v_w)]
    outs += [struct((tokens, d_model), f32), struct((out_w, rows), f32), struct((rows, gate_w), f32), struct((rows, up_w), f32), struct((down_w, rows), f32), struct((8, 128), f32)]
    return pl.pallas_call(
        functools.partial(backward_kernel, line, cols, tuple(starts)),
        out_shape=outs,
        in_specs=[hbm] * 8 + [vmem] * 4 + [hbm] * 8,
        out_specs=[hbm] * 4 + [vmem] * 6,
        scratch_shapes=[
            V((own_ring, line, 2, 2, rows, cols), bf16),
            V((ring, line, 2, rows, cols), bf16),
            V((ring, line, rows, cols), bf16),
            V((ring, line - 1, rows, cols), bf16),
            V((ring, line - 1, rows, cols), bf16),
            V((2, d_model, 2 * tokens), bf16),
            V((2, 2, tokens, cols), bf16),
            V(head(heads), bf16),
            V(head(groups), bf16),
            V(head(groups), bf16),
            V((tokens, heads * HEAD_SIZE), bf16),
            V((tokens, heads * HEAD_SIZE), f32),
            V(head(heads), bf16),
            V((heads, tokens, 1), f32),
            V(head(heads), f32),
            V(head(groups), f32),
            V(head(groups), f32),
            V((tokens, 2 * qkv_w), bf16),
            V((2, line, 2, 2, rows, width), bf16),
            V((tokens, d_model), f32),
            V((tokens, d_model), bf16),
            V((rows, qkv_w), f32),
            V((1, d_model), f32),
            V((n, 8, 128), f32),
            V((n, 8, 128), f32),
            V((8, 128), f32),
            dma((ring, sems)),
            dma((ring, sems)),
            dma((2,)),
            dma((2,)),
            dma((5,)),
            dma((2,)),
            dma((2,)),
            dma,
            dma,
            dma,
            dma((n,)),
            dma((n,)),
            dma((3,)),
            dma((2,)),
        ],
        compiler_params=pltpu.CompilerParams(collective_id=1, has_side_effects=True, vmem_limit_bytes=64 * 2**20 - 2**17),
        name="backward_scatter",
    )(*arrays)


def layer(n_dp, n_tensor, hidden_in, query_weight, key_matrix, value_matrix, out_weight, gate_weight, up_weight, down_weight, attention_gain, feedforward_gain, cotangent):
    line = n_dp // 4
    rows = attention_gain.shape[0]
    block = (query_weight.shape[1] // 3) & -128
    cosine, sine = rope_tables(SEQUENCE_LENGTH, HEAD_SIZE)
    (full, _, q, k, v, mixed, n1, n2, ct, mixed_pair, gm, hidden, gate, up, hidden_out, grad_middle, grad_mixed, gain_two, gain_rows) = forward(
        line,
        (query_weight, key_matrix, value_matrix, gate_weight, up_weight, out_weight, down_weight),
        (attention_gain.reshape(1, rows), feedforward_gain.reshape(1, rows)),
        hidden_in,
        cotangent,
        cosine,
        sine,
        block,
    )
    arrays = (q, k, v, mixed, grad_mixed, full, hidden_in, grad_middle, gain_rows, gain_two, cosine, sine, n1, n2, ct, gm, mixed_pair, hidden, gate, up)
    halves = (down_weight.shape[0], gate_weight.shape[1], up_weight.shape[1], out_weight.shape[0], query_weight.shape[1], key_matrix.shape[1], value_matrix.shape[1])
    _, g_query, g_key, g_value, grad_in, g_out, g_gate, g_up, g_down, g_gains = backward(line, 256 if line <= 4 else 128, arrays, halves)
    return hidden_out, grad_in, g_query, g_key, g_value, g_out, g_gate, g_up, g_down, g_gains[0, :rows], g_gains[1, :rows]


def solution(mesh):
    split = P(("dp", "tensor"), None)
    row, column, gain = P("dp", "tensor"), P("tensor", "dp"), P("dp")
    return jax.shard_map(
        functools.partial(layer, mesh.shape["dp"], mesh.shape["tensor"]),
        mesh=mesh,
        in_specs=(split, row, row, row, column, row, row, column, gain, gain, split),
        out_specs=(split, split, row, row, row, column, row, row, column, gain, gain),
        check_vma=False,
    )
```

time: 689 us -> 626 us (0.909); the launches traced: 680 us -> 625 us
  matrix products: 41.7 us -> 0 us
  local copies, waits for them, and re-layouts: 40.7 us -> 17.5 us
  Pallas kernels: 590 us -> 605 us
    dot_general x5 -> x0, matrix products: 41.7 us -> none  [dot_tn(): lax.dot_general(a, b, (((0,), (0,)), ((), ())), preferred_element_type=jn...]
    unnamed x81 -> x23, local copies, waits for them, and re-layouts: 30.5 us -> 16.2 us
    pallas_call x3 -> x1, Pallas kernels: 319 us -> 332 us  [backward(): pl.pallas_call(functools.partial(backward_kernel, line, cols, tuple(start...]
  transfers between devices with their start and end apart: 1 -> 0, of which waited for: 0 -> 0; matrix products, arithmetic and copies ran while one was open for 6% -> 0% of each run, Pallas kernels for 1% -> 0%
where the time goes in v3:
time: 626 us; the launch traced here: 625 us
  Pallas kernels  605 us (97%)
  local copies, waits for them, and re-layouts  17.5 us (3%)
    pallas_call x1, Pallas kernels, backward(): pl.pallas_call(functools.partial(backward_kernel, line, cols, tuple(start...  332 us
    pallas_call x1, Pallas kernels, forward(): pl.pallas_call(functools.partial(forward_kernel, line, width, block), out...  273 us
    unnamed x23, local copies, waits for them, and re-layouts  16.2 us

profile of v3, /device:TPU:0, one launch (start us, length us, event | category | flops | bytes accessed | tf_op | source)
XLA Modules:
  0.0 625.3 jit_solution(6444475250158214671)
XLA Ops:
  0.7 1.7 copy.22.refs_5_
  2.4 2.0 copy.23.refs_6_
  4.4 1.0 fusion.2
  5.4 1.0 pad_maximum_fusion
  6.4 273.3 %gather_forward.1 = (bf16[4,2,2,96,16896]{4,3,2,1,0:T(8,128)(2,1)}, bf16[4,2,2,8,128]{4,3,2,1,0:T(8,128)(2,1)}, bf16[16,512,96]{2,1,0:T(8,128)(2,1)}, bf16[8,512...) custom-call(bf16[96,768]{1,0:T(8,128)(2,1)} %refs_0_.1, ...), custom_call_target="tpu_custom_call" | custom-call | tf_op jit(solution)/shard_map/gather_forward/pallas_call | solution.py:526
  279.7 331.8 %backward_scatter.1 = (bf16[2,512,1536]{2,1,0:T(8,128)(2,1)}, f32[96,768]{1,0:T(8,128)}, f32[96,384]{1,0:T(8,128)}, f32[96,384]{1,0:T(8,128)}, f32[512,1536]{1,0...) custom-call(bf16[16,512,96]{2,1,0:T(8,128)(2,1)} %get-tuple-element., ...), custom_call_target="tpu_custom_call" | custom-call | tf_op jit(solution)/shard_map/backward_scatter/pallas_call | solution.py:997
  611.5 0.0 copy-start
  611.5 1.3 slice_bitcast_fusion
  612.8 1.9 copy.24
  614.7 2.4 copy.25
  617.1 2.7 copy.33
  619.8 0.0 copy-done
  619.8 0.0 copy-start.2
  619.8 0.0 copy-start.1
  619.8 1.7 copy.34
  621.5 0.0 copy-done.3
  621.5 0.7 copy.35
  622.2 0.0 copy-done.5
  622.2 0.7 copy.36
  622.9 0.0 copy-done.4
  622.9 0.7 copy.37
  623.5 0.0 copy-done.2
  623.5 0.9 copy.38
  624.4 0.9 copy.39
  (5 shorter events, 0.0 us)
Async XLA Ops:
  611.5 8.3 %copy-start = (f32[512,1536]{1,0:T(8,128)S(1)}, f32[512,1536]{1,0:T(8,128)}, u32[]{:S(2)}) copy-start(f32[512,1536]{1,0:T(8,128)} %get-tuple-element.95) | copy-start | bytes 9437188
  619.8 1.7 copy-start.3
  619.8 2.4 copy-start.5
  619.8 3.1 copy-start.4
  619.8 3.7 copy-start.2
  619.8 4.6 copy-start.1

commit v4 on v3

--- a/solution.py
+++ b/solution.py
@@ -122,7 +122,7 @@
     def each(self, t, fn):
         there = (t >= 0) & (t < self.count)
         for v, orders in enumerate(self.orders):
-            turn_of = there if len(self.orders) == 1 else there & ((lax.rem(t + 4, 4) == 0) == (v == 1))
+            turn_of = there if len(self.orders) == 1 else there & ((lax.rem(t + 6, 6) == 0) == (v == 1))
 
             @pl.when(turn_of)
             def _():
@@ -209,10 +209,10 @@
     refs = list(refs)
     take = lambda n: [refs.pop(0) for _ in range(n)]
     query_in, key_in, value_in, gate_in, up_in, out_in, down_in, gain_a, gain_b, hid, ct, cosine, sine = take(13)
-    full, gains_full, q_out, k_out, v_out, mixed_out, n1_pair, n2_pair, ct_pair, mixed_pair, gm_pair = take(11)
+    full, gains_full, q_out, k_out, v_out, mixed_out, n1_pair, n2_pair, ct_pair, mixed_pair, middle_out = take(11)
     tile_pairs = take(3)
-    hidden_out, grad_middle, grad_mixed, gain_sum, gain = take(5)
-    wbuf, gain_buf, n1, n2, flat, qh, kh, vh, mh, mixed, middle, acc, grad_n2, act, tiles, shard, gains, turned = take(18)
+    hidden_out, grad_n2, gain = take(3)
+    wbuf, gain_buf, n1, n2, flat, qh, kh, vh, mh, mixed, middle, acc, act, tiles, shard, gains, turned = take(17)
     send, recv, gsend, grecv, own_sem, load_sem, gain_sem, local_sem, pair_send, pair_recv, tile_local, tile_send, tile_recv, shard_sem = take(14)
 
     pos = place()
@@ -231,9 +231,10 @@
     for src in (query_in, key_in, value_in):
         fills.append((src, at, src.shape[1]))
         at += src.shape[1]
-    out_at, at = at, at + out_in.shape[0]
+    fills.append((out_in, at, out_in.shape[1]))
+    at += out_in.shape[1]
     for j in range(steps):
-        for i, src in enumerate((gate_in, up_in)):
+        for i, src in enumerate((gate_in, up_in, down_in)):
             fills.append((src.at[:, pl.ds(j * block, block)], at + j * width + i * block, block))
     fills = [pltpu.make_async_copy(src, shard.at[:, pl.ds(to, n)], shard_sem.at[i]) for i, (src, to, n) in enumerate(fills)]
     for cp in fills:
@@ -241,9 +242,6 @@
     gains[...] = jnp.zeros_like(gains)
     top = lax.broadcasted_iota(jnp.int32, (gains.shape[0], gain_a.shape[1]), 0) == 0
     gains[:, : gain_a.shape[1]] = jnp.where(top, gain_a[...].astype(f32), gain_b[...].astype(f32)).astype(bf16)
-    shard[:, out_at:at] = out_in[...].T
-    for j in range(steps):
-        shard[:, at + j * width + 2 * block : at + (j + 1) * width] = down_in[j * block : (j + 1) * block, :].T
     enter(line, pos)
     for cp in fills:
         cp.wait()
@@ -261,12 +259,12 @@
         return pltpu.make_async_copy(own_src, own_dst, local_sem.at[i]), remote(other_src, other_dst, pair_send.at[i], pair_recv.at[i], sibling)
 
     ends = (pl.ds(0, tokens), pl.ds(tokens, tokens))
-    lefts = ((ct, ct_pair), (n1, n1_pair), (n2, n2_pair), (n1, gm_pair))
+    lefts = ((ct, ct_pair), (n1, n1_pair), (n2, n2_pair))
     shares = [share(i, turned.at[i], pair.at[:, ends[0]], turned.at[i], pair.at[:, ends[1]]) for i, (_, pair) in enumerate(lefts)]
     hw = mixed.shape[1] // 2
     side = lambda ref, s, w: ref.at[:, pl.ds(pl.multiple_of(s * w, 128), w)]
-    shares.append(share(4, side(mixed, c, hw), mixed_pair.at[0], side(mixed, 1 - c, hw), mixed_pair.at[1]))
-    keeps = [pltpu.make_async_copy(src, dst, local_sem.at[5 + i]) for i, (src, dst) in enumerate(((qh, q_out), (kh, k_out), (vh, v_out), (mixed, mixed_out)))]
+    shares.append(share(3, side(mixed, c, hw), mixed_pair.at[0], side(mixed, 1 - c, hw), mixed_pair.at[1]))
+    keeps = [pltpu.make_async_copy(src, dst, local_sem.at[4 + i]) for i, (src, dst) in enumerate(((qh, q_out), (kh, k_out), (vh, v_out), (mixed, mixed_out), (middle, middle_out)))]
 
     def begin(i):
         if i < len(lefts):
@@ -349,8 +347,8 @@
             mixed[rows, :] = jnp.concatenate([mh[h, rows] for h in range(2 * heads)], axis=1)
 
         each_rows(tokens, ROWS, join)
-        begin(4)
-        for cp in keeps:
+        begin(3)
+        for cp in keeps[:4]:
             cp.start()
         middle[...] = hid[...].astype(f32) + dot_nt(mixed[:, :hw], weight(slot, 0))
         middle[...] += dot_nt(mixed[:, hw:], weight(slot, 1))
@@ -362,6 +360,7 @@
             n2[rows, :] = (v * gain[1:2, :]).astype(bf16)
             grad_n2[rows, :] = jnp.zeros_like(v)
 
+        keeps[4].start()
         each_rows(tokens, ROWS, rows_of_norm)
         begin(2)
 
@@ -446,29 +445,11 @@
             def _():
                 feed_forward(u - 3, slot)
 
-    for hh in range(2):
-        load(2, hh, 0).start()
-    gain_sum[...] = jnp.zeros_like(gain_sum)
-
-    def rows_back(rows):
-        v = middle[rows, :]
-        inverse = lax.rsqrt(jnp.mean(v * v, axis=1, keepdims=True) + EPSILON)
-        unit, grad = v * inverse, grad_n2[rows, :]
-        scaled = grad * gain[1:2, :]
-        inner = jnp.mean(scaled * unit, axis=1, keepdims=True)
-        total = ct[rows, :].astype(f32) + inverse * (scaled - unit * inner)
-        grad_middle[rows, :] = total
-        n1[rows, :] = total.astype(bf16)
-        gain_sum[...] += jnp.sum(grad * unit, axis=0, keepdims=True)
+    def rows_out(rows):
         hidden_out[rows, :] = acc[rows, :].astype(bf16)
 
-    each_rows(tokens, ROWS, rows_back)
-    begin(3)
-    for hh in range(2):
-        load(2, hh, 0).wait()
-        grad_mixed[:, hh * hw : (hh + 1) * hw] = dot_nn(n1[...], weight(0, hh))
-
-    for i in (0, 1, 2, 3, 4):
+    each_rows(tokens, ROWS, rows_out)
+    for i in range(len(shares)):
         end(i)
     for cp in keeps:
         cp.wait()
@@ -487,7 +468,7 @@
 def forward(line, shards, gain_pair, hidden_in, cotangent, cosine, sine, block):
     tokens, d_model = hidden_in.shape
     rows = gain_pair[0].shape[1]
-    half = sum(s.shape[1] for s in shards[:5]) + sum(s.shape[0] for s in shards[5:])
+    half = sum(s.shape[1] for s in shards)
     gains = jax.ShapeDtypeStruct((8, 128), jnp.bfloat16)
     width = 3 * block
     count = half // width
@@ -512,22 +493,20 @@
         pair,
         pair,
         struct((2, tokens, heads * HEAD_SIZE), bf16),
-        pair,
+        struct((tokens, d_model), f32),
         tile_pair,
         tile_pair,
         tile_pair,
         struct((tokens, d_model), bf16),
         struct((tokens, d_model), f32),
-        struct((tokens, 2 * heads * HEAD_SIZE), f32),
-        struct((1, d_model), f32),
         struct((8, d_model), f32),
     ]
     V = pltpu.VMEM
     return pl.pallas_call(
         functools.partial(forward_kernel, line, width, block),
         out_shape=outs,
-        in_specs=[hbm] * 5 + [vmem] * 8,
-        out_specs=[hbm] * 14 + [vmem] * 5,
+        in_specs=[hbm] * 7 + [vmem] * 6,
+        out_specs=[hbm] * 14 + [vmem] * 3,
         scratch_shapes=[
             V((2, 2, line, 2, 2, rows, width), bf16),
             V((line, 2, 2) + gains.shape, bf16),
@@ -541,12 +520,11 @@
             V((tokens, 2 * heads * HEAD_SIZE), bf16),
             V((tokens, d_model), f32),
             V((tokens, d_model), f32),
-            V((tokens, d_model), f32),
             V((3, tokens, block), f32),
             V((2, 2, 3, tokens, block), bf16),
             V((rows, half), bf16),
             V(gains.shape, bf16),
-            V((4, d_model, tokens), bf16),
+            V((3, d_model, tokens), bf16),
             dma((count, 2, slots)),
             dma((count, 2, slots)),
             dma((1, 1, slots)),
@@ -555,12 +533,12 @@
             dma((2, 2)),
             dma,
             dma((9,)),
-            dma((5,)),
-            dma((5,)),
+            dma((4,)),
+            dma((4,)),
             dma((steps, 3)),
             dma((steps, 3)),
             dma((steps, 3)),
-            dma((3 + 2 * steps,)),
+            dma((4 + 3 * steps,)),
         ],
         compiler_params=pltpu.CompilerParams(collective_id=0, has_side_effects=True, vmem_limit_bytes=64 * 2**20 - 2**17),
         name="gather_forward",
@@ -607,24 +585,33 @@
         two = self.copy(t, 1, first.at[:, a], second, who[1])
         return one, two, keep, first, second, first.at[:, b]
 
-    def hop(self, t, j):
+    def hop(self, p, j, way):
         z, y, x, c = self.pos
-        r = lax.rem(t, self.ring)
-        cur = self.second.at[r]
-        for way, ref, target, edge in ((0, self.up.at[r, j], self.line - 1 - j, z == 0), (1, self.down.at[r, j], j, z == self.line - 1)):
+        last = self.line - 1
+        travelled = z if way == 0 else last - z
+        t = p - self.lags[3] - j - travelled
+        target = last - j if way == 0 else j
+        passes = (target > z) if way == 0 else (target < z)
+
+        def go():
+            r = lax.rem(t, self.ring)
+            cur, ref = self.second.at[r], (self.up if way == 0 else self.down).at[r, j]
             nxt = dev(z + 1, y, x, c) if way == 0 else dev(z - 1, y, x, c)
-            passes = (target > z) if way == 0 else (target < z)
-
-            @pl.when(passes & edge)
+
+            @pl.when(travelled == 0)
             def _():
                 self.copy(t, 2 + 2 * j + way, cur.at[target], ref, nxt).start()
 
-            @pl.when(passes & ~edge)
+            @pl.when(travelled > 0)
             def _():
                 cp = self.copy(t, 2 + 2 * j + way, ref, ref, nxt)
                 cp.wait_recv()
                 ref[...] = ref[...] + cur[target]
                 cp.start()
+
+        @pl.when(passes & (t >= 0) & (t < self.count))
+        def _():
+            go()
 
     def close(self, t):
         z, y, x, c = self.pos
@@ -692,8 +679,8 @@
         t = p - self.lags[2]
         self.both(t, lambda v, t=t: two(v, t))
         for j in range(line - 1):
-            t = p - self.lags[3 + j]
-            self.when(t, lambda t=t, j=j: self.hop(t, j))
+            for way in range(2):
+                self.hop(p, j, way)
         t = p - self.lags[-2]
         self.when(t, lambda t=t: self.close(t))
         t = p - self.lags[-1]
@@ -716,11 +703,11 @@
 def backward_kernel(line, cols, starts, *refs):
     refs = list(refs)
     take = lambda n: [refs.pop(0) for _ in range(n)]
-    q, k, v, mixed, grad_mixed, full, hid, grad_middle, gains, gain_two, cosine, sine = take(12)
-    n1_pair, n2_pair, ct_pair, gm_pair, mixed_pair, hidden_pair, gate_pair, up_pair = take(8)
-    qkv_pair, grad_query, grad_key, grad_value, grad_in, out_out, out_gate, out_up, out_down, out_gains = take(10)
-    own, first, second, up, down, xt, ybuf, qh, kh, vh, mh, gh, gm, dots, dq, dk, dv, dqkv, wbuf, gmid, hbuf, out_qkv, gain_one, part, parts_in, pair_in = take(26)
-    send, recv, xsem, ysem, half_sem, wsem, msem, qkv_local, qkv_send, qkv_recv, part_send, part_recv, out_sem, swap_sem = take(14)
+    q, k, v, mixed, full, hid, ct, middle, grad_n2, gains, cosine, sine = take(12)
+    n1_pair, n2_pair, ct_pair, mixed_pair, hidden_pair, gate_pair, up_pair = take(7)
+    qkv_pair, grad_query, grad_key, grad_value, grad_in, out_out, out_gate, out_up, out_down, out_gains, gm_pair = take(11)
+    own, first, second, up, down, xt, ybuf, qh, kh, vh, mh, gh, gm, dots, dq, dk, dv, dqkv, wbuf, gmid, hbuf, out_qkv, gain_one, part, parts_in, pair_in, gain_two, gmb, turned = take(29)
+    send, recv, xsem, ysem, half_sem, wsem, msem, qkv_local, qkv_send, qkv_recv, part_send, part_recv, out_sem, swap_sem, gm_sem = take(15)
 
     pos = place()
     z, y, x, c = pos
@@ -739,15 +726,12 @@
     lefts = ((0, ct_pair), (starts[1], n2_pair), (starts[3], gm_pair), (starts[4], n1_pair))
 
     def final(t, total):
-        for i, (out, turned) in enumerate(((out_down, True), (out_gate, False), (out_up, False), (out_out, True), (out_qkv, False))):
+        for i, out in enumerate((out_down, out_gate, out_up, out_out, out_qkv)):
             at = pl.ds(pl.multiple_of((t - starts[i]) * cols, 128), cols)
 
             @pl.when((t >= starts[i]) & (t < starts[i + 1]))
             def _():
-                if turned:
-                    out[at, :] = total.T
-                else:
-                    out[:, at] = total
+                out[:, at] = total
 
     s = Scatter(line, pos, count, own, first, second, up, down, send, recv, final)
 
@@ -767,7 +751,7 @@
     def half_loads(hh):
         take_heads = lambda ref, m: ref.at[pl.ds(hh * m, m)]
         lanes = pl.ds(pl.multiple_of(hh * mh.shape[1], 128), mh.shape[1])
-        pairs = ((take_heads(q, heads), qh), (take_heads(k, groups), kh), (take_heads(v, groups), vh), (mixed.at[:, lanes], mh), (grad_mixed.at[:, lanes], gh))
+        pairs = ((take_heads(q, heads), qh), (take_heads(k, groups), kh), (take_heads(v, groups), vh), (mixed.at[:, lanes], mh))
         return [pltpu.make_async_copy(src, dst, half_sem.at[i]) for i, (src, dst) in enumerate(pairs)]
 
     def half_load(hh, act):
@@ -778,10 +762,15 @@
     half_columns = full.shape[-1] // 2
 
     def weights(i):
-        at = pl.ds(pl.multiple_of((i // each) * half_columns + (i % each) * width, 128), width)
-        return pltpu.make_async_copy(full.at[:, :, :, :, at], wbuf.at[i % 2], wsem.at[i % 2])
-
-    others = [pltpu.make_async_copy(grad_middle, gmid, msem.at[0]), pltpu.make_async_copy(hid, hbuf, msem.at[1])]
+        at = (i * half_columns + each * width) if i < 2 else ((i - 2) // each * half_columns + (i - 2) % each * width)
+        return pltpu.make_async_copy(full.at[:, :, :, :, pl.ds(at, width)], wbuf.at[i % 2], wsem.at[i % 2])
+
+    def weight(i):
+        return wbuf[i % 2].reshape(d_model, width)
+
+    middle_in = pltpu.make_async_copy(middle, grad_in, msem.at[0])
+    grad_n2_in = pltpu.make_async_copy(grad_n2, gmid, msem.at[1])
+    ct_in, hid_in = (pltpu.make_async_copy(src, hbuf, msem.at[2]) for src in (ct, hid))
 
     own_half = lambda ref, which: ref.at[:, pl.ds(pl.multiple_of(which * half_width, 128), half_width)]
 
@@ -790,6 +779,45 @@
             pltpu.make_async_copy(own_half(dqkv, c), qkv_pair.at[0], qkv_local),
             remote(own_half(dqkv, 1 - c), qkv_pair.at[1], qkv_send, qkv_recv, (d, 1 - c)),
         )
+
+    def gm_copies():
+        return (
+            pltpu.make_async_copy(turned, gm_pair.at[:, pl.ds(0, tokens)], gm_sem.at[0]),
+            remote(turned, gm_pair.at[:, pl.ds(tokens, tokens)], gm_sem.at[1], gm_sem.at[2], (d, 1 - c)),
+        )
+
+    def norm_two_back():
+        for cp in (middle_in, grad_n2_in, ct_in):
+            cp.wait()
+        gain_two[...] = jnp.zeros_like(gain_two)
+
+        def rows_back(rows):
+            a, grad = grad_in[rows, :], gmid[rows, :]
+            inverse = lax.rsqrt(jnp.mean(a * a, axis=1, keepdims=True) + EPSILON)
+            unit = a * inverse
+            scaled = grad * gains[1:2, :]
+            inner = jnp.mean(scaled * unit, axis=1, keepdims=True)
+            total = hbuf[rows, :].astype(f32) + inverse * (scaled - unit * inner)
+            gmid[rows, :] = total
+            gmb[rows, :] = total.astype(bf16)
+            gain_two[...] += jnp.sum(grad * unit, axis=0, keepdims=True)
+
+        each_rows(tokens, ROWS, rows_back)
+        hid_in.start()
+        span = 256
+
+        @pl.loop(0, d_model // span)
+        def _(e):
+            at = pl.ds(pl.multiple_of(e * span, span), span)
+            turned[at, :] = gmb[:, at].T
+
+        for cp in gm_copies():
+            cp.start()
+
+    def through_out(i):
+        weights(i).wait()
+        gh[...] = dot_nn(gmb[...], weight(i))
+        weights(i + 2).start()
 
     def prepare(hh):
         half_load(hh, "wait")
@@ -829,18 +857,17 @@
         each_rows(tokens, ROWS, rows_of_join)
 
     def against(i):
-        weights(i).wait()
-        r = dot_nt(dqkv[:, i * width : (i + 1) * width], wbuf[i % 2].reshape(d_model, width))
+        weights(i + 2).wait()
+        r = dot_nt(dqkv[:, i * width : (i + 1) * width], weight(i))
         if i == 0:
             grad_in[...] = r
         else:
             grad_in[...] += r
         if i + 2 < 2 * each:
-            weights(i + 2).start()
+            weights(i + 4).start()
 
     def norm_one_back():
-        for cp in others:
-            cp.wait()
+        hid_in.wait()
         gain_one[...] = jnp.zeros_like(gain_one)
 
         def rows_back(rows):
@@ -867,14 +894,14 @@
     load_left(1).start()
     load_right(0, "start")
     half_load(0, "start")
-    for cp in others:
+    for cp in (middle_in, grad_n2_in, ct_in):
         cp.start()
     for i in range(2):
         weights(i).start()
     greet_all(n, pos)
 
-    stages = 2 * groups + 2
-    turns = 2 * stages
+    stages = 2 * groups + 3
+    turns = 1 + 2 * stages
     norm_at = turns + 2 * each
 
     @pl.loop(0, count + s.depth)
@@ -888,6 +915,11 @@
                 if 1 <= i < len(lefts) - 1:
                     load_left(i + 1).start()
 
+        @pl.when(p == starts[1] - 1)
+        def _():
+            for cp in gm_copies():
+                cp.wait()
+
         @pl.when(p == starts[4] - 2)
         def _():
             for cp in qkv_copies():
@@ -908,9 +940,19 @@
 
         s.advance(p)
 
-        @pl.when(p < turns)
-        def _():
-            hh, r = lax.div(p, stages), lax.rem(p, stages)
+        @pl.when(p == 0)
+        def _():
+            norm_two_back()
+
+        for i in range(2):
+
+            @pl.when(p == 1 + i * stages)
+            def _():
+                through_out(i)
+
+        @pl.when((p > 0) & (p < turns))
+        def _():
+            hh, r = lax.div(p - 1, stages), lax.rem(p - 1, stages) - 1
 
             @pl.when(r == 0)
             def _():
@@ -922,7 +964,7 @@
                 def _():
                     group_back(lax.div(r - 1, 2), which)
 
-            @pl.when(r == stages - 1)
+            @pl.when(r == stages - 2)
             def _():
                 join(hh)
 
@@ -974,7 +1016,7 @@
 
 
 def backward(line, cols, arrays, halves):
-    q, k, v, mixed, grad_mixed, full, hid = arrays[:7]
+    q, k, v, mixed, full, hid = arrays[:6]
     tokens, d_model = hid.shape
     rows = full.shape[3]
     n = line * 4
@@ -993,12 +1035,13 @@
     sems = 2 + 2 * (line - 1)
     outs = [struct((2, tokens, qkv_w), bf16)]
     outs += [struct((rows, w), f32) for w in (q_w, k_w, v_w)]
-    outs += [struct((tokens, d_model), f32), struct((out_w, rows), f32), struct((rows, gate_w), f32), struct((rows, up_w), f32), struct((down_w, rows), f32), struct((8, 128), f32)]
+    outs += [struct((tokens, d_model), f32), struct((rows, out_w), f32), struct((rows, gate_w), f32), struct((rows, up_w), f32), struct((rows, down_w), f32), struct((8, 128), f32)]
+    outs += [struct((d_model, 2 * tokens), bf16)]
     return pl.pallas_call(
         functools.partial(backward_kernel, line, cols, tuple(starts)),
         out_shape=outs,
-        in_specs=[hbm] * 8 + [vmem] * 4 + [hbm] * 8,
-        out_specs=[hbm] * 4 + [vmem] * 6,
+        in_specs=[hbm] * 9 + [vmem] * 3 + [hbm] * 7,
+        out_specs=[hbm] * 4 + [vmem] * 6 + [hbm],
         scratch_shapes=[
             V((own_ring, line, 2, 2, rows, cols), bf16),
             V((ring, line, 2, rows, cols), bf16),
@@ -1026,13 +1069,16 @@
             V((n, 8, 128), f32),
             V((n, 8, 128), f32),
             V((8, 128), f32),
+            V((1, d_model), f32),
+            V((tokens, d_model), bf16),
+            V((d_model, tokens), bf16),
             dma((ring, sems)),
             dma((ring, sems)),
             dma((2,)),
             dma((2,)),
-            dma((5,)),
+            dma((4,)),
             dma((2,)),
-            dma((2,)),
+            dma((3,)),
             dma,
             dma,
             dma,
@@ -1040,9 +1086,35 @@
             dma((n,)),
             dma((3,)),
             dma((2,)),
+            dma((3,)),
         ],
         compiler_params=pltpu.CompilerParams(collective_id=1, has_side_effects=True, vmem_limit_bytes=64 * 2**20 - 2**17),
         name="backward_scatter",
+    )(*arrays)
+
+
+def finish_kernel(n, *refs):
+    srcs, outs, bufs, (loads, stores) = refs[:n], refs[n : 2 * n], refs[2 * n : 3 * n], refs[3 * n :]
+    for i in range(n):
+        pltpu.make_async_copy(srcs[i], bufs[i], loads.at[i]).start()
+    for i in range(n):
+        pltpu.make_async_copy(srcs[i], bufs[i], loads.at[i]).wait()
+        pltpu.make_async_copy(bufs[i], outs[i], stores.at[i]).start()
+    for i in range(n):
+        pltpu.make_async_copy(bufs[i], outs[i], stores.at[i]).wait()
+
+
+def finish(arrays):
+    n = len(arrays)
+    hbm = pl.BlockSpec(memory_space=pl.ANY)
+    return pl.pallas_call(
+        functools.partial(finish_kernel, n),
+        out_shape=[jax.ShapeDtypeStruct(a.shape, a.dtype) for a in arrays],
+        in_specs=[hbm] * n,
+        out_specs=[hbm] * n,
+        scratch_shapes=[pltpu.VMEM(a.shape, a.dtype) for a in arrays] + [pltpu.SemaphoreType.DMA((n,)), pltpu.SemaphoreType.DMA((n,))],
+        compiler_params=pltpu.CompilerParams(vmem_limit_bytes=48 * 2**20),
+        name="finish",
     )(*arrays)
 
 
@@ -1051,9 +1123,9 @@
     rows = attention_gain.shape[0]
     block = (query_weight.shape[1] // 3) & -128
     cosine, sine = rope_tables(SEQUENCE_LENGTH, HEAD_SIZE)
-    (full, _, q, k, v, mixed, n1, n2, ct, mixed_pair, gm, hidden, gate, up, hidden_out, grad_middle, grad_mixed, gain_two, gain_rows) = forward(
+    (full, _, q, k, v, mixed, n1, n2, ct, mixed_pair, middle, hidden, gate, up, hidden_out, grad_n2, gain_rows) = forward(
         line,
-        (query_weight, key_matrix, value_matrix, gate_weight, up_weight, out_weight, down_weight),
+        (query_weight, key_matrix, value_matrix, gate_weight, up_weight, out_weight.T, down_weight.T),
         (attention_gain.reshape(1, rows), feedforward_gain.reshape(1, rows)),
         hidden_in,
         cotangent,
@@ -1061,10 +1133,12 @@
         sine,
         block,
     )
-    arrays = (q, k, v, mixed, grad_mixed, full, hidden_in, grad_middle, gain_rows, gain_two, cosine, sine, n1, n2, ct, gm, mixed_pair, hidden, gate, up)
+    arrays = (q, k, v, mixed, full, hidden_in, cotangent, middle, grad_n2, gain_rows, cosine, sine, n1, n2, ct, mixed_pair, hidden, gate, up)
     halves = (down_weight.shape[0], gate_weight.shape[1], up_weight.shape[1], out_weight.shape[0], query_weight.shape[1], key_matrix.shape[1], value_matrix.shape[1])
-    _, g_query, g_key, g_value, grad_in, g_out, g_gate, g_up, g_down, g_gains = backward(line, 256 if line <= 4 else 128, arrays, halves)
-    return hidden_out, grad_in, g_query, g_key, g_value, g_out, g_gate, g_up, g_down, g_gains[0, :rows], g_gains[1, :rows]
+    results = backward(line, 256 if line <= 4 else 128, arrays, halves)
+    g_query, g_key, g_value, grad_in, g_out, g_gate, g_up, g_down, hidden_out = finish(list(results[1:9]) + [hidden_out])
+    g_gains = results[9]
+    return hidden_out, grad_in, g_query, g_key, g_value, g_out.T, g_gate, g_up, g_down.T, g_gains[0, :rows], g_gains[1, :rows]
 
 
 def solution(mesh):

time: 626 us -> 539 us (0.86)
  Pallas kernels: 605 us -> 526 us
  local copies, waits for them, and re-layouts: 17.5 us -> 9.82 us
    pallas_call x1, Pallas kernels: 332 us -> 245 us  [backward(): pl.pallas_call(functools.partial(backward_kernel, line, cols, tuple(start...]
    unnamed x23 -> x16, local copies, waits for them, and re-layouts: 16.2 us -> 8.54 us
where the time goes in v4:
time: 539 us; the launch traced here: 538 us
  Pallas kernels  526 us (98%)
  local copies, waits for them, and re-layouts  9.82 us (2%)
    pallas_call x1, Pallas kernels, forward(): pl.pallas_call(functools.partial(forward_kernel, line, width, block), out...  275 us
    pallas_call x1, Pallas kernels, backward(): pl.pallas_call(functools.partial(backward_kernel, line, cols, tuple(start...  245 us

profile of v4, /device:TPU:0, one launch (start us, length us, event | category | flops | bytes accessed | tf_op | source)
XLA Modules:
  0.0 538.4 jit_solution(9149081762031169531)
XLA Ops:
  0.7 1.0 fusion.2
  1.7 1.0 pad_maximum_fusion
  2.6 274.7 %gather_forward.1 = (bf16[4,2,2,96,16896]{4,3,2,1,0:T(8,128)(2,1)}, bf16[4,2,2,8,128]{4,3,2,1,0:T(8,128)(2,1)}, bf16[16,512,96]{2,1,0:T(8,128)(2,1)}, bf16[8,512...) custom-call(bf16[96,768]{1,0:T(8,128)(2,1)} %refs_0_.1, ...), custom_call_target="tpu_custom_call" | custom-call | tf_op jit(solution)/shard_map/gather_forward/pallas_call | solution.py:505
  277.4 245.4 %backward_scatter.1 = (bf16[2,512,1536]{2,1,0:T(8,128)(2,1)}, f32[96,768]{1,0:T(8,128)}, f32[96,384]{1,0:T(8,128)}, f32[96,384]{1,0:T(8,128)}, f32[512,1536]{1,0...) custom-call(bf16[16,512,96]{2,1,0:T(8,128)(2,1)} %get-tuple-element., ...), custom_call_target="tpu_custom_call" | custom-call | tf_op jit(solution)/shard_map/backward_scatter/pallas_call | solution.py:1040
  522.8 0.0 copy-start
  522.8 1.4 copy-done
  524.2 0.0 copy-start.1
  524.2 1.1 copy-done.1
  525.3 0.0 copy-start.2
  525.4 1.1 copy-done.2
  526.5 0.0 copy-start.3
  526.5 1.1 copy-done.3
  527.6 0.0 copy-start.4
  527.6 1.0 copy-done.4
  528.6 0.0 copy-start.5
  528.6 1.0 copy-done.5
  529.5 0.0 copy-start.6
  529.5 0.9 copy-done.6
  530.5 0.0 copy-start.7
  530.5 0.9 copy-done.7
  531.4 5.7 %finish.1 = (f32[96,768]{1,0:T(8,128)}, f32[96,384]{1,0:T(8,128)}, f32[96,384]{1,0:T(8,128)}, f32[512,1536]{1,0:T(8,128)}, f32[96,768]{1,0:T(8,128)}, /*index=5*...) custom-call(f32[96,768]{1,0:T(8,128)S(1)} %copy-done.4, ...), custom_call_target="tpu_custom_call" | custom-call | tf_op jit(solution)/shard_map/finish/pallas_call | solution.py:1110
  537.1 1.3 slice_bitcast_fusion
  (1 shorter events, 0.0 us)
Async XLA Ops:
  522.8 1.4 copy-start
  524.2 1.1 copy-start.1
  525.3 1.1 copy-start.2
  526.5 1.1 copy-start.3
  527.6 1.0 copy-start.4
  528.6 1.0 copy-start.5
  529.5 0.9 copy-start.6
  530.5 0.9 copy-start.7

commit v5 on v4

--- a/solution.py
+++ b/solution.py
@@ -61,8 +61,7 @@
         self.depth = line + 1 + paired
 
     def columns(self, t, sub):
-        part = self.width // len(self.orders[0])
-        return t * self.width + sub * part, part
+        return t * self.width + sub[1], sub[2]
 
     def region(self, t, sub, have, z=None):
         first, part = self.columns(t, sub)
@@ -79,7 +78,7 @@
         return self.shard.at[:, pl.ds(pl.multiple_of(first, 128), part)]
 
     def copy(self, t, sub, slot, src, dst, who):
-        return remote(src, dst, self.send.at[t, sub, slot], self.recv.at[t, sub, slot], who)
+        return remote(src, dst, self.send.at[t, sub[0], slot], self.recv.at[t, sub[0], slot], who)
 
     def hop(self, t, sub, h, up, have, what):
         z, y, x, c = self.pos
@@ -122,12 +121,12 @@
     def each(self, t, fn):
         there = (t >= 0) & (t < self.count)
         for v, orders in enumerate(self.orders):
-            turn_of = there if len(self.orders) == 1 else there & ((lax.rem(t + 6, 6) == 0) == (v == 1))
+            turn_of = there if len(self.orders) == 1 else there & ((lax.rem(t + 3, 3) == 0) == (v == 1))
 
             @pl.when(turn_of)
             def _():
-                for sub, order in enumerate(orders):
-                    fn(sub, order)
+                for sub, (order, first, columns) in enumerate(orders):
+                    fn((sub, first, columns), order)
 
     def step(self, t, s):
         def go(sub, order):
@@ -223,8 +222,13 @@
     sibling = dev(z, y, x, 1 - c)
     bf16, f32 = jnp.bfloat16, jnp.float32
 
-    g = Gather(line, pos, shard, full, width, (("zyx", "zxy"), ("xyz", "yxz")), 1, send, recv)
-    gg = Gather(line, pos, gains, gains_full, gains.shape[-1], (("zyx",),), 0, gsend, grecv)
+    third, half_w = width // 3, width // 2
+    mixes = (
+        (("zyx", 0, third), ("zxy", third, third), ("xyz", 2 * third, third // 2), ("yxz", 2 * third + third // 2, third // 2)),
+        (("zyx", 0, half_w), ("zxy", half_w, half_w)),
+    )
+    g = Gather(line, pos, shard, full, width, mixes, 1, send, recv)
+    gg = Gather(line, pos, gains, gains_full, gains.shape[-1], ((("zyx", 0, gains.shape[-1]),),), 0, gsend, grecv)
     g_own, gg_own = own_copy(g, own_sem.at[0]), own_copy(gg, own_sem.at[1])
     steps = (half // width) - 3
     fills, at = [], 0
@@ -525,8 +529,8 @@
             V((rows, half), bf16),
             V(gains.shape, bf16),
             V((3, d_model, tokens), bf16),
-            dma((count, 2, slots)),
-            dma((count, 2, slots)),
+            dma((count, 4, slots)),
+            dma((count, 4, slots)),
             dma((1, 1, slots)),
             dma((1, 1, slots)),
             dma((2,)),
@@ -1113,7 +1117,7 @@
         in_specs=[hbm] * n,
         out_specs=[hbm] * n,
         scratch_shapes=[pltpu.VMEM(a.shape, a.dtype) for a in arrays] + [pltpu.SemaphoreType.DMA((n,)), pltpu.SemaphoreType.DMA((n,))],
-        compiler_params=pltpu.CompilerParams(vmem_limit_bytes=48 * 2**20),
+        compiler_params=pltpu.CompilerParams(vmem_limit_bytes=64 * 2**20 - 2**17),
         name="finish",
     )(*arrays)
 

time: 539 us -> 499 us (0.926)
  Pallas kernels: 526 us -> 494 us
  local copies, waits for them, and re-layouts: 9.82 us -> 1.27 us
    pallas_call x1, Pallas kernels: 275 us -> 243 us  [forward(): pl.pallas_call(functools.partial(forward_kernel, line, width, block), out...]
    unnamed x16 -> x0, local copies, waits for them, and re-layouts: 8.54 us -> none
where the time goes in v5:
time: 499 us; the launch traced here: 498 us
  Pallas kernels  494 us (99%)
    pallas_call x1, Pallas kernels, backward(): pl.pallas_call(functools.partial(backward_kernel, line, cols, tuple(start...  246 us
    pallas_call x1, Pallas kernels, forward(): pl.pallas_call(functools.partial(forward_kernel, line, width, block), out...  243 us

profile of v5, /device:TPU:0, one launch (start us, length us, event | category | flops | bytes accessed | tf_op | source)
XLA Modules:
  0.0 498.4 jit_solution(18284780730683779808)
XLA Ops:
  0.7 1.0 fusion.2
  1.7 1.0 pad_maximum_fusion
  2.6 242.8 %gather_forward.1 = (bf16[4,2,2,96,16896]{4,3,2,1,0:T(8,128)(2,1)}, bf16[4,2,2,8,128]{4,3,2,1,0:T(8,128)(2,1)}, bf16[16,512,96]{2,1,0:T(8,128)(2,1)}, bf16[8,512...) custom-call(bf16[96,768]{1,0:T(8,128)(2,1)} %refs_0_.1, ...), custom_call_target="tpu_custom_call" | custom-call | tf_op jit(solution)/shard_map/gather_forward/pallas_call | solution.py:509
  245.4 246.1 %backward_scatter.1 = (bf16[2,512,1536]{2,1,0:T(8,128)(2,1)}, f32[96,768]{1,0:T(8,128)}, f32[96,384]{1,0:T(8,128)}, f32[96,384]{1,0:T(8,128)}, f32[512,1536]{1,0...) custom-call(bf16[16,512,96]{2,1,0:T(8,128)(2,1)} %get-tuple-element., ...), custom_call_target="tpu_custom_call" | custom-call | tf_op jit(solution)/shard_map/backward_scatter/pallas_call | solution.py:1044
  491.6 5.5 %finish.1 = (f32[96,768]{1,0:T(8,128)}, f32[96,384]{1,0:T(8,128)}, f32[96,384]{1,0:T(8,128)}, f32[512,1536]{1,0:T(8,128)}, f32[96,768]{1,0:T(8,128)}, /*index=5*...) custom-call(f32[96,768]{1,0:T(8,128)} %get-tuple-element.60.refs_0_, ...), custom_call_target="tpu_custom_call" | custom-call | tf_op jit(solution)/shard_map/finish/pallas_call | solution.py:1114
  497.1 1.3 slice_bitcast_fusion
  (1 shorter events, 0.0 us)

commit v6 on v5

--- a/solution.py
+++ b/solution.py
@@ -550,16 +550,29 @@
 
 
 class Scatter:
-    def __init__(self, line, pos, count, own, first, second, up, down, send, recv, final):
+    def __init__(self, line, pos, count, plain, early, final):
         self.line, self.pos, self.count, self.final = line, pos, count, final
-        self.own, self.first, self.second, self.up, self.down, self.send, self.recv = own, first, second, up, down, send, recv
-        self.ring, self.own_ring = first.shape[0], own.shape[0]
-        self.lags = [0, 2, 4] + [5 + j for j in range(line - 1)] + [4 + line, 5 + line]
+        self.own, self.first, self.second, self.up, self.down, self.send, self.recv = plain
+        self.early = early
+        self.lags = [0, 2, 4, 5, 4 + line, 5 + line]
         self.depth = self.lags[-1]
 
-    def copy(self, t, slot, src, dst, who):
-        r = lax.rem(t, self.ring)
-        return remote(src, dst, self.send.at[r, slot], self.recv.at[r, slot], who)
+    def is_early(self, t):
+        return lax.rem(t + 5, 5) == 4
+
+    def plain_number(self, t):
+        return t - lax.div(t, 5)
+
+    def parts(self, t, early):
+        if early:
+            i, (own, first, second, up, down, send, recv) = lax.div(t, 5), self.early
+        else:
+            i, own, first, second, up, down, send, recv = self.plain_number(t), self.own, self.first, self.second, self.up, self.down, self.send, self.recv
+        o, r = lax.rem(i, own.shape[0]), lax.rem(i, first.shape[0])
+        return own.at[o], first.at[r], second.at[r], up.at[r], down.at[r], send.at[r], recv.at[r]
+
+    def place_of(self, t, early):
+        return self.parts(t, early)[0]
 
     def merge(self, dst, a, b, loops):
         def go(lead, rest):
@@ -577,118 +590,150 @@
 
     def pair_moves(self, t, v):
         z, y, x, c = self.pos
-        r, o = lax.rem(t, self.ring), lax.rem(t, self.own_ring)
-        own, first, second = self.own.at[o], self.first.at[r], self.second.at[r]
+        early = v >= 2
+        own, first, second, _, _, send, recv = self.parts(t, early)
         over_x, over_y = dev(z, y, 1 - x, c), dev(z, 1 - y, x, c)
-        if v == 0:
-            give, keep, who = own.at[:, :, 1 - x], own.at[:, :, x], (over_x, over_y)
+        lead = (z,) if early else (slice(None),)
+        if v % 2 == 0:
+            give, keep, who = own.at[lead + (slice(None), 1 - x)], own.at[lead + (slice(None), x)], (over_x, over_y)
         else:
-            give, keep, who = own.at[:, 1 - y], own.at[:, y], (over_y, over_x)
-        a, b = (1 - y, y) if v == 0 else (1 - x, x)
-        one = self.copy(t, 0, give, first, who[0])
-        two = self.copy(t, 1, first.at[:, a], second, who[1])
-        return one, two, keep, first, second, first.at[:, b]
-
-    def hop(self, p, j, way):
+            give, keep, who = own.at[lead + (1 - y,)], own.at[lead + (y,)], (over_y, over_x)
+        a, b = (1 - y, y) if v % 2 == 0 else (1 - x, x)
+        lead = () if early else (slice(None),)
+        one = remote(give, first, send.at[0], recv.at[0], who[0])
+        two = remote(first.at[lead + (a,)], second, send.at[1], recv.at[1], who[1])
+        return one, two, keep, first, second, first.at[lead + (b,)]
+
+    def hop(self, p, j, way, early):
         z, y, x, c = self.pos
         last = self.line - 1
         travelled = z if way == 0 else last - z
-        t = p - self.lags[3] - j - travelled
+        t = p - (0 if early else self.lags[3]) - j - travelled
         target = last - j if way == 0 else j
         passes = (target > z) if way == 0 else (target < z)
 
         def go():
-            r = lax.rem(t, self.ring)
-            cur, ref = self.second.at[r], (self.up if way == 0 else self.down).at[r, j]
+            own, _, second, up, down, send, recv = self.parts(t, early)
+            cur, ref = own if early else second, (up if way == 0 else down).at[j]
             nxt = dev(z + 1, y, x, c) if way == 0 else dev(z - 1, y, x, c)
+            slot = 2 + 2 * j + way
 
             @pl.when(travelled == 0)
             def _():
-                self.copy(t, 2 + 2 * j + way, cur.at[target], ref, nxt).start()
+                remote(cur.at[target], ref, send.at[slot], recv.at[slot], nxt).start()
 
             @pl.when(travelled > 0)
             def _():
-                cp = self.copy(t, 2 + 2 * j + way, ref, ref, nxt)
+                cp = remote(ref, ref, send.at[slot], recv.at[slot], nxt)
                 cp.wait_recv()
-                ref[...] = ref[...] + cur[target]
+                self.merge(ref, ref, cur.at[target], (2, 2) if early else ())
                 cp.start()
 
-        @pl.when(passes & (t >= 0) & (t < self.count))
+        @pl.when(passes & (t >= 0) & (t < self.count) & (self.is_early(t) == early))
         def _():
             go()
 
+    def arrive(self, t, early):
+        z, y, x, c = self.pos
+        _, _, _, up, down, send, recv = self.parts(t, early)
+        last = self.line - 1
+        ends = []
+        for way, ref, has, k in ((0, up, z > 0, last - z), (1, down, z < last, z)):
+
+            @pl.when(has)
+            def _():
+                slot = 2 + 2 * k + way
+                remote(ref.at[k], ref.at[k], send.at[slot], recv.at[slot], dev(z, y, x, 1 - c)).wait_recv()
+
+            ends.append((has, ref.at[jnp.minimum(k, last - 1)]))
+        return ends
+
     def close(self, t):
+        f32 = jnp.float32
+        total = self.parts(t, False)[2][self.pos[0]].astype(f32)
+        for has, ref in self.arrive(t, False):
+            total = total + jnp.where(has, ref[...].astype(f32), 0.0)
+        self.final(t, total)
+
+    def close_early(self, t, v):
+        z = self.pos[0]
+        mine = self.place_of(t, True).at[z]
+        ends = self.arrive(t, True)
+        for i in range(2):
+            for k in range(2):
+                total = mine[i, k].astype(jnp.float32)
+                for has, ref in ends:
+                    total = total + jnp.where(has, ref[i, k].astype(jnp.float32), 0.0)
+                mine[i, k] = total.astype(mine.dtype)
+        self.pair_moves(t, v)[0].start()
+
+    def drain(self, t, early):
         z, y, x, c = self.pos
-        r = lax.rem(t, self.ring)
-        ku, kd = self.line - 1 - z, z
-        has_up, has_down = z > 0, z < self.line - 1
-        for has, way, ref, k in ((has_up, 0, self.up, ku), (has_down, 1, self.down, kd)):
-
-            @pl.when(has)
-            def _():
-                self.copy(t, 2 + 2 * k + way, ref.at[r, k], ref.at[r, k], dev(z, y, x, 1 - c)).wait_recv()
-
-        f32 = jnp.float32
-        total = self.second[r, z].astype(f32)
-        last = self.line - 2
-        below = self.up[r, jnp.minimum(ku, last)].astype(f32)
-        above = self.down[r, jnp.minimum(kd, last)].astype(f32)
-        total = total + jnp.where(has_up, below, 0.0) + jnp.where(has_down, above, 0.0)
-        self.final(t, total)
-
-    def drain(self, t):
-        z, y, x, c = self.pos
-        r = lax.rem(t, self.ring)
-        self.pair_moves(t, 0)[1].wait_send()
+        _, _, _, up, down, send, recv = self.parts(t, early)
+        if early:
+            self.pair_moves(t, 2)[0].wait_send()
+        self.pair_moves(t, 2 * early)[1].wait_send()
         for j in range(self.line - 1):
-            for way, ref, target in ((0, self.up, self.line - 1 - j), (1, self.down, j)):
+            for way, ref, target in ((0, up, self.line - 1 - j), (1, down, j)):
 
                 @pl.when((target > z) if way == 0 else (target < z))
                 def _():
-                    self.copy(t, 2 + 2 * j + way, ref.at[r, j], ref.at[r, j], dev(z, y, x, 1 - c)).wait_send()
-
-    def when(self, t, fn):
-        @pl.when((t >= 0) & (t < self.count))
+                    slot = 2 + 2 * j + way
+                    remote(ref.at[j], ref.at[j], send.at[slot], recv.at[slot], dev(z, y, x, 1 - c)).wait_send()
+
+    def plain(self, t, fn):
+        @pl.when((t >= 0) & (t < self.count) & ~self.is_early(t))
         def _():
             fn()
 
-    def both(self, t, fn):
+    def sorts(self, t, fn, early):
+        number = lax.div(t, 5) if early else self.plain_number(t)
         for v in range(2):
-            @pl.when((t >= 0) & (t < self.count) & (lax.rem(t + 2, 2) == v))
-            def _():
-                fn(v)
+            @pl.when((t >= 0) & (t < self.count) & (self.is_early(t) == early) & (lax.rem(number + 2, 2) == v))
+            def _():
+                fn(v + 2 * early)
 
     def begin(self, t):
-        self.both(t, lambda v: self.pair_moves(t, v)[0].start())
-
-    def release(self, t):
-        self.when(t, lambda: self.pair_moves(t, 0)[0].wait_send())
+        self.sorts(t, lambda v: self.pair_moves(t, v)[0].start(), False)
+
+    def release(self, p):
+        t = p - self.own.shape[0] * 5 // 4
+        self.plain(t, lambda: self.pair_moves(t, 0)[0].wait_send())
 
     def advance(self, p):
         line = self.line
 
-        def one(v, t):
+        def one(t, v):
             first_copy, second_copy, keep, first, second, _ = self.pair_moves(t, v)
             first_copy.wait_recv()
-            self.merge(first, first, keep, (line, 2))
+            self.merge(first, first, keep, (2,) if v >= 2 else (line, 2))
             second_copy.start()
 
-        def two(v, t):
+        def two(t, v):
             _, second_copy, _, _, second, keep = self.pair_moves(t, v)
             second_copy.wait_recv()
-            self.merge(second, second, keep, (line,))
-
-        t = p - self.lags[1]
-        self.both(t, lambda v, t=t: one(v, t))
-        t = p - self.lags[2]
-        self.both(t, lambda v, t=t: two(v, t))
+            if v >= 2:
+                self.final(t, keep[...].astype(jnp.float32) + second[...].astype(jnp.float32))
+            else:
+                self.merge(second, second, keep, (line,))
+
         for j in range(line - 1):
             for way in range(2):
-                self.hop(p, j, way)
+                self.hop(p, j, way, True)
+        for step, lag, early in ((one, self.lags[1], False), (two, self.lags[2], False), (self.close_early, line, True), (one, line + 2, True), (two, line + 4, True)):
+            t = p - lag
+            self.sorts(t, lambda v, t=t, step=step: step(t, v), early)
+        for j in range(line - 1):
+            for way in range(2):
+                self.hop(p, j, way, False)
         t = p - self.lags[-2]
-        self.when(t, lambda t=t: self.close(t))
+        self.plain(t, lambda t=t: self.close(t))
         t = p - self.lags[-1]
-        self.when(t, lambda t=t: self.drain(t))
+        self.plain(t, lambda t=t: self.drain(t, False))
+
+        @pl.when((t >= 0) & (t < self.count) & self.is_early(t))
+        def _():
+            self.drain(t, True)
 
 
 def greet_all(n, pos):
@@ -710,8 +755,8 @@
     q, k, v, mixed, full, hid, ct, middle, grad_n2, gains, cosine, sine = take(12)
     n1_pair, n2_pair, ct_pair, mixed_pair, hidden_pair, gate_pair, up_pair = take(7)
     qkv_pair, grad_query, grad_key, grad_value, grad_in, out_out, out_gate, out_up, out_down, out_gains, gm_pair = take(11)
-    own, first, second, up, down, xt, ybuf, qh, kh, vh, mh, gh, gm, dots, dq, dk, dv, dqkv, wbuf, gmid, hbuf, out_qkv, gain_one, part, parts_in, pair_in, gain_two, gmb, turned = take(29)
-    send, recv, xsem, ysem, half_sem, wsem, msem, qkv_local, qkv_send, qkv_recv, part_send, part_recv, out_sem, swap_sem, gm_sem = take(15)
+    own, first, second, up, down, xt, ybuf, qh, kh, vh, mh, gh, gm, dots, dq, dk, dv, dqkv, wbuf, gmid, hbuf, out_qkv, gain_one, part, parts_in, pair_in, gain_two, gmb, turned, own_e, first_e, second_e, up_e, down_e = take(34)
+    send, recv, xsem, ysem, half_sem, wsem, msem, qkv_local, qkv_send, qkv_recv, part_send, part_recv, out_sem, swap_sem, gm_sem, send_e, recv_e = take(17)
 
     pos = place()
     z, y, x, c = pos
@@ -737,7 +782,7 @@
             def _():
                 out[:, at] = total
 
-    s = Scatter(line, pos, count, own, first, second, up, down, send, recv, final)
+    s = Scatter(line, pos, count, (own, first, second, up, down, send, recv), (own_e, first_e, second_e, up_e, down_e, send_e, recv_e), final)
 
     def load_left(i):
         return pltpu.make_async_copy(lefts[i][1], xt.at[i % 2], xsem.at[i % 2])
@@ -910,7 +955,7 @@
 
     @pl.loop(0, count + s.depth)
     def _(p):
-        s.release(p - s.own_ring)
+        s.release(p)
         for i, (at, _) in enumerate(lefts):
 
             @pl.when(p == at)
@@ -939,7 +984,12 @@
 
             side = lax.rem(sum((p >= at).astype(jnp.int32) for at, _ in lefts[1:]), 2)
             right = ybuf[lax.rem(p, 2)].reshape(2 * tokens, cols)
-            own[lax.rem(p, s.own_ring)] = dot_nn(xt[side], right).reshape(own.shape[1:]).astype(bf16)
+            for early in (False, True):
+
+                @pl.when(s.is_early(p) == early)
+                def _():
+                    s.place_of(p, early)[...] = dot_nn(xt[side], right).reshape(own.shape[1:]).astype(bf16)
+
             s.begin(p)
 
         s.advance(p)
@@ -1015,8 +1065,6 @@
         first_column += out.shape[1]
     swap.wait()
     out_gains[...] += pair_in[...]
-    for t in range(count - s.own_ring + s.depth, count):
-        s.release(t)
 
 
 def backward(line, cols, arrays, halves):
@@ -1034,7 +1082,8 @@
     bf16, f32 = jnp.bfloat16, jnp.float32
     struct, V, dma = jax.ShapeDtypeStruct, pltpu.VMEM, pltpu.SemaphoreType.DMA
     hbm, vmem = pl.BlockSpec(memory_space=pl.ANY), pl.BlockSpec(memory_space=pltpu.VMEM)
-    ring, own_ring = line + 12, 4
+    ring, own_ring = (line + 12) * 4 // 5 + 1, 4
+    ring_e, own_ring_e = (line + 16) // 5, (line + 5) // 5 + 1
     head = lambda m: (m, tokens, HEAD_SIZE)
     sems = 2 + 2 * (line - 1)
     outs = [struct((2, tokens, qkv_w), bf16)]
@@ -1076,6 +1125,11 @@
             V((1, d_model), f32),
             V((tokens, d_model), bf16),
             V((d_model, tokens), bf16),
+            V((own_ring_e, line, 2, 2, rows, cols), bf16),
+            V((ring_e, 2, rows, cols), bf16),
+            V((ring_e, rows, cols), bf16),
+            V((ring_e, line - 1, 2, 2, rows, cols), bf16),
+            V((ring_e, line - 1, 2, 2, rows, cols), bf16),
             dma((ring, sems)),
             dma((ring, sems)),
             dma((2,)),
@@ -1091,6 +1145,8 @@
             dma((3,)),
             dma((2,)),
             dma((3,)),
+            dma((ring_e, sems)),
+            dma((ring_e, sems)),
         ],
         compiler_params=pltpu.CompilerParams(collective_id=1, has_side_effects=True, vmem_limit_bytes=64 * 2**20 - 2**17),
         name="backward_scatter",

time: 499 us -> 469 us (0.940)
  Pallas kernels: 494 us -> 465 us
    pallas_call x1, Pallas kernels: 246 us -> 217 us  [backward(): pl.pallas_call(functools.partial(backward_kernel, line, cols, tuple(start...]
where the time goes in v6:
time: 469 us
  Pallas kernels  465 us (99%)
    pallas_call x1, Pallas kernels, forward(): pl.pallas_call(functools.partial(forward_kernel, line, width, block), out...  243 us
    pallas_call x1, Pallas kernels, backward(): pl.pallas_call(functools.partial(backward_kernel, line, cols, tuple(start...  217 us

profile of v6, /device:TPU:0, one launch (start us, length us, event | category | flops | bytes accessed | tf_op | source)
XLA Modules:
  0.0 468.9 jit_solution(4470704483770873588)
XLA Ops:
  0.7 1.0 fusion.2
  1.7 1.0 pad_maximum_fusion
  2.6 242.6 %gather_forward.1 = (bf16[4,2,2,96,16896]{4,3,2,1,0:T(8,128)(2,1)}, bf16[4,2,2,8,128]{4,3,2,1,0:T(8,128)(2,1)}, bf16[16,512,96]{2,1,0:T(8,128)(2,1)}, bf16[8,512...) custom-call(bf16[96,768]{1,0:T(8,128)(2,1)} %refs_0_.1, ...), custom_call_target="tpu_custom_call" | custom-call | tf_op jit(solution)/shard_map/gather_forward/pallas_call | solution.py:509
  245.3 216.8 %backward_scatter.1 = (bf16[2,512,1536]{2,1,0:T(8,128)(2,1)}, f32[96,768]{1,0:T(8,128)}, f32[96,384]{1,0:T(8,128)}, f32[96,384]{1,0:T(8,128)}, f32[512,1536]{1,0...) custom-call(bf16[16,512,96]{2,1,0:T(8,128)(2,1)} %get-tuple-element., ...), custom_call_target="tpu_custom_call" | custom-call | tf_op jit(solution)/shard_map/backward_scatter/pallas_call | solution.py:1093
  462.1 5.5 %finish.1 = (f32[96,768]{1,0:T(8,128)}, f32[96,384]{1,0:T(8,128)}, f32[96,384]{1,0:T(8,128)}, f32[512,1536]{1,0:T(8,128)}, f32[96,768]{1,0:T(8,128)}, /*index=5*...) custom-call(f32[96,768]{1,0:T(8,128)} %get-tuple-element.60.refs_0_, ...), custom_call_target="tpu_custom_call" | custom-call | tf_op jit(solution)/shard_map/finish/pallas_call | solution.py:1170
  467.6 1.3 slice_bitcast_fusion
  (1 shorter events, 0.0 us)

commit v7 on v6

--- a/solution.py
+++ b/solution.py
@@ -252,12 +252,12 @@
     g_own.start()
     gg_own.start()
 
-    def load(t, hh, slot):
+    def load(t, hh):
         cols = pl.ds(pl.multiple_of(hh * half + t * width, 128), width)
-        return pltpu.make_async_copy(full.at[:, :, :, :, cols], wbuf.at[slot, hh], load_sem.at[slot, hh])
-
-    def weight(slot, hh):
-        return wbuf[slot, hh].reshape(d_model, width)
+        return pltpu.make_async_copy(full.at[:, :, :, :, cols], wbuf.at[hh], load_sem.at[hh])
+
+    def weight(hh):
+        return wbuf[hh].reshape(d_model, width)
 
     def share(i, own_src, own_dst, other_src, other_dst):
         return pltpu.make_async_copy(own_src, own_dst, local_sem.at[i]), remote(other_src, other_dst, pair_send.at[i], pair_recv.at[i], sibling)
@@ -293,11 +293,16 @@
         out = [remote(tiles.at[slot, hh, i], pair.at[1, :, cols], tile_send.at[j, i], tile_recv.at[j, i], sibling) for i, pair in enumerate(tile_pairs)]
         return own, out
 
-    def drain_tiles(j):
-        for cp in tile_copies(j, 0)[0]:
-            cp.wait()
-        for cp in tile_copies(j, 0)[1]:
-            cp.wait_send()
+    def tile_act(j, hh, what):
+        @pl.when(hh == c)
+        def _():
+            for cp in tile_copies(j, hh)[0]:
+                cp.start() if what == "start" else cp.wait()
+
+        @pl.when(hh != c)
+        def _():
+            for cp in tile_copies(j, hh)[1]:
+                cp.start() if what == "start" else cp.wait_send()
 
     def normalize():
         loaded = pltpu.make_async_copy(gains_full, gain_buf, gain_sem)
@@ -316,21 +321,19 @@
         each_rows(tokens, ROWS, rows_of_norm)
         begin(1)
 
-    def project(slot, outs):
-        @pl.loop(0, 2)
-        def _(hh):
-            flat[...] = dot_nn(n1[...], weight(slot, hh))
-
-            def to_heads(rows):
-                cos, sin = cosine[rows, :], sine[rows, :]
-                first = 0
-                for n, target, turned in outs:
-                    for h in range(n):
-                        v = flat[rows, (first + h) * HEAD_SIZE : (first + h + 1) * HEAD_SIZE]
-                        target[hh * n + h, rows] = (turn(v, cos, sin) if turned else v).astype(bf16)
-                    first += n
-
-            each_rows(tokens, ROWS, to_heads)
+    def project(hh, outs):
+        flat[...] = dot_nn(n1[...], weight(hh))
+
+        def to_heads(rows):
+            cos, sin = cosine[rows, :], sine[rows, :]
+            first = 0
+            for n, target, turned in outs:
+                for h in range(n):
+                    v = flat[rows, (first + h) * HEAD_SIZE : (first + h + 1) * HEAD_SIZE]
+                    target[hh * n + h, rows] = (turn(v, cos, sin) if turned else v).astype(bf16)
+                first += n
+
+        each_rows(tokens, ROWS, to_heads)
 
     def attend_half(hh):
         per = heads // groups
@@ -346,108 +349,113 @@
                 for e in range(per):
                     mh[kv * per + e, rows] = m[e * BLOCK : (e + 1) * BLOCK]
 
-    def leave_attention(slot):
+        lanes = pl.ds(pl.multiple_of(hh * hw, 128), hw)
+
         def join(rows):
-            mixed[rows, :] = jnp.concatenate([mh[h, rows] for h in range(2 * heads)], axis=1)
+            mixed[rows, lanes] = jnp.concatenate([mh[hh * heads + h, rows] for h in range(heads)], axis=1)
 
         each_rows(tokens, ROWS, join)
-        begin(3)
-        for cp in keeps[:4]:
-            cp.start()
-        middle[...] = hid[...].astype(f32) + dot_nt(mixed[:, :hw], weight(slot, 0))
-        middle[...] += dot_nt(mixed[:, hw:], weight(slot, 1))
-
-        def rows_of_norm(rows):
-            v = middle[rows, :]
-            acc[rows, :] = v
-            v = v * lax.rsqrt(jnp.mean(v * v, axis=1, keepdims=True) + EPSILON)
-            n2[rows, :] = (v * gain[1:2, :]).astype(bf16)
-            grad_n2[rows, :] = jnp.zeros_like(v)
-
-        keeps[4].start()
-        each_rows(tokens, ROWS, rows_of_norm)
-        begin(2)
-
-    def feed_forward(j, slot):
+
+    def leave_attention(hh):
+        part = dot_nt(mixed[:, pl.ds(pl.multiple_of(hh * hw, 128), hw)], weight(hh))
+
+        @pl.when(hh == c)
+        def _():
+            middle[...] = hid[...].astype(f32) + part
+
+        @pl.when(hh != c)
+        def _():
+            middle[...] += part
+            begin(3)
+            for cp in keeps:
+                cp.start()
+
+            def rows_of_norm(rows):
+                v = middle[rows, :]
+                acc[rows, :] = v
+                v = v * lax.rsqrt(jnp.mean(v * v, axis=1, keepdims=True) + EPSILON)
+                n2[rows, :] = (v * gain[1:2, :]).astype(bf16)
+                grad_n2[rows, :] = jnp.zeros_like(v)
+
+            each_rows(tokens, ROWS, rows_of_norm)
+            begin(2)
+
+    def feed_forward(j, hh):
         @pl.when(j >= 2)
         def _():
-            drain_tiles(j - 2)
+            tile_act(j - 2, hh, "wait")
 
         part = lax.rem(j, 2)
-
-        @pl.loop(0, 2)
-        def _(hh):
-            act[0] = dot_nn(n2[...], weight(slot, hh)[:, :block])
-            act[1] = dot_nn(n2[...], weight(slot, hh)[:, block : 2 * block])
-            act[2] = dot_nn(ct[...], weight(slot, hh)[:, 2 * block :])
-
-            def gated(rows):
-                gate, up, grad = act[0, rows], act[1, rows], act[2, rows]
-                sigma = jax.nn.sigmoid(gate)
-                tiles[part, hh, 0, rows] = (gate * sigma * up).astype(bf16)
-                tiles[part, hh, 1, rows] = (grad * up * sigma * (1.0 + gate * (1.0 - sigma))).astype(bf16)
-                tiles[part, hh, 2, rows] = (grad * gate * sigma).astype(bf16)
-
-            each_rows(tokens, ROWS // 2, gated)
-            own, out = tile_copies(j, hh)
-
-            @pl.when(hh == c)
-            def _():
-                for cp in own:
-                    cp.start()
-
-            @pl.when(hh != c)
-            def _():
-                for cp in out:
-                    cp.start()
-
-            acc[...] += dot_nt(tiles[part, hh, 0], weight(slot, hh)[:, 2 * block :])
-            both = jnp.concatenate([tiles[part, hh, 1], tiles[part, hh, 2]], axis=1)
-            grad_n2[...] += dot_nt(both, weight(slot, hh)[:, : 2 * block])
-
-    count, lead = g.count, g.depth + 1
-
-    @pl.loop(0, count + lead)
+        act[0] = dot_nn(n2[...], weight(hh)[:, :block])
+        act[1] = dot_nn(n2[...], weight(hh)[:, block : 2 * block])
+        act[2] = dot_nn(ct[...], weight(hh)[:, 2 * block :])
+
+        def gated(rows):
+            gate, up, grad = act[0, rows], act[1, rows], act[2, rows]
+            sigma = jax.nn.sigmoid(gate)
+            tiles[part, hh, 0, rows] = (gate * sigma * up).astype(bf16)
+            tiles[part, hh, 1, rows] = (grad * up * sigma * (1.0 + gate * (1.0 - sigma))).astype(bf16)
+            tiles[part, hh, 2, rows] = (grad * gate * sigma).astype(bf16)
+
+        each_rows(tokens, ROWS // 2, gated)
+        tile_act(j, hh, "start")
+        acc[...] += dot_nt(tiles[part, hh, 0], weight(hh)[:, 2 * block :])
+        both = jnp.concatenate([tiles[part, hh, 1], tiles[part, hh, 2]], axis=1)
+        grad_n2[...] += dot_nt(both, weight(hh)[:, : 2 * block])
+
+    count = g.count
+
+    @pl.loop(0, count + g.depth)
     def _(p):
+        gg.advance(p)
+        g.advance(p)
+
         @pl.when(p == 0)
         def _():
             g_own.wait()
             gg_own.wait()
+
+        @pl.when(p == 1)
+        def _():
             begin(0)
 
-        gg.advance(p)
-        g.advance(p)
-        u = p - lead
-
-        @pl.when((u >= -1) & (u + 1 < count))
-        def _():
-            for hh in range(2):
-                load(u + 1, hh, lax.rem(u + 1, 2)).start()
-
-        @pl.when(u >= 0)
-        def _():
-            slot = lax.rem(u, 2)
-            for hh in range(2):
-                load(u, hh, slot).wait()
-
-            @pl.when(u == 0)
-            def _():
-                normalize()
-                project(slot, ((heads, qh, True),))
-
-            @pl.when(u == 1)
-            def _():
-                project(slot, ((groups, kh, True), (groups, vh, False)))
-                attend_half(0)
-
-            @pl.when(u == 2)
-            def _():
-                attend_half(1)
-                leave_attention(slot)
-
-            @pl.when(u >= 3)
-            def _():
-                feed_forward(u - 3, slot)
+        chunk_of = lambda hh: jnp.where(hh == c, p - g.depth + 1, p - g.depth)
+        for hh in range(2):
+            u = chunk_of(hh)
+
+            @pl.when((u >= 0) & (u < count))
+            def _():
+                load(u, hh).start()
+
+        @pl.loop(0, 2)
+        def _(i):
+            hh = jnp.where(i == 0, 1 - c, c)
+            u = chunk_of(hh)
+
+            @pl.when((u >= 0) & (u < count))
+            def _():
+                load(u, hh).wait()
+
+                @pl.when((u == 0) & (hh == c))
+                def _():
+                    normalize()
+
+                @pl.when(u == 0)
+                def _():
+                    project(hh, ((heads, qh, True),))
+
+                @pl.when(u == 1)
+                def _():
+                    project(hh, ((groups, kh, True), (groups, vh, False)))
+                    attend_half(hh)
+
+                @pl.when(u == 2)
+                def _():
+                    leave_attention(hh)
+
+                @pl.when(u >= 3)
+                def _():
+                    feed_forward(u - 3, hh)
 
     def rows_out(rows):
         hidden_out[rows, :] = acc[rows, :].astype(bf16)
@@ -458,7 +466,8 @@
     for cp in keeps:
         cp.wait()
     for j in range(max(steps - 2, 0), steps):
-        drain_tiles(j)
+        for hh in range(2):
+            tile_act(j, hh, "wait")
 
     @pl.loop(0, steps)
     def _(j):
@@ -512,7 +521,7 @@
         in_specs=[hbm] * 7 + [vmem] * 6,
         out_specs=[hbm] * 14 + [vmem] * 3,
         scratch_shapes=[
-            V((2, 2, line, 2, 2, rows, width), bf16),
+            V((2, line, 2, 2, rows, width), bf16),
             V((line, 2, 2) + gains.shape, bf16),
             V((tokens, d_model), bf16),
             V((tokens, d_model), bf16),
@@ -534,7 +543,7 @@
             dma((1, 1, slots)),
             dma((1, 1, slots)),
             dma((2,)),
-            dma((2, 2)),
+            dma((2,)),
             dma,
             dma((9,)),
             dma((4,)),
@@ -754,8 +763,8 @@
     take = lambda n: [refs.pop(0) for _ in range(n)]
     q, k, v, mixed, full, hid, ct, middle, grad_n2, gains, cosine, sine = take(12)
     n1_pair, n2_pair, ct_pair, mixed_pair, hidden_pair, gate_pair, up_pair = take(7)
-    qkv_pair, grad_query, grad_key, grad_value, grad_in, out_out, out_gate, out_up, out_down, out_gains, gm_pair = take(11)
-    own, first, second, up, down, xt, ybuf, qh, kh, vh, mh, gh, gm, dots, dq, dk, dv, dqkv, wbuf, gmid, hbuf, out_qkv, gain_one, part, parts_in, pair_in, gain_two, gmb, turned, own_e, first_e, second_e, up_e, down_e = take(34)
+    qkv_pair, grad_query, grad_key, grad_value, grad_in_out, out_out, out_gate, out_up, out_down, out_gains, gm_pair = take(11)
+    own, first, second, up, down, xt, ybuf, qh, kh, vh, mh, gh, gm, dots, dq, dk, dv, dqkv, wbuf, gmid, hbuf, out_qkv, gain_one, part, parts_in, pair_in, gain_two, gmb, turned, own_e, first_e, second_e, up_e, down_e, grad_in = take(35)
     send, recv, xsem, ysem, half_sem, wsem, msem, qkv_local, qkv_send, qkv_recv, part_send, part_recv, out_sem, swap_sem, gm_sem, send_e, recv_e = take(17)
 
     pos = place()
@@ -949,8 +958,11 @@
         weights(i).start()
     greet_all(n, pos)
 
+    swap = remote(out_gains, pair_in, swap_sem.at[0], swap_sem.at[1], (d, 1 - c))
+    grad_in_copy = pltpu.make_async_copy(grad_in, grad_in_out, out_sem.at[3])
     stages = 2 * groups + 3
-    turns = 1 + 2 * stages
+    chain = 1
+    turns = chain + 2 * stages
     norm_at = turns + 2 * each
 
     @pl.loop(0, count + s.depth)
@@ -994,19 +1006,19 @@
 
         s.advance(p)
 
-        @pl.when(p == 0)
+        @pl.when(p == chain - 1)
         def _():
             norm_two_back()
 
         for i in range(2):
 
-            @pl.when(p == 1 + i * stages)
+            @pl.when(p == chain + i * stages)
             def _():
                 through_out(i)
 
-        @pl.when((p > 0) & (p < turns))
-        def _():
-            hh, r = lax.div(p - 1, stages), lax.rem(p - 1, stages) - 1
+        @pl.when((p >= chain) & (p < turns))
+        def _():
+            hh, r = lax.div(p - chain, stages), lax.rem(p - chain, stages) - 1
 
             @pl.when(r == 0)
             def _():
@@ -1043,28 +1055,31 @@
 
         @pl.when(p == norm_at + 1)
         def _():
+            grad_in_copy.start()
+
             @pl.loop(1, n)
             def _(i):
                 part_copy(i).start()
 
-    total = part[d]
-
-    @pl.loop(1, n)
-    def _(i):
-        part_copy(i).wait()
-
-    total = total + jnp.sum(parts_in[1:], axis=0)
-    out_gains[...] = total
-    swap = remote(out_gains, pair_in, swap_sem.at[0], swap_sem.at[1], (d, 1 - c))
-    swap.start()
-    first_column = 0
+        @pl.when(p == count + s.depth - 2)
+        def _():
+            @pl.loop(1, n)
+            def _(i):
+                part_copy(i).wait()
+
+            out_gains[...] = part[d] + jnp.sum(parts_in[1:], axis=0)
+            swap.start()
+
+    ends, first_column = [grad_in_copy], 0
     for i, out in enumerate((grad_query, grad_key, grad_value)):
         cp = pltpu.make_async_copy(out_qkv.at[:, pl.ds(first_column, out.shape[1])], out, out_sem.at[i])
         cp.start()
-        cp.wait()
+        ends.append(cp)
         first_column += out.shape[1]
     swap.wait()
     out_gains[...] += pair_in[...]
+    for cp in ends:
+        cp.wait()
 
 
 def backward(line, cols, arrays, halves):
@@ -1094,7 +1109,7 @@
         functools.partial(backward_kernel, line, cols, tuple(starts)),
         out_shape=outs,
         in_specs=[hbm] * 9 + [vmem] * 3 + [hbm] * 7,
-        out_specs=[hbm] * 4 + [vmem] * 6 + [hbm],
+        out_specs=[hbm] * 5 + [vmem] * 5 + [hbm],
         scratch_shapes=[
             V((own_ring, line, 2, 2, rows, cols), bf16),
             V((ring, line, 2, rows, cols), bf16),
@@ -1130,6 +1145,7 @@
             V((ring_e, rows, cols), bf16),
             V((ring_e, line - 1, 2, 2, rows, cols), bf16),
             V((ring_e, line - 1, 2, 2, rows, cols), bf16),
+            V((tokens, d_model), f32),
             dma((ring, sems)),
             dma((ring, sems)),
             dma((2,)),
@@ -1142,7 +1158,7 @@
             dma,
             dma((n,)),
             dma((n,)),
-            dma((3,)),
+            dma((4,)),
             dma((2,)),
             dma((3,)),
             dma((ring_e, sems)),

time: 469 us -> 463 us (0.987)
  Pallas kernels: 465 us -> 458 us
where the time goes in v7:
time: 463 us; the launch traced here: 462 us
  Pallas kernels  458 us (99%)
    pallas_call x1, Pallas kernels, forward(): pl.pallas_call(functools.partial(forward_kernel, line, width, block), out...  238 us
    pallas_call x1, Pallas kernels, backward(): pl.pallas_call(functools.partial(backward_kernel, line, cols, tuple(start...  214 us

profile of v7, /device:TPU:0, one launch (start us, length us, event | category | flops | bytes accessed | tf_op | source)
XLA Modules:
  0.0 462.2 jit_solution(6479262168792185010)
XLA Ops:
  0.7 1.0 fusion.2
  1.7 1.0 pad_maximum_fusion
  2.6 238.4 %gather_forward.1 = (bf16[4,2,2,96,16896]{4,3,2,1,0:T(8,128)(2,1)}, bf16[4,2,2,8,128]{4,3,2,1,0:T(8,128)(2,1)}, bf16[16,512,96]{2,1,0:T(8,128)(2,1)}, bf16[8,512...) custom-call(bf16[96,768]{1,0:T(8,128)(2,1)} %refs_0_.1, ...), custom_call_target="tpu_custom_call" | custom-call | tf_op jit(solution)/shard_map/gather_forward/pallas_call | solution.py:518
  241.1 214.3 %backward_scatter.1 = (bf16[2,512,1536]{2,1,0:T(8,128)(2,1)}, f32[96,768]{1,0:T(8,128)}, f32[96,384]{1,0:T(8,128)}, f32[96,384]{1,0:T(8,128)}, f32[512,1536]{1,0...) custom-call(bf16[16,512,96]{2,1,0:T(8,128)(2,1)} %get-tuple-element., ...), custom_call_target="tpu_custom_call" | custom-call | tf_op jit(solution)/shard_map/backward_scatter/pallas_call | solution.py:1108
  455.4 5.5 %finish.1 = (f32[96,768]{1,0:T(8,128)}, f32[96,384]{1,0:T(8,128)}, f32[96,384]{1,0:T(8,128)}, f32[512,1536]{1,0:T(8,128)}, f32[96,768]{1,0:T(8,128)}, /*index=5*...) custom-call(f32[96,768]{1,0:T(8,128)} %get-tuple-element.60.refs_0_, ...), custom_call_target="tpu_custom_call" | custom-call | tf_op jit(solution)/shard_map/finish/pallas_call | solution.py:1186
  460.9 1.3 slice_bitcast_fusion
  (1 shorter events, 0.0 us)

commit v8 on v7

--- a/solution.py
+++ b/solution.py
@@ -3,6 +3,7 @@
 
 import jax
 import jax.numpy as jnp
+import numpy as np
 from jax import lax
 from jax.experimental import pallas as pl
 from jax.experimental.pallas import tpu as pltpu
@@ -121,7 +122,7 @@
     def each(self, t, fn):
         there = (t >= 0) & (t < self.count)
         for v, orders in enumerate(self.orders):
-            turn_of = there if len(self.orders) == 1 else there & ((lax.rem(t + 3, 3) == 0) == (v == 1))
+            turn_of = there if len(self.orders) == 1 else there & (((t == 0) | (t == 2) | (t == 5)) == (v == 1))
 
             @pl.when(turn_of)
             def _():
@@ -154,11 +155,10 @@
 
 
 def rope_tables(length, width):
-    half_width = width // 2
-    inverse = THETA_BASE ** (-(jnp.arange(half_width, dtype=jnp.float32) * 2.0 / width))
-    angles = jnp.arange(length, dtype=jnp.float32)[:, None] * inverse[None, :]
-    cosine, sine = jnp.cos(angles), jnp.sin(angles)
-    return jnp.concatenate([cosine, cosine], axis=1), jnp.concatenate([-sine, sine], axis=1)
+    inverse = np.float32(THETA_BASE) ** (-(np.arange(width // 2, dtype=np.float32) * np.float32(2.0 / width)))
+    angles = np.arange(length, dtype=np.float32)[:, None] * inverse[None, :]
+    cosine, sine = np.cos(angles), np.sin(angles)
+    return jnp.asarray(np.concatenate([cosine, cosine], axis=1)), jnp.asarray(np.concatenate([-sine, sine], axis=1))
 
 
 def turn(x, cosine, sine):
@@ -1170,9 +1170,11 @@
 
 
 def finish_kernel(n, *refs):
-    srcs, outs, bufs, (loads, stores) = refs[:n], refs[n : 2 * n], refs[2 * n : 3 * n], refs[3 * n :]
+    srcs, gains, outs, gain_outs, bufs, (loads, stores) = refs[:n], refs[n], refs[n + 1 : 2 * n + 1], refs[2 * n + 1 : 2 * n + 3], refs[2 * n + 3 : 3 * n + 3], refs[3 * n + 3 :]
     for i in range(n):
         pltpu.make_async_copy(srcs[i], bufs[i], loads.at[i]).start()
+    for row, out in enumerate(gain_outs):
+        out[...] = gains[row : row + 1, : out.shape[1]]
     for i in range(n):
         pltpu.make_async_copy(srcs[i], bufs[i], loads.at[i]).wait()
         pltpu.make_async_copy(bufs[i], outs[i], stores.at[i]).start()
@@ -1180,18 +1182,18 @@
         pltpu.make_async_copy(bufs[i], outs[i], stores.at[i]).wait()
 
 
-def finish(arrays):
+def finish(arrays, gains, rows):
     n = len(arrays)
-    hbm = pl.BlockSpec(memory_space=pl.ANY)
+    hbm, vmem = pl.BlockSpec(memory_space=pl.ANY), pl.BlockSpec(memory_space=pltpu.VMEM)
     return pl.pallas_call(
         functools.partial(finish_kernel, n),
-        out_shape=[jax.ShapeDtypeStruct(a.shape, a.dtype) for a in arrays],
-        in_specs=[hbm] * n,
-        out_specs=[hbm] * n,
+        out_shape=[jax.ShapeDtypeStruct(a.shape, a.dtype) for a in arrays] + [jax.ShapeDtypeStruct((1, rows), gains.dtype)] * 2,
+        in_specs=[hbm] * n + [vmem],
+        out_specs=[hbm] * n + [vmem] * 2,
         scratch_shapes=[pltpu.VMEM(a.shape, a.dtype) for a in arrays] + [pltpu.SemaphoreType.DMA((n,)), pltpu.SemaphoreType.DMA((n,))],
         compiler_params=pltpu.CompilerParams(vmem_limit_bytes=64 * 2**20 - 2**17),
         name="finish",
-    )(*arrays)
+    )(*arrays, gains)
 
 
 def layer(n_dp, n_tensor, hidden_in, query_weight, key_matrix, value_matrix, out_weight, gate_weight, up_weight, down_weight, attention_gain, feedforward_gain, cotangent):
@@ -1212,9 +1214,8 @@
     arrays = (q, k, v, mixed, full, hidden_in, cotangent, middle, grad_n2, gain_rows, cosine, sine, n1, n2, ct, mixed_pair, hidden, gate, up)
     halves = (down_weight.shape[0], gate_weight.shape[1], up_weight.shape[1], out_weight.shape[0], query_weight.shape[1], key_matrix.shape[1], value_matrix.shape[1])
     results = backward(line, 256 if line <= 4 else 128, arrays, halves)
-    g_query, g_key, g_value, grad_in, g_out, g_gate, g_up, g_down, hidden_out = finish(list(results[1:9]) + [hidden_out])
-    g_gains = results[9]
-    return hidden_out, grad_in, g_query, g_key, g_value, g_out.T, g_gate, g_up, g_down.T, g_gains[0, :rows], g_gains[1, :rows]
+    g_query, g_key, g_value, grad_in, g_out, g_gate, g_up, g_down, hidden_out, first_gain, second_gain = finish(list(results[1:9]) + [hidden_out], results[9], rows)
+    return hidden_out, grad_in, g_query, g_key, g_value, g_out.T, g_gate, g_up, g_down.T, first_gain.reshape(rows), second_gain.reshape(rows)
 
 
 def solution(mesh):

time: 463 us -> 455 us (0.983)
    pallas_call x1, Pallas kernels: 238 us -> 233 us  [forward(): pl.pallas_call(functools.partial(forward_kernel, line, width, block), out...]
where the time goes in v8:
time: 455 us
  Pallas kernels  454 us (100%)
    pallas_call x1, Pallas kernels, forward(): pl.pallas_call(functools.partial(forward_kernel, line, width, block), out...  233 us
    pallas_call x1, Pallas kernels, backward(): pl.pallas_call(functools.partial(backward_kernel, line, cols, tuple(start...  214 us

profile of v8, /device:TPU:0, one launch (start us, length us, event | category | flops | bytes accessed | tf_op | source)
XLA Modules:
  0.0 454.9 jit_solution(10640610881066195479)
XLA Ops:
  0.6 233.0 %gather_forward.1 = (bf16[4,2,2,96,16896]{4,3,2,1,0:T(8,128)(2,1)}, bf16[4,2,2,8,128]{4,3,2,1,0:T(8,128)(2,1)}, bf16[16,512,96]{2,1,0:T(8,128)(2,1)}, bf16[8,512...) custom-call(bf16[96,768]{1,0:T(8,128)(2,1)} %refs_0_.1, ...), custom_call_target="tpu_custom_call" | custom-call | tf_op jit(solution)/shard_map/gather_forward/pallas_call | solution.py:518
  233.7 214.3 %backward_scatter.1 = (bf16[2,512,1536]{2,1,0:T(8,128)(2,1)}, f32[96,768]{1,0:T(8,128)}, f32[96,384]{1,0:T(8,128)}, f32[96,384]{1,0:T(8,128)}, f32[512,1536]{1,0...) custom-call(bf16[16,512,96]{2,1,0:T(8,128)(2,1)} %get-tuple-element., ...), custom_call_target="tpu_custom_call" | custom-call | tf_op jit(solution)/shard_map/backward_scatter/pallas_call | solution.py:1108
  448.0 6.7 %finish.1 = (f32[96,768]{1,0:T(8,128)}, f32[96,384]{1,0:T(8,128)}, f32[96,384]{1,0:T(8,128)}, f32[512,1536]{1,0:T(8,128)}, f32[96,768]{1,0:T(8,128)}, /*index=5*...) custom-call(f32[96,768]{1,0:T(8,128)} %get-tuple-element.62.refs_0_,, ...), custom_call_target="tpu_custom_call" | custom-call | tf_op jit(solution)/shard_map/finish/pallas_call | solution.py:1188
